TPU v7x, 128 devices: a whole 4x4x4 slice. The times are simulated.
128 devices in a mesh: member: 8 (over x, y_lo), slab: 16 (over y_hi, z, core).
Axes of the slice: x: 4, y: 4 (y_hi: 2, y_lo: 2; y = y_hi * 2 + y_lo), z: 4, core: 2. Of those that a mesh axis runs over, the one named last changes fastest.
Arguments:
- control: float32 [32, 2, 1024, 2048], P('member', None, 'slab'), may hold values from -6 to 6
- perturbation: bfloat16 [32, 2, 1024, 2048], P('member', None, 'slab'), may hold values from -6 to 6
- loc_row: float32 [2, 1024], P(None, 'slab'), may hold values from 0.2 to 2
- loc_col: float32 [2, 2048], replicated, may hold values from 0.2 to 2
- obs_tile: int32 [4096], P('slab'), may hold values from 0 to 2047, as said below
- obs_count: int32 [4096], P('slab'), may hold values from 1 to 128
- obs_value: float32 [4096, 128], P('slab'), may hold values from -12 to 12
Outputs:
- gradient: float32 [32, 2, 1024, 2048], P('member', None, 'slab')
Inputs may be any that keep to these rules, and one draw needn't show every extreme that they name: `obs_tile`: entry i names a tile of slab block i // 256 in that block's numbering, whose columns lie in column share k = (i mod 256) // (256 / 16), i.e. columns k * 2048 / 16 onward; tiles may repeat. cells 0 to obs_count - 1 of a tile are observed.
All inputs are finite; a program needn't handle non-finite values.
Results may differ from a plain program's by a relative error of at most 0.012.
Values may be sent and summed in bfloat16 or wider, within the bound.
No kernel may reach another device: no remote copies, remote signals or barrier semaphores. Data moves between devices by JAX's collectives and lax.ppermute only.
A program may use at most 64 MiB of HBM per device.

v0:
```python
import jax
import jax.numpy as jnp
import numpy as np
from jax import lax
from jax.experimental import pallas as pl
from jax.experimental.pallas import tpu as pltpu
from jax.sharding import Mesh
from jax.sharding import PartitionSpec as P

TILE = 128
WIDE = 256
BF16 = jnp.bfloat16
F32 = jnp.float32
SLAB = ("chip", "core")
SAME_CORE = ("member", "chip")
VMEM = pl.BlockSpec(memory_space=pltpu.VMEM)
SMEM = pl.BlockSpec(memory_space=pltpu.SMEM)
HBM = pl.BlockSpec(memory_space=pltpu.HBM)


def run(kernel, out_shape, in_specs, mib, flops, scratch=(), out_specs=None):
    outs = out_shape if isinstance(out_shape, list) else [out_shape]
    if out_specs is None:
        out_specs = [VMEM] * len(outs)
    moved = sum(int(np.prod(o.shape)) * o.dtype.itemsize for o in outs) * 2
    call = pl.pallas_call(
        kernel,
        in_specs=in_specs,
        out_specs=out_specs,
        out_shape=outs,
        scratch_shapes=list(scratch),
        compiler_params=pltpu.CompilerParams(vmem_limit_bytes=mib << 20),
        cost_estimate=pl.CostEstimate(flops=flops, bytes_accessed=moved, transcendentals=0),
        name=kernel.__name__,
    )
    if isinstance(out_shape, list):
        return call
    return lambda *args: call(*args)[0]


def bf16(*shape):
    return jax.ShapeDtypeStruct(shape, BF16)


def f32(*shape):
    return jax.ShapeDtypeStruct(shape, F32)


def cas(first, second, order):
    angle = 2.0 * np.pi * (np.outer(first, second) % order) / order
    c, s = np.cos(angle), np.sin(angle)
    return [a.astype(np.float32) for a in (c + s, c - s, c, s)]


def select(core_ref, tile_ref, pert_ref, own_ref, send_ref):
    members = pert_ref.shape[0]
    core = core_ref[0]
    place = tile_ref[...] // 16
    row = lax.broadcasted_iota(jnp.int32, (TILE, TILE), 0)
    for ref, half in ((send_ref, 1 - core), (own_ref, core)):
        mine = jnp.where(half == 0, place[0:1, :], place[1:2, :])
        chosen = jnp.transpose((row == mine).astype(F32)).astype(BF16)
        for k in range(8):
            cols = pl.ds(pl.multiple_of((half * 8 + k) * TILE, TILE), TILE)
            tile = jnp.concatenate(
                [pert_ref[m, :, :, cols].reshape(TILE, TILE) for m in range(members)], axis=1
            )
            rows = jnp.dot(
                chosen[16 * k : 16 * k + 16], tile, preferred_element_type=F32
            ).astype(BF16)
            for m in range(members):
                ref[k * members + m] = rows[:, m * TILE : (m + 1) * TILE]
        ref[8 * members] = jnp.broadcast_to(mine.astype(F32), (16, TILE)).astype(BF16)


def forward(
    core_ref, control_ref, row_ref, col_ref,
    outer_c, outer_s, inner_p, inner_m, lead_c, lead_s,
    send_ref, own_ref, table_ref, scaled, plus, minus, block_ref, sems,
):
    members, levels, rows, width = control_ref.shape
    core = core_ref[0]
    steps = width // WIDE
    half = steps // 2
    block = inner_p.shape[0]
    for u in range(width // block):
        at = slice(u * block, (u + 1) * block)
        c, s = outer_c[u : u + 1, :], outer_s[u : u + 1, :]
        plus[at, :] = c * inner_p[...] + s * inner_m[...]
        minus[at, :] = c * inner_m[...] - s * inner_p[...]
    for l in range(levels):
        amplitude = row_ref[l][:, :1] * col_ref[l : l + 1, :]
        for m in range(members):
            at = (m * levels + l) * rows
            scaled[at : at + rows, :] = (control_ref[m, l] * amplitude).astype(BF16)

    def copy(nb, slot):
        return pltpu.make_async_copy(block_ref.at[slot], table_ref.at[nb], sems.at[slot])

    def step(which, target, n):
        nb = which * half + n
        slot = lax.rem(n, 2)

        @pl.when(n >= 2)
        def _():
            copy(nb, slot).wait()

        for q in range(WIDE // TILE):
            c = lead_c[nb * (WIDE // TILE) + q]
            s = lead_s[nb * (WIDE // TILE) + q]
            c = jnp.broadcast_to(c[None], (width // 16, 16, TILE)).reshape(width, TILE)
            s = jnp.broadcast_to(s[None], (width // 16, 16, TILE)).reshape(width, TILE)
            block_ref[slot, :, q * TILE : (q + 1) * TILE] = (
                c * plus[...] + s * minus[...]
            ).astype(BF16)
        copy(nb, slot).start()
        product = jnp.dot(scaled[...], block_ref[slot], preferred_element_type=F32)
        to = pl.ds(pl.multiple_of(n * WIDE, WIDE), WIDE)
        target[:, :, to] = product.astype(BF16).reshape(members, levels * rows, WIDE)

    def drain():
        for slot in range(2):
            copy(0, slot).wait()

    lax.fori_loop(0, half, lambda n, _: (step(1 - core, send_ref, n), 0)[1], 0)
    drain()
    lax.fori_loop(0, half, lambda n, _: (step(core, own_ref, n), 0)[1], 0)
    drain()


def spread_rows(place_ref, inner_p, inner_m, lead_c, lead_s, lane_c, lane_s, out_ref):
    chip, core = place_ref[0], place_ref[1]
    rows = inner_p.shape[0]
    plus, minus = [], []
    for q in range(2):
        slab = chip * 2 + (core + q) % 2
        c = jnp.broadcast_to(lead_c[slab][None], (rows // 16, 16, TILE)).reshape(rows, TILE)
        s = jnp.broadcast_to(lead_s[slab][None], (rows // 16, 16, TILE)).reshape(rows, TILE)
        plus.append(c * inner_p[...] + s * inner_m[...])
        minus.append(c * inner_m[...] - s * inner_p[...])
    left = lax.broadcasted_iota(jnp.int32, (rows, TILE), 1) < rows
    plus = jnp.where(left, plus[0], plus[1])
    minus = jnp.where(left, minus[0], minus[1])
    nothing = jnp.zeros((rows, TILE), BF16)
    for h in range(out_ref.shape[0]):
        for r in range(2):
            slab = h * 2 + (core + r) % 2
            entry = (lane_c[pl.ds(slab, 1), :] * plus + lane_s[pl.ds(slab, 1), :] * minus).astype(BF16)
            for l in range(2):
                at = slice((2 * l + r) * rows, (2 * l + r + 1) * rows)
                out_ref[h, at, l * TILE : (l + 1) * TILE] = entry
                out_ref[h, at, (1 - l) * TILE : (2 - l) * TILE] = nothing


def tiles_of(ref, k):
    chips = ref.shape[0]
    return jnp.concatenate(
        [
            ref[h, r * TILE + k * 16 : r * TILE + (k + 1) * 16, :]
            for h in range(chips)
            for r in range(2)
        ],
        axis=0,
    )


def cells(pert_ref, own_ref, par_ref, rows_ref, cells_ref, spread_ref):
    members, depth, _ = own_ref.shape
    rows = depth // 2
    chips = pert_ref.shape[0]
    last = pert_ref.shape[2] - 1
    lane = lax.broadcasted_iota(jnp.int32, (1, 2 * TILE), 1)
    row = lax.broadcasted_iota(jnp.int32, (4 * rows, 2 * TILE), 0)
    for h in range(chips):
        place = jnp.concatenate(
            [pert_ref[h, r, last].astype(F32)[0:1, :] for r in range(2)], axis=1
        ).astype(jnp.int32)
        level, inside = place // rows, place % rows
        place = level * (2 * rows) + inside + jnp.where(lane < TILE, 0, rows)
        chosen = (row == place).astype(F32).astype(BF16)
        spread_ref[h] = lax.dot_general(
            chosen, rows_ref[h], (((0,), (0,)), ((), ())), preferred_element_type=F32
        ).astype(BF16)
    for k in range(8):
        cols = slice(k * TILE, (k + 1) * TILE)
        along = jnp.concatenate(
            [
                jnp.concatenate(
                    [ref[m, l * rows : (l + 1) * rows, cols] for m in range(members)], axis=1
                )
                for l in range(2)
                for ref in (own_ref, par_ref)
            ],
            axis=0,
        )
        field = jnp.dot(tiles_of(spread_ref, k), along, preferred_element_type=F32)
        total = None
        for m in range(members):
            pert = pert_ref[:, :, k * members + m].reshape(-1, TILE).astype(F32)
            term = pert * field[:, m * TILE : (m + 1) * TILE]
            total = term if total is None else total + term
        cells_ref[k] = total.astype(BF16)


def turn(spread_ref, own_ref, par_ref):
    rows = own_ref.shape[1] // 2
    for k in range(8):
        turned = jnp.transpose(tiles_of(spread_ref, k).astype(F32)).astype(BF16)
        for l in range(2):
            to = slice(l * rows, (l + 1) * rows)
            own_ref[k, to, :] = turned[2 * l * rows : (2 * l + 1) * rows]
            par_ref[k, to, :] = turned[(2 * l + 1) * rows : (2 * l + 2) * rows]


def score(cells_ref, own_ref, lent_ref, out_ref):
    copies = out_ref.shape[0]
    total = jnp.sum(cells_ref[...].astype(F32), axis=0)
    value = jnp.concatenate([own_ref[0], lent_ref[0]], axis=0)
    seen = jnp.concatenate([own_ref[1], lent_ref[1]], axis=0)
    resid = total - value
    result = jnp.where(seen > 0.5, resid / jnp.sqrt(1.0 + resid * resid * 0.25), 0.0)
    result = result.astype(BF16)
    for i in range(copies):
        out_ref[i] = result


def to_members(ref, k, back):
    for m in range(ref.shape[0]):
        ref[m, :, k * TILE : (k + 1) * TILE] = back[:, m * TILE : (m + 1) * TILE]


def back_par(pert_ref, score_ref, turned_ref, weighted_ref, par_ref):
    members = par_ref.shape[0]
    for k in range(8):
        weight = score_ref[k].astype(F32)
        weighted = jnp.concatenate(
            [
                (pert_ref[:, :, k * members + m].reshape(-1, TILE).astype(F32) * weight).astype(BF16)
                for m in range(members)
            ],
            axis=1,
        )
        weighted_ref[k] = weighted
        to_members(
            par_ref, k, jnp.dot(turned_ref[k], weighted, preferred_element_type=F32).astype(BF16)
        )


def inverse_own(core_ref, weighted_ref, turned_ref, table_ref, sum_ref, own, block_ref, sems):
    members, depth, width = own.shape
    steps = sum_ref.shape[0]
    near = pl.ds(pl.multiple_of(core_ref[0] * width, width), width)

    def fetch(n, slot):
        return pltpu.make_async_copy(
            table_ref.at[n, near, :], block_ref.at[slot], sems.at[slot]
        )

    fetch(0, 0).start()
    for k in range(8):
        to_members(
            own,
            k,
            jnp.dot(turned_ref[k], weighted_ref[k], preferred_element_type=F32).astype(BF16),
        )

    def step(n, carry):
        slot = lax.rem(n, 2)

        @pl.when(n + 1 < steps)
        def _():
            fetch(n + 1, 1 - slot).start()

        fetch(n, slot).wait()
        sum_ref[n] = jnp.dot(
            own[...].reshape(members * depth, width),
            block_ref[slot],
            preferred_element_type=F32,
        )
        return carry

    lax.fori_loop(0, steps, step, 0)


def inverse_par(
    core_ref, par_ref, sum_ref, table_ref, row_ref, col_ref, out_ref, piece, sems, block_ref, reads
):
    members, depth, width = par_ref.shape
    levels, rows, _ = row_ref.shape
    steps = sum_ref.shape[0]
    far = pl.ds(pl.multiple_of((1 - core_ref[0]) * width, width), width)

    def fetch(n, slot):
        return pltpu.make_async_copy(
            table_ref.at[n, far, :], block_ref.at[slot], reads.at[slot]
        )

    fetch(0, 0).start()

    def copy(n, slot):
        cols = pl.ds(pl.multiple_of(n * WIDE, WIDE), WIDE)
        return pltpu.make_async_copy(piece.at[slot], out_ref.at[:, :, :, cols], sems.at[slot])

    def step(n, carry):
        slot = lax.rem(n, 2)
        cols = pl.ds(pl.multiple_of(n * WIDE, WIDE), WIDE)

        @pl.when(n + 1 < steps)
        def _():
            fetch(n + 1, 1 - slot).start()

        fetch(n, slot).wait()
        product = sum_ref[n] + jnp.dot(
            par_ref[...].reshape(members * depth, width),
            block_ref[slot],
            preferred_element_type=F32,
        )
        product = product.reshape(members, levels, rows, WIDE)

        @pl.when(n >= 2)
        def _():
            copy(n - 2, slot).wait()

        for l in range(levels):
            amplitude = row_ref[l][:, :1] * col_ref[l : l + 1, cols]
            for m in range(members):
                piece[slot, m, l] = product[m, l] * amplitude
        copy(n, slot).start()
        return carry

    lax.fori_loop(0, steps, step, 0)
    copy(steps - 2, steps % 2).wait()
    copy(steps - 1, (steps - 1) % 2).wait()


def shards(control, perturbation, loc_row, loc_col, obs_tile, obs_count, obs_value):
    members, levels, rows, width = control.shape
    chips = lax.axis_size("chip")
    slabs = chips * 2
    peers = lax.axis_size("member") * chips
    height = rows * slabs
    half = width // 2
    per_core = half // TILE
    depth = levels * rows
    chip = lax.axis_index("chip").astype(jnp.int32)
    core = lax.axis_index("core").astype(jnp.int32)
    group = lax.axis_index("member").astype(jnp.int32)
    core_index = core.reshape(1)
    swap = [(0, 1), (1, 0)]

    blocks = per_core * members + 1
    own_tiles, send_tiles = run(
        select, [bf16(blocks, 16, TILE)] * 2, [SMEM, VMEM, VMEM], 16, 1 << 27
    )(core_index, obs_tile.reshape(2, TILE), perturbation)
    par_tiles = lax.ppermute(send_tiles, "core", swap)
    message = jnp.broadcast_to(
        jnp.stack([own_tiles, par_tiles])[None], (chips, 2, blocks, 16, TILE)
    )
    arrived = lax.all_to_all(message, "chip", split_axis=0, concat_axis=0, tiled=True)

    lane = jnp.arange(TILE, dtype=jnp.int32)

    def of_column(column, array):
        return lax.dynamic_slice_in_dim(array, column * 16, 16, 0)

    seen = (lane[None, :] < obs_count[:, None]).astype(F32)
    mine = per_core * core + group
    other = per_core * (1 - core) + group
    stated = jnp.stack([of_column(mine, obs_value), of_column(mine, seen)])
    lent = jnp.stack([of_column(other, obs_value), of_column(other, seen)])
    lent = lax.ppermute(lent, "core", swap)

    lead = cas(np.arange(16), np.arange(16), 16)
    lead_c, lead_s = [jnp.asarray(np.repeat(a[:, :, None], TILE, axis=2)) for a in lead[2:]]
    inner = 64
    outer = cas(np.arange(width // inner), np.arange(TILE), width // inner)
    outer_c, outer_s = [jnp.asarray(a) for a in outer[2:]]
    near = cas(np.arange(inner), np.arange(TILE), width)
    near_p, near_m = [jnp.asarray(a / np.float32(np.sqrt(width))) for a in near[:2]]
    wave = np.arange(TILE) % rows
    base = cas(np.arange(rows), wave, height)
    base_p, base_m = [jnp.asarray(a / np.float32(np.sqrt(height))) for a in base[:2]]
    lane_c, lane_s = [jnp.asarray(a) for a in cas(np.arange(16), wave, 16)[2:]]

    row_b = jnp.broadcast_to(loc_row[:, :, None], (levels, rows, TILE))
    send, own, table = run(
        forward,
        [bf16(members, depth, half), bf16(members, depth, half), bf16(width // WIDE, width, WIDE)],
        [SMEM] + [VMEM] * 9,
        24,
        2 * members * depth * width * width,
        [
            pltpu.VMEM((members * depth, width), BF16),
            pltpu.VMEM((width, TILE), F32),
            pltpu.VMEM((width, TILE), F32),
            pltpu.VMEM((2, width, WIDE), BF16),
            pltpu.SemaphoreType.DMA((2,)),
        ],
        [VMEM, VMEM, HBM],
    )(core_index, control, row_b, loc_col, outer_c, outer_s, near_p, near_m, lead_c, lead_s)
    par = lax.ppermute(send, "core", swap)
    table_rows = run(
        spread_rows, bf16(chips, 4 * rows, 2 * TILE), [SMEM] + [VMEM] * 6, 4, 1 << 22
    )(jnp.stack([chip, core]), base_p, base_m, lead_c, lead_s, lane_c, lane_s)

    tiles = slabs * 16
    partial, spread = run(
        cells,
        [bf16(per_core, tiles, TILE), bf16(chips, tiles, 4 * rows)],
        [VMEM] * 4,
        12,
        1 << 30,
    )(arrived, own, par, table_rows)
    partial = lax.all_to_all(
        partial.reshape(peers, 2 * 16, TILE), SAME_CORE, split_axis=0, concat_axis=0, tiled=True
    )
    turned, turned_par = run(
        turn, [bf16(per_core, depth, tiles), bf16(per_core, depth, tiles)], [VMEM], 6, 1 << 22
    )(spread)
    scores = run(score, bf16(peers, 2 * 16, TILE), [VMEM] * 3, 4, 1 << 20)(partial, stated, lent)
    scores = lax.all_to_all(scores, SAME_CORE, split_axis=0, concat_axis=0, tiled=True)

    weighted, back_send = run(
        back_par,
        [bf16(per_core, tiles, members * TILE), bf16(members, depth, half)],
        [VMEM] * 3,
        12,
        1 << 28,
    )(arrived, scores.reshape(per_core, tiles, TILE), turned_par)
    back_other = lax.ppermute(back_send, "core", swap)
    summed = run(
        inverse_own,
        f32(width // WIDE, members * depth, WIDE),
        [SMEM, VMEM, VMEM, HBM],
        14,
        members * depth * width * width,
        [
            pltpu.VMEM((members, depth, half), BF16),
            pltpu.VMEM((2, half, WIDE), BF16),
            pltpu.SemaphoreType.DMA((2,)),
        ],
    )(core_index, weighted, turned, table)
    return run(
        inverse_par,
        f32(*control.shape),
        [SMEM, VMEM, VMEM, HBM, VMEM, VMEM],
        14,
        members * depth * width * width,
        [
            pltpu.VMEM((2, members, levels, rows, WIDE), F32),
            pltpu.SemaphoreType.DMA((2,)),
            pltpu.VMEM((2, half, WIDE), BF16),
            pltpu.SemaphoreType.DMA((2,)),
        ],
        [HBM],
    )(core_index, back_other, summed, table, row_b, loc_col)


def solution(mesh):
    torus = Mesh(
        mesh.devices.reshape(mesh.shape["member"], mesh.shape["slab"] // 2, 2),
        ("member", "chip", "core"),
    )
    placed = (
        P("member", None, SLAB, None),
        P("member", None, SLAB, None),
        P(None, SLAB),
        P(),
        P(SLAB),
        P(SLAB),
        P(SLAB, None),
    )
    return jax.shard_map(
        shards,
        mesh=torus,
        in_specs=placed,
        out_specs=P("member", None, SLAB, None),
        check_vma=False,
    )
```

profile of v0, /device:TPU:1, one launch (start us, length us, event | category | flops | bytes accessed | tf_op | source)
XLA Modules:
  0.0 106.7 jit_solution(7593696330422333881)
XLA Ops:
  0.0 1.6 %copy-done.3 = bf16[4,2,64,2048]{3,2,1,0:T(8,128)(2,1)S(1)} copy-done((bf16[4,2,64,2048]{3,2,1,0:T(8,128)(2,1)S(1)}, bf16[4,2,64,2048]{3,2,1,0:T(8,128)(2,1)}, u32[]{:S(2)}) %copy-start.3) | copy-done | bytes 2097176
  1.6 0.7 copy-done.18
  2.3 0.7 select.1
  2.9 0.0 copy-start.15
  3.0 0.0 copy-start.20
  3.0 0.0 copy-start.21
  3.0 0.0 copy-start.22
  3.0 0.0 copy-start.23
  3.0 1.5 %collective-permute-start = (bf16[33,16,128]{2,1,0:T(8,128)(2,1)S(1)}, bf16[33,16,128]{2,1,0:T(8,128)(2,1)S(1)}, u32[]{:S(2)}, u32[]{:S(2)}) collective-permute-start(bf16[33,16,128]{2,1,0:T(8,128)(2,1)S(1)} %get-tuple-element.17), channel_id=1, source_target_pairs={{0,1},{1,0},{2,3},{3,2},{4,5},{5,4},{6,7},{7,6},{8,9},{9,8},{10,11... | collective-permute-start | bytes 405512 | tf_op jit(solution)/shard_map/ppermute | solution.py:355
  4.5 1.0 collective-permute-done
  5.5 1.6 %broadcast_in_dim.4 = bf16[8,2,33,16,128]{4,3,2,1,0:T(8,128)(2,1)} broadcast(bf16[2,33,16,128]{3,2,1,0:T(8,128)(2,1)S(1)} %pad_maximum_fusion), dimensions={1,2,3,4} | broadcast | bytes 2433024 | tf_op jit(solution)/shard_map/broadcast_in_dim | solution.py:356
  7.1 7.8 %all-to-all-start = ((bf16[8,2,33,16,128]{4,3,2,1,0:T(8,128)(2,1)}), bf16[8,2,33,16,128]{4,3,2,1,0:T(8,128)(2,1)S(1)}, u32[]{:S(2)}, u32[]{:S(2)}) async-start(bf16[8,2,33,16,128]{4,3,2,1,0:T(8,128)(2,1)} %broadcast_in_dim.4), calls=%async_computation | async-start | bytes 4325376 | tf_op jit(solution)/shard_map/all_to_all | solution.py:359
  14.9 0.1 broadcast_in_dim.5.row_ref
  15.0 2.2 %copy-done.19 = f32[4,2,64,2048]{3,2,1,0:T(8,128)S(1)} copy-done((f32[4,2,64,2048]{3,2,1,0:T(8,128)S(1)}, f32[4,2,64,2048]{3,2,1,0:T(8,128)}, u32[]{:S(2)}) %copy-start.19) | copy-done | bytes 4194328
  17.2 10.4 %forward.1 = (bf16[4,128,1024]{2,1,0:T(8,128)(2,1)}, bf16[4,128,1024]{2,1,0:T(8,128)(2,1)S(1)}, bf16[8,2048,256]{2,1,0:T(8,128)(2,1)S(1)}) custom-call(s32[1]{0:T(128)} %bitcast.core_ref, f32[4,2,64,2048]{3,2,1,0:T(8,128)S(1)} %copy-done.19, f32[2,64,128]{2,1,0:T(8,128)S(1)} %broadcast_in_dim.5.row_ref, f32[2,2048]{1,0:T(2,128)S(1)} %copy-done.15, ...), custom_call_target="tpu_custom_call" | custom-call | flops 4294967296 | bytes 20971520 | tf_op jit(solution)/shard_map/forward/pallas_call | solution.py:386
  27.6 3.3 %copy-done = bf16[8,2048,256]{2,1,0:T(8,128)(2,1)} copy-done((bf16[8,2048,256]{2,1,0:T(8,128)(2,1)}, bf16[8,2048,256]{2,1,0:T(8,128)(2,1)S(1)}, u32[]{:S(2)}) %copy-start) | copy-done | bytes 8388632
  30.9 1.0 copy-done.6
  31.9 0.6 collective-permute-start.1
  32.5 0.1 pad_add_fusion.place_ref
  32.6 0.8 copy-done.13
  33.4 0.8 copy-done.14
  34.1 0.7 copy-done.16
  34.8 0.7 copy-done.17
  35.5 0.7 spread_rows.1.rows_ref
  36.2 5.5 %all-to-all-done.pert_ref = bf16[8,2,33,16,128]{4,3,2,1,0:T(8,128)(2,1)S(1)} async-done(((bf16[8,2,33,16,128]{4,3,2,1,0:T(8,128)(2,1)}), bf16[8,2,33,16,128]{4,3,2,1,0:T(8,128)(2,1)S(1)}, u32[]{:S(2)}, u32[]{:S(2)}) %all-to-all-start) | async-done | bytes 2162720 | tf_op jit(solution)/shard_map/all_to_all | solution.py:359
  41.8 1.2 %copy-done.7 = bf16[4,128,1024]{2,1,0:T(8,128)(2,1)S(1)} copy-done((bf16[4,128,1024]{2,1,0:T(8,128)(2,1)S(1)}, bf16[4,128,1024]{2,1,0:T(8,128)(2,1)}, u32[]{:S(2)}) %copy-start.7) | copy-done | bytes 1048600
  43.0 2.5 %cells.1 = (bf16[8,256,128]{2,1,0:T(8,128)(2,1)S(1)}, bf16[8,256,256]{2,1,0:T(8,128)(2,1)S(1)}) custom-call(bf16[8,2,33,16,128]{4,3,2,1,0:T(8,128)(2,1)S(1)} %all-to-all-done.pert_ref, bf16[4,128,1024]{2,1,0:T(8,128)(2,1)S(1)} %copy-done.7, bf16[4,128,1024]{2,1,0:T(8,128)(2,1)} %collective-permute-done.1.par_ref, bf16[8,256,256]{2,1,0:T(8,128)(2,1)S(1)} %spread_rows.1.rows_ref), custom_call_target="tpu_custom_call" | custom-call | flops 1073741824 | bytes 3145728 | tf_op jit(solution)/shard_map/cells/pallas_call | solution.py:407
  45.5 1.0 copy-done.4
  46.5 0.8 copy-done.10
  47.3 8.6 %all-to-all-start.1 = ((bf16[64,32,128]{2,1,0:T(8,128)(2,1)}), bf16[64,32,128]{2,1,0:T(8,128)(2,1)S(1)}, u32[]{:S(2)}, u32[]{:S(2)}) async-start(bf16[64,32,128]{2,1,0:T(8,128)(2,1)} %bitcast.16), calls=%async_computation.1 | async-start | bytes 1048576 | tf_op jit(solution)/shard_map/all_to_all | solution.py:414
  55.9 0.8 fusion
  56.7 0.7 dynamic-slice_bitcast_fusion
  57.5 0.8 collective-permute-start.2
  58.2 0.8 collective-permute-done.2.lent_ref
  59.1 8.8 %all-to-all-done.1.cells_ref = bf16[64,32,128]{2,1,0:T(8,128)(2,1)S(1)} async-done(((bf16[64,32,128]{2,1,0:T(8,128)(2,1)}), bf16[64,32,128]{2,1,0:T(8,128)(2,1)S(1)}, u32[]{:S(2)}, u32[]{:S(2)}) %all-to-all-start.1) | async-done | bytes 524320 | tf_op jit(solution)/shard_map/all_to_all | solution.py:414
  67.9 1.0 score.1
  68.9 5.2 %all-to-all-start.2 = ((bf16[64,32,128]{2,1,0:T(8,128)(2,1)}), bf16[64,32,128]{2,1,0:T(8,128)(2,1)S(1)}, u32[]{:S(2)}, u32[]{:S(2)}) async-start(bf16[64,32,128]{2,1,0:T(8,128)(2,1)} %score.1), calls=%async_computation.2 | async-start | bytes 1048576 | tf_op jit(solution)/shard_map/all_to_all | solution.py:421
  74.1 1.2 %copy-done.5 = bf16[8,256,256]{2,1,0:T(8,128)(2,1)S(1)} copy-done((bf16[8,256,256]{2,1,0:T(8,128)(2,1)S(1)}, bf16[8,256,256]{2,1,0:T(8,128)(2,1)}, u32[]{:S(2)}) %copy-start.5) | copy-done | bytes 1048600
  75.4 0.3 turn.1
  75.7 0.8 copy-done.8
  76.5 8.5 %all-to-all-done.2 = bf16[64,32,128]{2,1,0:T(8,128)(2,1)S(1)} async-done(((bf16[64,32,128]{2,1,0:T(8,128)(2,1)}), bf16[64,32,128]{2,1,0:T(8,128)(2,1)S(1)}, u32[]{:S(2)}, u32[]{:S(2)}) %all-to-all-start.2) | async-done | bytes 524320 | tf_op jit(solution)/shard_map/all_to_all | solution.py:421
  85.0 1.0 copy-done.9
  86.1 0.8 back_par.1
  86.9 3.2 %collective-permute-start.3 = (bf16[4,128,1024]{2,1,0:T(8,128)(2,1)S(1)}, bf16[4,128,1024]{2,1,0:T(8,128)(2,1)S(1)}, u32[]{:S(2)}, u32[]{:S(2)}) collective-permute-start(bf16[4,128,1024]{2,1,0:T(8,128)(2,1)S(1)} %get-tuple-element.23), channel_id=1, source_target_pairs={{0,1},{1,0},{2,3},{3,2},{4,5},{5,4},{6,7},{7,6},{8,9},{9,8},{10,11... | collective-permute-start | bytes 3145736 | tf_op jit(solution)/shard_map/ppermute | solution.py:430
  90.1 3.4 %copy-done.1 = bf16[8,2048,256]{2,1,0:T(8,128)(2,1)S(1)} copy-done((bf16[8,2048,256]{2,1,0:T(8,128)(2,1)S(1)}, bf16[8,2048,256]{2,1,0:T(8,128)(2,1)}, u32[]{:S(2)}) %copy-start.1) | copy-done | bytes 8388632
  93.4 4.4 %inverse_own.1.sum_ref = f32[8,512,256]{2,1,0:T(8,128)S(1)} custom-call(s32[1]{0:T(128)} %bitcast.core_ref, bf16[8,256,512]{2,1,0:T(8,128)(2,1)S(1)} %get-tuple-element.24.weighted_ref, bf16[8,128,256]{2,1,0:T(8,128)(2,1)S(1)} %get-tuple-element.25.turned_ref, bf16[8,2048,256]{2,1,0:T(8,128)(2,1)S(1)} %copy-done.1), custom_call_target="tpu_custom_call" | custom-call | flops 2147483648 | bytes 8388608 | tf_op jit(solution)/shard_map/inverse_own/pallas_call | solution.py:38
  97.8 3.4 %copy-done.2 = bf16[8,2048,256]{2,1,0:T(8,128)(2,1)S(1)} copy-done((bf16[8,2048,256]{2,1,0:T(8,128)(2,1)S(1)}, bf16[8,2048,256]{2,1,0:T(8,128)(2,1)}, u32[]{:S(2)}) %copy-start.2) | copy-done | bytes 8388632
  101.2 5.5 %inverse_par.1 = f32[4,2,64,2048]{3,2,1,0:T(8,128)} custom-call(s32[1]{0:T(128)} %bitcast.core_ref, bf16[4,128,1024]{2,1,0:T(8,128)(2,1)S(1)} %collective-permute-done.3.par_ref, f32[8,512,256]{2,1,0:T(8,128)S(1)} %inverse_own.1.sum_ref, bf16[8,2048,256]{2,1,0:T(8,128)(2,1)S(1)} %copy-done.2, f32[2,64,128]{2,1,0:T(8,128)S(1)} %broadcast_in_dim.5.row_ref, ...), custom_call_target="tpu_custom_call" | custom-call | flops 2147483648 | bytes 8388608 | tf_op jit(solution)/shard_map/inverse_par/pallas_call | solution.py:38
  (33 shorter events, 0.1 us)
Async XLA Ops:
  0.0 1.6 %copy-start.3 = (bf16[4,2,64,2048]{3,2,1,0:T(8,128)(2,1)S(1)}, bf16[4,2,64,2048]{3,2,1,0:T(8,128)(2,1)}, u32[]{:S(2)}) copy-start(bf16[4,2,64,2048]{3,2,1,0:T(8,128)(2,1)} %pert_ref.1) | copy-start | bytes 6291460
  1.6 0.7 copy-start.18
  2.3 12.6 %copy-start.24 = (f32[2,64]{1,0:T(2,128)S(1)}, f32[2,64]{1,0:T(2,128)}, u32[]{:S(2)}) copy-start(f32[2,64]{1,0:T(2,128)} %param.19) | copy-start | bytes 1540
  2.9 12.0 %copy-start.11 = (f32[16,16,128]{2,1,0:T(8,128)S(1)}, f32[16,16,128]{2,1,0:T(8,128)}, u32[]{:S(2)}) copy-start(f32[16,16,128]{2,1,0:T(8,128)} %constant.43.clone.lead_s) | copy-start | bytes 393220
  2.9 12.0 %copy-start.12 = (f32[16,16,128]{2,1,0:T(8,128)S(1)}, f32[16,16,128]{2,1,0:T(8,128)}, u32[]{:S(2)}) copy-start(f32[16,16,128]{2,1,0:T(8,128)} %constant.42.clone.lead_c) | copy-start | bytes 393220
  2.9 12.0 %copy-start.15 = (f32[2,2048]{1,0:T(2,128)S(1)}, f32[2,2048]{1,0:T(2,128)}, u32[]{:S(2)}) copy-start(f32[2,2048]{1,0:T(2,128)} %col_ref.3) | copy-start | bytes 49156
  3.0 12.0 %copy-start.20 = (f32[64,128]{1,0:T(8,128)S(1)}, f32[64,128]{1,0:T(8,128)}, u32[]{:S(2)}) copy-start(f32[64,128]{1,0:T(8,128)} %constant.47.clone.inner_m) | copy-start | bytes 98308
  3.0 12.0 %copy-start.21 = (f32[64,128]{1,0:T(8,128)S(1)}, f32[64,128]{1,0:T(8,128)}, u32[]{:S(2)}) copy-start(f32[64,128]{1,0:T(8,128)} %constant.46.clone.inner_p) | copy-start | bytes 98308
  3.0 12.0 %copy-start.22 = (f32[32,128]{1,0:T(8,128)S(1)}, f32[32,128]{1,0:T(8,128)}, u32[]{:S(2)}) copy-start(f32[32,128]{1,0:T(8,128)} %constant.45.clone.outer_s) | copy-start | bytes 49156
  3.0 12.0 %copy-start.23 = (f32[32,128]{1,0:T(8,128)S(1)}, f32[32,128]{1,0:T(8,128)}, u32[]{:S(2)}) copy-start(f32[32,128]{1,0:T(8,128)} %constant.44.clone.outer_c) | copy-start | bytes 49156
  3.0 2.5 %collective-permute-start = (bf16[33,16,128]{2,1,0:T(8,128)(2,1)S(1)}, bf16[33,16,128]{2,1,0:T(8,128)(2,1)S(1)}, u32[]{:S(2)}, u32[]{:S(2)}) collective-permute-start(bf16[33,16,128]{2,1,0:T(8,128)(2,1)S(1)} %get-tuple-element.17), channel_id=1, source_target_pairs={{0,1},{1,0},{2,3},{3,2},{4,5},{5,4},{6,7},{7,6},{8,9},{9,8},{10,11... | collective-permute-start | bytes 405512 | tf_op jit(solution)/shard_map/ppermute | solution.py:355
  7.1 34.7 %all-to-all-start = ((bf16[8,2,33,16,128]{4,3,2,1,0:T(8,128)(2,1)}), bf16[8,2,33,16,128]{4,3,2,1,0:T(8,128)(2,1)S(1)}, u32[]{:S(2)}, u32[]{:S(2)}) async-start(bf16[8,2,33,16,128]{4,3,2,1,0:T(8,128)(2,1)} %broadcast_in_dim.4), calls=%async_computation | async-start | bytes 4325376 | tf_op jit(solution)/shard_map/all_to_all | solution.py:359
  15.0 2.2 %copy-start.19 = (f32[4,2,64,2048]{3,2,1,0:T(8,128)S(1)}, f32[4,2,64,2048]{3,2,1,0:T(8,128)}, u32[]{:S(2)}) copy-start(f32[4,2,64,2048]{3,2,1,0:T(8,128)} %control_ref.1) | copy-start | bytes 12582916
  27.6 3.3 %copy-start = (bf16[8,2048,256]{2,1,0:T(8,128)(2,1)}, bf16[8,2048,256]{2,1,0:T(8,128)(2,1)S(1)}, u32[]{:S(2)}) copy-start(bf16[8,2048,256]{2,1,0:T(8,128)(2,1)S(1)} %get-tuple-element.26.table_ref) | copy-start | bytes 25165828
  30.9 1.0 copy-start.6
  31.9 4.3 %collective-permute-start.1 = (bf16[4,128,1024]{2,1,0:T(8,128)(2,1)}, bf16[4,128,1024]{2,1,0:T(8,128)(2,1)}, u32[]{:S(2)}, u32[]{:S(2)}) collective-permute-start(bf16[4,128,1024]{2,1,0:T(8,128)(2,1)} %get-tuple-element.19), channel_id=1, source_target_pairs={{0,1},{1,0},{2,3},{3,2},{4,5},{5,4},{6,7},{7,6},{8,9},{9,8},{10,11... | collective-permute-start | bytes 3145736 | tf_op jit(solution)/shard_map/ppermute | solution.py:401
  32.6 0.8 copy-start.13
  33.4 0.8 copy-start.14
  34.1 0.7 copy-start.16
  34.8 0.7 copy-start.17
  41.8 1.2 %copy-start.7 = (bf16[4,128,1024]{2,1,0:T(8,128)(2,1)S(1)}, bf16[4,128,1024]{2,1,0:T(8,128)(2,1)}, u32[]{:S(2)}) copy-start(bf16[4,128,1024]{2,1,0:T(8,128)(2,1)} %copy-done.6) | copy-start | bytes 3145732
  45.5 1.0 copy-start.4
  46.4 0.8 copy-start.10
  47.3 20.6 %all-to-all-start.1 = ((bf16[64,32,128]{2,1,0:T(8,128)(2,1)}), bf16[64,32,128]{2,1,0:T(8,128)(2,1)S(1)}, u32[]{:S(2)}, u32[]{:S(2)}) async-start(bf16[64,32,128]{2,1,0:T(8,128)(2,1)} %bitcast.16), calls=%async_computation.1 | async-start | bytes 1048576 | tf_op jit(solution)/shard_map/all_to_all | solution.py:414
  57.5 1.6 %collective-permute-start.2 = (f32[2,16,128]{2,1,0:T(8,128)S(1)}, f32[2,16,128]{2,1,0:T(8,128)S(1)}, u32[]{:S(2)}, u32[]{:S(2)}) collective-permute-start(f32[2,16,128]{2,1,0:T(8,128)S(1)} %pad_maximum_fusion.2), channel_id=1, source_target_pairs={{0,1},{1,0},{2,3},{3,2},{4,5},{5,4},{6,7},{7,6},{8,9},{9,8},{10,11... | collective-permute-start | bytes 49160 | tf_op jit(solution)/shard_map/ppermute | solution.py:371
  68.9 16.1 %all-to-all-start.2 = ((bf16[64,32,128]{2,1,0:T(8,128)(2,1)}), bf16[64,32,128]{2,1,0:T(8,128)(2,1)S(1)}, u32[]{:S(2)}, u32[]{:S(2)}) async-start(bf16[64,32,128]{2,1,0:T(8,128)(2,1)} %score.1), calls=%async_computation.2 | async-start | bytes 1048576 | tf_op jit(solution)/shard_map/all_to_all | solution.py:421
  74.1 1.2 %copy-start.5 = (bf16[8,256,256]{2,1,0:T(8,128)(2,1)S(1)}, bf16[8,256,256]{2,1,0:T(8,128)(2,1)}, u32[]{:S(2)}) copy-start(bf16[8,256,256]{2,1,0:T(8,128)(2,1)} %copy-done.4) | copy-start | bytes 3145732
  75.7 0.8 copy-start.8
  85.0 1.0 copy-start.9
  86.9 10.9 %collective-permute-start.3 = (bf16[4,128,1024]{2,1,0:T(8,128)(2,1)S(1)}, bf16[4,128,1024]{2,1,0:T(8,128)(2,1)S(1)}, u32[]{:S(2)}, u32[]{:S(2)}) collective-permute-start(bf16[4,128,1024]{2,1,0:T(8,128)(2,1)S(1)} %get-tuple-element.23), channel_id=1, source_target_pairs={{0,1},{1,0},{2,3},{3,2},{4,5},{5,4},{6,7},{7,6},{8,9},{9,8},{10,11... | collective-permute-start | bytes 3145736 | tf_op jit(solution)/shard_map/ppermute | solution.py:430
  90.1 3.4 %copy-start.1 = (bf16[8,2048,256]{2,1,0:T(8,128)(2,1)S(1)}, bf16[8,2048,256]{2,1,0:T(8,128)(2,1)}, u32[]{:S(2)}) copy-start(bf16[8,2048,256]{2,1,0:T(8,128)(2,1)} %copy-done) | copy-start | bytes 25165828
  97.8 3.4 %copy-start.2 = (bf16[8,2048,256]{2,1,0:T(8,128)(2,1)S(1)}, bf16[8,2048,256]{2,1,0:T(8,128)(2,1)}, u32[]{:S(2)}) copy-start(bf16[8,2048,256]{2,1,0:T(8,128)(2,1)} %copy-done) | copy-start | bytes 25165828
where the time goes:
time: 108 us; the launch traced here: 107 us
  starting transfers between devices  27.7 us (26%)
  local copies, waits for them, and re-layouts  26.9 us (25%)
  Pallas kernels  26.2 us (24%)
  waiting for transfers between devices  24.8 us (23%)
    unnamed x50, local copies, waits for them, and re-layouts  24.5 us
    pallas_call x4, Pallas kernels, run(): return lambda *args: call(*args)[0]  11.5 us
    pallas_call x1, Pallas kernels, shards(): run(forward, [bf16(members, depth, half), bf16(members, depth, half), bf1...  10.4 us
    all_to_all x1, waiting for transfers between devices, shards(): lax.all_to_all(partial.reshape(peers, 2 * 16, TILE), SAME_CORE, split_axi...  8.85 us
    all_to_all x1, starting transfers between devices, shards(): lax.all_to_all(partial.reshape(peers, 2 * 16, TILE), SAME_CORE, split_axi...  8.63 us
    all_to_all x1, waiting for transfers between devices, shards(): lax.all_to_all(scores, SAME_CORE, split_axis=0, concat_axis=0, tiled=True)  8.55 us
    all_to_all x1, starting transfers between devices, shards(): lax.all_to_all(message, 'chip', split_axis=0, concat_axis=0, tiled=True)  7.78 us
    all_to_all x1, waiting for transfers between devices, shards(): lax.all_to_all(message, 'chip', split_axis=0, concat_axis=0, tiled=True)  5.54 us
  transfers between devices with their start and end apart: 7, of which 5 were waited for; matrix products, arithmetic and copies ran while one was open for 2% of the time, Pallas kernels for 15%

commit v1 on v0

v1 whole, which is shorter than its diff:
```python
import jax
import jax.numpy as jnp
import numpy as np
from jax import lax
from jax.experimental import pallas as pl
from jax.experimental.pallas import tpu as pltpu
from jax.sharding import Mesh
from jax.sharding import PartitionSpec as P

TILE = 128
WIDE = 256
BF16 = jnp.bfloat16
F32 = jnp.float32
SLAB = ("across", "along", "core")
SAME_CORE = ("member", "across", "along")
VMEM = pl.BlockSpec(memory_space=pltpu.VMEM)
SMEM = pl.BlockSpec(memory_space=pltpu.SMEM)
HBM = pl.BlockSpec(memory_space=pltpu.HBM)


def run(kernel, out_shape, in_specs, flops, scratch=(), out_specs=None, mib=60):
    outs = out_shape if isinstance(out_shape, list) else [out_shape]
    if out_specs is None:
        out_specs = [VMEM] * len(outs)
    moved = sum(int(np.prod(o.shape)) * o.dtype.itemsize for o in outs) * 2
    call = pl.pallas_call(
        kernel,
        in_specs=in_specs,
        out_specs=out_specs,
        out_shape=outs,
        scratch_shapes=list(scratch),
        compiler_params=pltpu.CompilerParams(vmem_limit_bytes=mib << 20),
        cost_estimate=pl.CostEstimate(flops=flops, bytes_accessed=moved, transcendentals=0),
    )

    def launch(*args):
        results = call(*args)
        return results if isinstance(out_shape, list) else results[0]

    return launch


def bf16(*shape):
    return jax.ShapeDtypeStruct(shape, BF16)


def f32(*shape):
    return jax.ShapeDtypeStruct(shape, F32)


def cas(first, second, order):
    angle = 2.0 * np.pi * (np.outer(first, second) % order) / order
    c, s = np.cos(angle), np.sin(angle)
    return [a.astype(np.float32) for a in (c + s, c - s, c, s)]


def select(core_ref, tile_ref, pert_ref, own_ref, send_ref, tiles, pert, sems):
    members = pert.shape[0]
    core = core_ref[0]
    copies = [pltpu.make_async_copy(tile_ref, tiles, sems.at[members])]
    copies += [pltpu.make_async_copy(pert_ref.at[m], pert.at[m], sems.at[m]) for m in range(members)]
    for copy in copies:
        copy.start()
    copies[0].wait()
    place = tiles[...] // 16
    row = lax.broadcasted_iota(jnp.int32, (TILE, TILE), 0)
    halves = []
    for half in (1 - core, core):
        mine = jnp.where(half == 0, place[0:1, :], place[1:2, :])
        halves.append((mine, jnp.transpose((row == mine).astype(F32)).astype(BF16)))
    for copy in copies[1:]:
        copy.wait()
    for ref, half, (mine, chosen) in zip((send_ref, own_ref), (1 - core, core), halves):
        for k in range(8):
            cols = pl.ds(pl.multiple_of((half * 8 + k) * TILE, TILE), TILE)
            tile = jnp.concatenate(
                [pert[m, :, :, cols].reshape(TILE, TILE) for m in range(members)], axis=1
            )
            rows = jnp.dot(
                chosen[16 * k : 16 * k + 16], tile, preferred_element_type=F32
            ).astype(BF16)
            for m in range(members):
                ref[k * members + m] = rows[:, m * TILE : (m + 1) * TILE]
        ref[8 * members] = jnp.broadcast_to(mine.astype(F32), (16, TILE)).astype(BF16)


def table_factors(factor_ref, width, plus, minus):
    inner = 64
    outer = width // inner
    near_p = factor_ref[2 * outer : 2 * outer + inner, :]
    near_m = factor_ref[2 * outer + inner : 2 * outer + 2 * inner, :]
    for u in range(outer):
        at = slice(u * inner, (u + 1) * inner)
        c, s = factor_ref[u : u + 1, :], factor_ref[outer + u : outer + u + 1, :]
        plus[at, :] = c * near_p + s * near_m
        minus[at, :] = c * near_m - s * near_p


def transform(which, scaled, lead_ref, plus, minus, block_ref, table_ref, sems, target):
    width = plus.shape[0]
    members, depth, _ = target.shape
    half = width // WIDE // 2

    def copy(nb, slot):
        return pltpu.make_async_copy(block_ref.at[slot], table_ref.at[nb], sems.at[slot])

    def step(n, carry):
        nb = which * half + n
        slot = lax.rem(n, 2)

        @pl.when(n >= 2)
        def _():
            copy(n - 2, slot).wait()

        for q in range(WIDE // TILE):
            c = lead_ref[0, nb * (WIDE // TILE) + q]
            s = lead_ref[1, nb * (WIDE // TILE) + q]
            c = jnp.broadcast_to(c[None], (width // 16, 16, TILE)).reshape(width, TILE)
            s = jnp.broadcast_to(s[None], (width // 16, 16, TILE)).reshape(width, TILE)
            block_ref[slot, :, q * TILE : (q + 1) * TILE] = (
                c * plus[...] + s * minus[...]
            ).astype(BF16)
        copy(n, slot).start()
        product = jnp.dot(scaled[...], block_ref[slot], preferred_element_type=F32)
        to = pl.ds(pl.multiple_of(n * WIDE, WIDE), WIDE)
        target[:, :, to] = product.astype(BF16).reshape(members, depth, WIDE)
        return carry

    lax.fori_loop(0, half, step, 0)
    for slot in range(2):
        copy(slot, slot).wait()


def forward_send(
    core_ref, control_ref, row_ref, col_ref, factor_ref, lead_ref, after_ref,
    send_ref, scaled_ref, table_ref,
    control, plus, minus, block_ref, sems, reads,
):
    members, levels, rows, width = control.shape
    copies = [
        pltpu.make_async_copy(control_ref.at[m], control.at[m], reads.at[m]) for m in range(members)
    ]
    for copy in copies:
        copy.start()
    table_factors(factor_ref, width, plus, minus)
    for m in range(members):
        copies[m].wait()
        for l in range(levels):
            amplitude = row_ref[l][:, :1] * col_ref[l : l + 1, :]
            at = (m * levels + l) * rows
            scaled_ref[at : at + rows, :] = (control[m, l] * amplitude).astype(BF16)
    transform(
        1 - core_ref[0], scaled_ref, lead_ref, plus, minus, block_ref, table_ref, sems, send_ref
    )


def forward_own(
    core_ref, scaled_ref, factor_ref, lead_ref, after0_ref, after1_ref,
    own_ref, table_ref, plus, minus, block_ref, sems,
):
    table_factors(factor_ref, plus.shape[0], plus, minus)
    transform(core_ref[0], scaled_ref, lead_ref, plus, minus, block_ref, table_ref, sems, own_ref)


def chip_of(place_ref, h):
    across, along = place_ref[0], place_ref[1]
    return ((across + h // 4) % 2) * 4 + (along + h % 4) % 4


def spread_rows(place_ref, factor_ref, lead_ref, out_ref):
    core = place_ref[2]
    rows = out_ref.shape[1] // 4
    inner_p, inner_m = factor_ref[:rows, :], factor_ref[rows : 2 * rows, :]
    plus, minus = [], []
    for q in range(2):
        slab = chip_of(place_ref, 0) * 2 + (core + q) % 2
        c = jnp.broadcast_to(lead_ref[0, slab][None], (rows // 16, 16, TILE)).reshape(rows, TILE)
        s = jnp.broadcast_to(lead_ref[1, slab][None], (rows // 16, 16, TILE)).reshape(rows, TILE)
        plus.append(c * inner_p + s * inner_m)
        minus.append(c * inner_m - s * inner_p)
    left = lax.broadcasted_iota(jnp.int32, (rows, TILE), 1) < rows
    plus = jnp.where(left, plus[0], plus[1])
    minus = jnp.where(left, minus[0], minus[1])
    nothing = jnp.zeros((rows, TILE), BF16)
    for h in range(out_ref.shape[0]):
        for r in range(2):
            slab = chip_of(place_ref, h) * 2 + (core + r) % 2
            c = factor_ref[pl.ds(2 * rows + slab, 1), :]
            s = factor_ref[pl.ds(2 * rows + 16 + slab, 1), :]
            entry = (c * plus + s * minus).astype(BF16)
            for l in range(2):
                at = slice((2 * l + r) * rows, (2 * l + r + 1) * rows)
                out_ref[h, at, l * TILE : (l + 1) * TILE] = entry
                out_ref[h, at, (1 - l) * TILE : (2 - l) * TILE] = nothing


def pert_of(blocks, at):
    return jnp.concatenate([ref[:, at].reshape(-1, TILE) for ref in blocks], axis=0).astype(F32)


def cells(place_ref, *refs):
    blocks, (own_hbm, par_hbm, rows_ref, cells_hbm, turned_hbm) = refs[:8], refs[8:13]
    own, par, spread, cells_ref, turned_ref, reads, writes = refs[13:]
    members, depth, _ = own.shape
    rows = depth // 2
    last = blocks[0].shape[1] - 1
    loads = [
        pltpu.make_async_copy(own_hbm, own, reads.at[0]),
        pltpu.make_async_copy(par_hbm, par, reads.at[1]),
    ]
    for load in loads:
        load.start()
    lane = lax.broadcasted_iota(jnp.int32, (1, 2 * TILE), 1)
    row = lax.broadcasted_iota(jnp.int32, (4 * rows, 2 * TILE), 0)
    for h, block in enumerate(blocks):
        place = jnp.concatenate(
            [block[r, last].astype(F32)[0:1, :] for r in range(2)], axis=1
        ).astype(jnp.int32)
        level, inside = place // rows, place % rows
        place = level * (2 * rows) + inside + jnp.where(lane < TILE, 0, rows)
        chosen = (row == place).astype(F32).astype(BF16)
        spread[h] = lax.dot_general(
            chosen, rows_ref[h], (((0,), (0,)), ((), ())), preferred_element_type=F32
        ).astype(BF16)
    for load in loads:
        load.wait()
    stores = []
    for k in range(8):
        cols = slice(k * TILE, (k + 1) * TILE)
        along = jnp.concatenate(
            [
                jnp.concatenate(
                    [ref[m, l * rows : (l + 1) * rows, cols] for m in range(members)], axis=1
                )
                for l in range(2)
                for ref in (own, par)
            ],
            axis=0,
        )
        tiles = jnp.concatenate(
            [
                spread[h, r * TILE + k * 16 : r * TILE + (k + 1) * 16, :]
                for h in range(8)
                for r in range(2)
            ],
            axis=0,
        )
        field = jnp.dot(tiles, along, preferred_element_type=F32)
        total = None
        for m in range(members):
            term = pert_of(blocks, k * members + m) * field[:, m * TILE : (m + 1) * TILE]
            total = term if total is None else total + term
        total = total.astype(BF16)
        for h in range(8):
            cells_ref[k, chip_of(place_ref, h)] = total[h * 32 : (h + 1) * 32]
        stores.append(pltpu.make_async_copy(cells_ref.at[k], cells_hbm.at[k], writes.at[k]))
        stores[-1].start()
        turned = jnp.transpose(tiles.astype(F32)).astype(BF16)
        for q in range(2):
            for l in range(2):
                at = (2 * l + q) * rows
                turned_ref[k, (2 * q + l) * rows : (2 * q + l + 1) * rows, :] = turned[at : at + rows]
    stores.append(pltpu.make_async_copy(turned_ref, turned_hbm, writes.at[8]))
    stores[-1].start()
    for store in stores:
        store.wait()


def score(cells_ref, own_ref, lent_ref, out_ref):
    copies = out_ref.shape[0]
    total = jnp.sum(cells_ref[...].astype(F32), axis=0)
    value = jnp.concatenate([own_ref[0], lent_ref[0]], axis=0)
    seen = jnp.concatenate([own_ref[1], lent_ref[1]], axis=0)
    resid = total - value
    result = jnp.where(seen > 0.5, resid / jnp.sqrt(1.0 + resid * resid * 0.25), 0.0)
    result = result.astype(BF16)
    for i in range(copies):
        out_ref[i] = result


def back(place_ref, *refs):
    blocks, (score_ref, turned_hbm, own_ref, par_ref, turned, sem) = refs[:8], refs[8:]
    members, depth, _ = own_ref.shape
    load = pltpu.make_async_copy(turned_hbm, turned, sem)
    load.start()
    for k in range(8):
        weight = jnp.concatenate(
            [score_ref[k, chip_of(place_ref, h)] for h in range(8)], axis=0
        ).astype(F32)
        weighted = jnp.concatenate(
            [(pert_of(blocks, k * members + m) * weight).astype(BF16) for m in range(members)],
            axis=1,
        )
        if k == 0:
            load.wait()
        result = jnp.dot(turned[k], weighted, preferred_element_type=F32).astype(BF16)
        for m in range(members):
            part = result[:, m * TILE : (m + 1) * TILE]
            own_ref[m, :, k * TILE : (k + 1) * TILE] = part[:depth]
            par_ref[m, :, k * TILE : (k + 1) * TILE] = part[depth:]


def streamed(tables, rows, block_ref, sems):
    steps = tables[0].shape[0]

    def fetch(i, n, slot):
        return pltpu.make_async_copy(tables[i].at[n, rows, :], block_ref.at[slot], sems.at[slot])

    def at(i, n):
        slot = lax.rem(n, 2)

        @pl.when(n + 1 < steps)
        def _():
            fetch(i, n + 1, 1 - slot).start()

        if i + 1 < len(tables):

            @pl.when(n + 1 == steps)
            def _():
                fetch(i + 1, 0, 1 - slot).start()

        fetch(i, n, slot).wait()
        return block_ref[slot]

    fetch(0, 0, 0).start()
    return at


def inverse_own(core_ref, own_ref, table0_ref, table1_ref, sum_ref, block_ref, sems):
    members, depth, width = own_ref.shape
    near = pl.ds(pl.multiple_of(core_ref[0] * width, width), width)
    half = table0_ref.shape[0]
    core = core_ref[0]
    block = streamed((table0_ref, table1_ref), near, block_ref, sems)
    for i in range(2):
        which = (1 - core) if i == 0 else core

        def step(n, carry, i=i, which=which):
            sum_ref[which * half + n] = jnp.dot(
                own_ref[...].reshape(members * depth, width),
                block(i, n),
                preferred_element_type=F32,
            )
            return carry

        lax.fori_loop(0, half, step, 0)


def inverse_par(
    core_ref, par_ref, sum_ref, table0_ref, table1_ref, row_ref, col_ref, out_ref,
    piece, sems, block_ref, reads,
):
    members, depth, width = par_ref.shape
    levels, rows, _ = row_ref.shape
    core = core_ref[0]
    half = table0_ref.shape[0]
    far = pl.ds(pl.multiple_of((1 - core) * width, width), width)

    def copy(nb, slot):
        cols = pl.ds(pl.multiple_of(nb * WIDE, WIDE), WIDE)
        return pltpu.make_async_copy(piece.at[slot], out_ref.at[:, :, :, cols], sems.at[slot])

    block = streamed((table0_ref, table1_ref), far, block_ref, reads)
    for i in range(2):
        which = (1 - core) if i == 0 else core

        def step(n, carry, i=i, which=which):
            slot = lax.rem(n, 2)
            nb = which * half + n
            cols = pl.ds(pl.multiple_of(nb * WIDE, WIDE), WIDE)
            product = sum_ref[nb] + jnp.dot(
                par_ref[...].reshape(members * depth, width),
                block(i, n),
                preferred_element_type=F32,
            )
            product = product.reshape(members, levels, rows, WIDE)

            @pl.when(n >= (2 if i == 0 else 0))
            def _():
                copy(nb, slot).wait()

            for l in range(levels):
                amplitude = row_ref[l][:, :1] * col_ref[l : l + 1, cols]
                for m in range(members):
                    piece[slot, m, l] = product[m, l] * amplitude
            copy(nb, slot).start()
            return carry

        lax.fori_loop(0, half, step, 0)
    for slot in range(2):
        copy(slot, slot).wait()


def shards(control, perturbation, loc_row, loc_col, obs_tile, obs_count, obs_value):
    members, levels, rows, width = control.shape
    slabs = 16
    peers = lax.axis_size("member") * 8
    height = rows * slabs
    half = width // 2
    per_core = half // TILE
    depth = levels * rows
    across = lax.axis_index("across").astype(jnp.int32)
    along = lax.axis_index("along").astype(jnp.int32)
    core = lax.axis_index("core").astype(jnp.int32)
    group = lax.axis_index("member").astype(jnp.int32)
    core_index = core.reshape(1)
    place = jnp.stack([across, along, core])
    swap = [(0, 1), (1, 0)]

    def from_next(array, step):
        return lax.ppermute(array, "along", [((i + step) % 4, i) for i in range(4)])

    blocks = per_core * members + 1
    own_tiles, send_tiles = run(
        select,
        [bf16(blocks, 16, TILE)] * 2,
        [SMEM, HBM, HBM],
        1 << 27,
        [
            pltpu.VMEM((2, TILE), jnp.int32),
            pltpu.VMEM(perturbation.shape, BF16),
            pltpu.SemaphoreType.DMA((members + 1,)),
        ],
    )(core_index, obs_tile.reshape(2, TILE), perturbation)
    here = jnp.stack([own_tiles, lax.ppermute(send_tiles, "core", swap)])
    facing = lax.ppermute(here, "across", swap)
    here2 = from_next(here, 2)
    here1, here3 = from_next(here, 1), from_next(here, 3)
    facing1, facing3 = from_next(facing, 1), from_next(facing, 3)
    facing2 = lax.ppermute(here2, "across", swap)
    arrived = (here, here1, here2, here3, facing, facing1, facing2, facing3)

    lane = jnp.arange(TILE, dtype=jnp.int32)

    def of_column(column, array):
        return lax.dynamic_slice_in_dim(array, column * 16, 16, 0)

    seen = (lane[None, :] < obs_count[:, None]).astype(F32)
    mine = per_core * core + group
    other = per_core * (1 - core) + group
    stated = jnp.stack([of_column(mine, obs_value), of_column(mine, seen)])
    lent = jnp.stack([of_column(other, obs_value), of_column(other, seen)])
    lent = lax.ppermute(lent, "core", swap)

    lead = cas(np.arange(16), np.arange(16), 16)
    lead = jnp.asarray(np.repeat(np.stack(lead[2:])[:, :, :, None], TILE, axis=3))
    inner = 64
    outer = cas(np.arange(width // inner), np.arange(TILE), width // inner)
    near = cas(np.arange(inner), np.arange(TILE), width)
    root = np.float32(np.sqrt(width))
    factors = jnp.asarray(np.concatenate([outer[2], outer[3], near[0] / root, near[1] / root]))
    wave = np.arange(TILE) % rows
    base = cas(np.arange(rows), wave, height)
    turn = cas(np.arange(16), wave, 16)
    root = np.float32(np.sqrt(height))
    row_factors = jnp.asarray(np.concatenate([base[0] / root, base[1] / root, turn[2], turn[3]]))

    row_b = jnp.broadcast_to(loc_row[:, :, None], (levels, rows, TILE))
    table_half = bf16(width // WIDE // 2, width, WIDE)
    work = [
        pltpu.VMEM((width, TILE), F32),
        pltpu.VMEM((width, TILE), F32),
        pltpu.VMEM((2, width, WIDE), BF16),
        pltpu.SemaphoreType.DMA((2,)),
    ]
    flops = members * depth * width * width
    send, scaled, table0 = run(
        forward_send,
        [bf16(members, depth, half), bf16(members * depth, width), table_half],
        [SMEM, HBM, VMEM, VMEM, VMEM, VMEM, HBM],
        flops,
        [pltpu.VMEM(control.shape, F32)] + work + [pltpu.SemaphoreType.DMA((members,))],
        [VMEM, VMEM, HBM],
    )(core_index, control, row_b, loc_col, factors, lead, here)
    par = lax.ppermute(send, "core", swap)
    own, table1 = run(
        forward_own,
        [bf16(members, depth, half), table_half],
        [SMEM, VMEM, VMEM, VMEM, HBM, HBM],
        flops,
        work,
        [VMEM, HBM],
    )(core_index, scaled, factors, lead, facing, here2)
    table_rows = run(
        spread_rows, bf16(8, 4 * rows, 2 * TILE), [SMEM, VMEM, VMEM], 1 << 22
    )(place, row_factors, lead)

    tiles = slabs * 16
    partial, turned = run(
        cells,
        [bf16(per_core, 8, 2 * 16, TILE), bf16(per_core, 4 * rows, tiles)],
        [SMEM] + [VMEM] * 8 + [HBM, HBM, VMEM],
        1 << 30,
        [
            pltpu.VMEM((members, depth, half), BF16),
            pltpu.VMEM((members, depth, half), BF16),
            pltpu.VMEM((8, tiles, 4 * rows), BF16),
            pltpu.VMEM((per_core, 8, 2 * 16, TILE), BF16),
            pltpu.VMEM((per_core, 4 * rows, tiles), BF16),
            pltpu.SemaphoreType.DMA((2,)),
            pltpu.SemaphoreType.DMA((9,)),
        ],
        [HBM, HBM],
    )(place, *arrived, own, par, table_rows)
    partial = lax.all_to_all(
        partial.reshape(peers, 2 * 16, TILE), SAME_CORE, split_axis=0, concat_axis=0, tiled=True
    )
    scores = run(score, bf16(peers, 2 * 16, TILE), [VMEM] * 3, 1 << 20)(partial, stated, lent)
    scores = lax.all_to_all(scores, SAME_CORE, split_axis=0, concat_axis=0, tiled=True)

    back_own, back_send = run(
        back,
        [bf16(members, depth, half)] * 2,
        [SMEM] + [VMEM] * 9 + [HBM],
        1 << 28,
        [pltpu.VMEM((per_core, 4 * rows, tiles), BF16), pltpu.SemaphoreType.DMA],
        mib=58,
    )(place, *arrived, scores.reshape(per_core, 8, 2 * 16, TILE), turned)
    back_other = lax.ppermute(back_send, "core", swap)
    stream = [pltpu.VMEM((2, half, WIDE), BF16), pltpu.SemaphoreType.DMA((2,))]
    summed = run(
        inverse_own,
        f32(width // WIDE, members * depth, WIDE),
        [SMEM, VMEM, HBM, HBM],
        flops,
        stream,
        mib=54,
    )(core_index, back_own, table0, table1)
    return run(
        inverse_par,
        f32(*control.shape),
        [SMEM, VMEM, VMEM, HBM, HBM, VMEM, VMEM],
        flops,
        [pltpu.VMEM((2, members, levels, rows, WIDE), F32), pltpu.SemaphoreType.DMA((2,))] + stream,
        [HBM],
        mib=54,
    )(core_index, back_other, summed, table0, table1, row_b, loc_col)


def solution(mesh):
    torus = Mesh(
        mesh.devices.reshape(mesh.shape["member"], 2, 4, 2),
        ("member", "across", "along", "core"),
    )
    placed = (
        P("member", None, SLAB, None),
        P("member", None, SLAB, None),
        P(None, SLAB),
        P(),
        P(SLAB),
        P(SLAB),
        P(SLAB, None),
    )
    return jax.shard_map(
        shards,
        mesh=torus,
        in_specs=placed,
        out_specs=P("member", None, SLAB, None),
        check_vma=False,
    )
```

time: 108 us -> 125 us (1.16)
  Pallas kernels: 26.2 us -> 54.9 us
  local copies, waits for them, and re-layouts: 26.9 us -> 5.21 us
  blocking collectives: 0 us -> 16 us
  waiting for transfers between devices: 24.8 us -> 16.1 us
  other arithmetic: 0.88 us -> 2.99 us
    pallas_call x9, Pallas kernels: 26.2 us -> 54.9 us  [launch(): results = call(*args)]
    unnamed x50 -> x26, local copies, waits for them, and re-layouts: 24.5 us -> 3.04 us
    all_to_all x0 -> x1, blocking collectives: none -> 16 us  [shards(): lax.all_to_all(scores, SAME_CORE, split_axis=0, concat_axis=0, tiled=True)]
    all_to_all x2 -> x0, waiting for transfers between devices: 14.1 us -> none  [the longest x1 8.55 us: shards(): lax.all_to_all(scores, SAME_CORE, split_axis=0, concat_axis=0, tiled=True)]
    all_to_all x2 -> x0, starting transfers between devices: 13 us -> none  [the longest x1 7.78 us: shards(): lax.all_to_all(message, 'chip', split_axis=0, concat_axis=0, tiled=True)]
    ppermute x1 -> x8, starting transfers between devices: 1.46 us -> 13 us  [the longest x5 8.5 us: from_next(): return lax.ppermute(array, 'along', [((i + step) % 4, i) for i in range(4)])]
    ppermute x1 -> x8, waiting for transfers between devices: 0.99 us -> 9.64 us  [the longest x5 7.63 us: from_next(): return lax.ppermute(array, 'along', [((i + step) % 4, i) for i in range(4)])]
    all_to_all x1, waiting for transfers between devices: 8.85 us -> 6.24 us  [shards(): lax.all_to_all(partial.reshape(peers, 2 * 16, TILE), SAME_CORE, split_axi...]
  transfers between devices with their start and end apart: 7 -> 12, of which waited for: 5 -> 6; matrix products, arithmetic and copies ran while one was open for 2% -> 2% of each run, Pallas kernels for 15% -> 15%
where the time goes in v1:
time: 125 us; the launch traced here: 124 us
  Pallas kernels  54.9 us (44%)
  starting transfers between devices  28.7 us (23%)
  waiting for transfers between devices  16.1 us (13%)
  blocking collectives  16 us (13%)
  local copies, waits for them, and re-layouts  5.21 us (4%)
  other arithmetic  2.99 us (2%)
    pallas_call x9, Pallas kernels, launch(): results = call(*args)  54.9 us
    all_to_all x1, blocking collectives, shards(): lax.all_to_all(scores, SAME_CORE, split_axis=0, concat_axis=0, tiled=True)  16 us
    ppermute x5, starting transfers between devices, from_next(): return lax.ppermute(array, 'along', [((i + step) % 4, i) for i in range(4)])  8.5 us
    all_to_all x1, starting transfers between devices, shards(): lax.all_to_all(partial.reshape(peers, 2 * 16, TILE), SAME_CORE, split_axi...  7.69 us
    ppermute x5, waiting for transfers between devices, from_next(): return lax.ppermute(array, 'along', [((i + step) % 4, i) for i in range(4)])  7.63 us
    all_to_all x1, waiting for transfers between devices, shards(): lax.all_to_all(partial.reshape(peers, 2 * 16, TILE), SAME_CORE, split_axi...  6.24 us
    ppermute x1, starting transfers between devices, shards(): back_other = lax.ppermute(back_send, 'core', swap)  4.83 us
    unnamed x26, local copies, waits for them, and re-layouts  3.04 us
  transfers between devices with their start and end apart: 12, of which 6 were waited for; matrix products, arithmetic and copies ran while one was open for 2% of the time, Pallas kernels for 15%

profile of v1, /device:TPU:1, one launch (start us, length us, event | category | flops | bytes accessed | tf_op | source)
XLA Modules:
  0.0 124.1 jit_solution(14457438064645710105)
XLA Ops:
  0.0 2.9 %shard_map.100 = (bf16[33,16,128]{2,1,0:T(8,128)(2,1)}, bf16[33,16,128]{2,1,0:T(8,128)(2,1)}) custom-call(s32[1]{0:T(128)} %bitcast.core_ref, s32[2,128]{1,0:T(2,128)} %bitcast.20, bf16[4,2,64,2048]{3,2,1,0:T(8,128)(2,1)} %pert_ref.1), custom_call_target="tpu_custom_call" | custom-call | flops 134217728 | bytes 540672 | tf_op jit(solution)/shard_map/pallas_call | solution.py:37
  2.9 1.5 %collective-permute-start = (bf16[33,16,128]{2,1,0:T(8,128)(2,1)}, bf16[33,16,128]{2,1,0:T(8,128)(2,1)S(1)}, u32[]{:S(2)}, u32[]{:S(2)}) collective-permute-start(bf16[33,16,128]{2,1,0:T(8,128)(2,1)} %get-tuple-element.17), channel_id=1, source_target_pairs={{0,1},{1,0},{2,3},{3,2},{4,5},{5,4},{6,7},{7,6},{8,9},{9,8},{10,11... | collective-permute-start | bytes 405512 | tf_op jit(solution)/shard_map/ppermute | solution.py:425
  4.4 1.2 collective-permute-done
  5.6 1.6 %pad_maximum_fusion.after_ref.refs_0_ = bf16[2,33,16,128]{3,2,1,0:T(8,128)(2,1)} fusion(bf16[1,33,16,128]{3,2,1,0:T(8,128)(2,1)S(1)} %bitcast.19, bf16[1,33,16,128]{3,2,1,0:T(8,128)(2,1)} %bitcast.18), kind=kLoop, calls=%fused_computation | loop fusion | flops 135168 | bytes 540672 | tf_op jit(solution)/shard_map/stack | solution.py:425
  7.2 1.4 %broadcast_in_dim.2.row_ref = f32[2,64,128]{2,1,0:T(8,128)} broadcast(f32[2,64]{1,0:T(2,128)} %param.12), dimensions={0,1} | broadcast | bytes 66048 | tf_op jit(solution)/shard_map/broadcast_in_dim | solution.py:458
  8.6 9.2 %shard_map.101 = (bf16[4,128,1024]{2,1,0:T(8,128)(2,1)}, bf16[512,2048]{1,0:T(8,128)(2,1)}, bf16[4,2048,256]{2,1,0:T(8,128)(2,1)}) custom-call(s32[1]{0:T(128)} %bitcast.core_ref, f32[4,2,64,2048]{3,2,1,0:T(8,128)} %control_ref.1, f32[2,64,128]{2,1,0:T(8,128)} %broadcast_in_dim.2.row_ref, f32[2,2048]{1,0:T(2,128)} %col_ref.3, ...), custom_call_target="tpu_custom_call" | custom-call | flops 2147483648 | bytes 14680064 | tf_op jit(solution)/shard_map/pallas_call | solution.py:37
  17.8 0.4 collective-permute-start.8
  18.2 3.0 %collective-permute-start.4 = (bf16[2,33,16,128]{3,2,1,0:T(8,128)(2,1)S(1)}, bf16[2,33,16,128]{3,2,1,0:T(8,128)(2,1)S(1)}, u32[]{:S(2)}, u32[]{:S(2)}) collective-permute-start(bf16[2,33,16,128]{3,2,1,0:T(8,128)(2,1)S(1)} %copy-done), channel_id=1, source_target_pairs={{0,8},{8,0},{1,9},{9,1},{2,10},{10,2},{3,11},{11,3},{4,12},{12,4},... | collective-permute-start | bytes 811016 | tf_op jit(solution)/shard_map/ppermute | solution.py:426
  21.3 1.6 %collective-permute-start.3 = (bf16[2,33,16,128]{3,2,1,0:T(8,128)(2,1)S(1)}, bf16[2,33,16,128]{3,2,1,0:T(8,128)(2,1)S(1)}, u32[]{:S(2)}, u32[]{:S(2)}) collective-permute-start(bf16[2,33,16,128]{3,2,1,0:T(8,128)(2,1)S(1)} %copy-done), channel_id=1, source_target_pairs={{6,0},{0,2},{2,4},{4,6},{7,1},{1,3},{3,5},{5,7},{14,8},{8,10},{10,... | collective-permute-start | bytes 811016 | tf_op jit(solution)/shard_map/ppermute | solution.py:411
  22.9 3.3 %collective-permute-start.2 = (bf16[2,33,16,128]{3,2,1,0:T(8,128)(2,1)S(1)}, bf16[2,33,16,128]{3,2,1,0:T(8,128)(2,1)S(1)}, u32[]{:S(2)}, u32[]{:S(2)}) collective-permute-start(bf16[2,33,16,128]{3,2,1,0:T(8,128)(2,1)S(1)} %copy-done), channel_id=1, source_target_pairs={{4,0},{6,2},{0,4},{2,6},{5,1},{7,3},{1,5},{3,7},{12,8},{14,10},{8,... | collective-permute-start | bytes 811016 | tf_op jit(solution)/shard_map/ppermute | solution.py:411
  26.2 0.7 collective-permute-start.1
  26.9 0.8 collective-permute-done.4.after0_ref.refs_4_
  27.7 1.6 %collective-permute-start.7 = (bf16[2,33,16,128]{3,2,1,0:T(8,128)(2,1)S(1)}, bf16[2,33,16,128]{3,2,1,0:T(8,128)(2,1)S(1)}, u32[]{:S(2)}, u32[]{:S(2)}) collective-permute-start(bf16[2,33,16,128]{3,2,1,0:T(8,128)(2,1)S(1)} %collective-permute-done.4.after0_ref.refs_4_), channel_id=1, source_target_pairs={{6,0},{0,2},{2,4},{4,6},{7,1},{1,3},{3,5},{5,7},{14,8},{8,10},{10,... | collective-permute-start | bytes 811016 | tf_op jit(solution)/shard_map/ppermute | solution.py:411
  29.4 2.1 %collective-permute-done.3.refs_3_ = bf16[2,33,16,128]{3,2,1,0:T(8,128)(2,1)S(1)} collective-permute-done((bf16[2,33,16,128]{3,2,1,0:T(8,128)(2,1)S(1)}, bf16[2,33,16,128]{3,2,1,0:T(8,128)(2,1)S(1)}, u32[]{:S(2)}, u32[]{:S(2)}) %collective-permute-start.3) | collective-permute-done | bytes 270368 | tf_op jit(solution)/shard_map/ppermute | solution.py:411
  31.5 1.2 collective-permute-start.5
  32.6 5.6 %collective-permute-done.2.after1_ref.refs_2_ = bf16[2,33,16,128]{3,2,1,0:T(8,128)(2,1)S(1)} collective-permute-done((bf16[2,33,16,128]{3,2,1,0:T(8,128)(2,1)S(1)}, bf16[2,33,16,128]{3,2,1,0:T(8,128)(2,1)S(1)}, u32[]{:S(2)}, u32[]{:S(2)}) %collective-permute-start.2) | collective-permute-done | bytes 270368 | tf_op jit(solution)/shard_map/ppermute | solution.py:411
  38.2 0.0 collective-permute-start.6
  38.2 0.7 pad_add_fusion.place_ref
  38.9 2.1 %shard_map.103.refs_10_ = bf16[8,256,256]{2,1,0:T(8,128)(2,1)} custom-call(s32[3]{0:T(128)} %pad_add_fusion.place_ref, f32[160,128]{1,0:T(8,128)} %constant.34.clone.factor_ref, f32[2,16,16,128]{3,2,1,0:T(8,128)} %constant.32.clone.lead_ref), custom_call_target="tpu_custom_call" | custom-call | flops 4194304 | bytes 2097152 | tf_op jit(solution)/shard_map/pallas_call | solution.py:37
  41.0 7.0 %shard_map.102 = (bf16[4,128,1024]{2,1,0:T(8,128)(2,1)}, bf16[4,2048,256]{2,1,0:T(8,128)(2,1)}) custom-call(s32[1]{0:T(128)} %bitcast.core_ref, bf16[512,2048]{1,0:T(8,128)(2,1)} %get-tuple-element.18.scaled_ref, f32[192,128]{1,0:T(8,128)} %constant.33.clone.factor_ref, f32[2,16,16,128]{3,2,1,0:T(8,128)} %constant.32.clone.lead_ref, ...), custom_call_target="tpu_custom_call" | custom-call | flops 2147483648 | bytes 10485760 | tf_op jit(solution)/shard_map/pallas_call | solution.py:37
  48.1 0.0 copy-start.12
  48.1 0.0 collective-permute-done.1.refs_1_
  48.1 0.0 collective-permute-done.7.refs_7_
  48.2 0.0 collective-permute-done.5.refs_5_
  48.2 0.0 collective-permute-done.6.refs_6_
  48.2 0.0 collective-permute-done.8.refs_9_
  48.2 0.0 copy-start.10
  48.2 0.6 copy-done.5
  48.8 0.1 copy-done.6
  48.9 0.1 copy-done.7
  49.0 0.1 copy-done.8
  49.1 0.3 copy-done.10
  49.4 5.7 %shard_map.104 = (bf16[8,8,32,128]{3,2,1,0:T(8,128)(2,1)}, bf16[8,256,256]{2,1,0:T(8,128)(2,1)}) custom-call(s32[3]{0:T(128)} %pad_add_fusion.place_ref, bf16[2,33,16,128]{3,2,1,0:T(8,128)(2,1)} %pad_maximum_fusion.after_ref.refs_0_, bf16[2,33,16,128]{3,2,1,0:T(8,128)(2,1)} %copy-done.5, bf16[2,33,16,128]{3,2,1,0:T(8,128)(2,1)} %copy-done.4, ...), custom_call_target="tpu_custom_call" | custom-call | flops 1073741824 | bytes 3145728 | tf_op jit(solution)/shard_map/pallas_call | solution.py:37
  55.2 7.7 %all-to-all-start = ((bf16[64,32,128]{2,1,0:T(8,128)(2,1)}), bf16[64,32,128]{2,1,0:T(8,128)(2,1)S(1)}, u32[]{:S(2)}, u32[]{:S(2)}) async-start(bf16[64,32,128]{2,1,0:T(8,128)(2,1)} %bitcast.17), calls=%async_computation | async-start | bytes 1048576 | tf_op jit(solution)/shard_map/all_to_all | solution.py:505
  62.9 0.1 fusion
  63.0 0.7 dynamic-slice_bitcast_fusion
  63.7 2.7 %collective-permute-start.9 = (f32[2,16,128]{2,1,0:T(8,128)S(1)}, f32[2,16,128]{2,1,0:T(8,128)S(1)}, u32[]{:S(2)}, u32[]{:S(2)}) collective-permute-start(f32[2,16,128]{2,1,0:T(8,128)S(1)} %pad_maximum_fusion.2), channel_id=1, source_target_pairs={{0,1},{1,0},{2,3},{3,2},{4,5},{5,4},{6,7},{7,6},{8,9},{9,8},{10,11... | collective-permute-start | bytes 49160 | tf_op jit(solution)/shard_map/ppermute | solution.py:443
  66.4 0.6 pad_maximum_fusion.1.own_ref
  67.0 0.2 collective-permute-done.9.lent_ref
  67.3 6.2 %all-to-all-done.cells_ref = bf16[64,32,128]{2,1,0:T(8,128)(2,1)S(1)} async-done(((bf16[64,32,128]{2,1,0:T(8,128)(2,1)}), bf16[64,32,128]{2,1,0:T(8,128)(2,1)S(1)}, u32[]{:S(2)}, u32[]{:S(2)}) %all-to-all-start) | async-done | bytes 524320 | tf_op jit(solution)/shard_map/all_to_all | solution.py:505
  73.5 0.8 copy-done.1
  74.3 2.0 %shard_map.105 = bf16[64,32,128]{2,1,0:T(8,128)(2,1)} custom-call(bf16[64,32,128]{2,1,0:T(8,128)(2,1)} %copy-done.1, f32[2,16,128]{2,1,0:T(8,128)} %pad_maximum_fusion.1.own_ref, f32[2,16,128]{2,1,0:T(8,128)} %copy-done.11), custom_call_target="tpu_custom_call" | custom-call | flops 1048576 | bytes 1048576 | tf_op jit(solution)/shard_map/pallas_call | solution.py:37
  76.3 16.0 %all_to_all.10 = bf16[64,32,128]{2,1,0:T(8,128)(2,1)} all-to-all(bf16[64,32,128]{2,1,0:T(8,128)(2,1)} %shard_map.105), channel_id=1, replica_groups=mesh['member'=8,'across'=2,'along'=4,'core'=2] {'member','across','along'}, dimensions={0} | all-to-all | bytes 1048576 | tf_op jit(solution)/shard_map/all_to_all | solution.py:509
  92.3 5.1 %shard_map.106 = (bf16[4,128,1024]{2,1,0:T(8,128)(2,1)}, bf16[4,128,1024]{2,1,0:T(8,128)(2,1)}) custom-call(s32[3]{0:T(128)} %pad_add_fusion.place_ref, bf16[2,33,16,128]{3,2,1,0:T(8,128)(2,1)} %pad_maximum_fusion.after_ref.refs_0_, bf16[2,33,16,128]{3,2,1,0:T(8,128)(2,1)} %copy-done.5, bf16[2,33,16,128]{3,2,1,0:T(8,128)(2,1)} %copy-done.4, ...), custom_call_target="tpu_custom_call" | custom-call | flops 268435456 | bytes 4194304 | tf_op jit(solution)/shard_map/pallas_call | solution.py:37
  97.5 4.8 %collective-permute-start.10 = (bf16[4,128,1024]{2,1,0:T(8,128)(2,1)}, bf16[4,128,1024]{2,1,0:T(8,128)(2,1)S(1)}, u32[]{:S(2)}, u32[]{:S(2)}) collective-permute-start(bf16[4,128,1024]{2,1,0:T(8,128)(2,1)} %get-tuple-element.23), channel_id=1, source_target_pairs={{0,1},{1,0},{2,3},{3,2},{4,5},{5,4},{6,7},{7,6},{8,9},{9,8},{10,11... | collective-permute-start | bytes 3145736 | tf_op jit(solution)/shard_map/ppermute | solution.py:519
  102.3 9.8 %shard_map.107.sum_ref = f32[8,512,256]{2,1,0:T(8,128)} custom-call(s32[1]{0:T(128)} %bitcast.core_ref, bf16[4,128,1024]{2,1,0:T(8,128)(2,1)} %get-tuple-element.24.own_ref, bf16[4,2048,256]{2,1,0:T(8,128)(2,1)} %get-tuple-element.25.table0_ref, bf16[4,2048,256]{2,1,0:T(8,128)(2,1)} %get-tuple-element.26.table1_ref), custom_call_target="tpu_custom_call" | custom-call | flops 2147483648 | bytes 8388608 | tf_op jit(solution)/shard_map/pallas_call | solution.py:37
  112.1 1.0 copy-done.9
  113.1 11.0 %shard_map.108 = f32[4,2,64,2048]{3,2,1,0:T(8,128)} custom-call(s32[1]{0:T(128)} %bitcast.core_ref, bf16[4,128,1024]{2,1,0:T(8,128)(2,1)} %copy-done.9, f32[8,512,256]{2,1,0:T(8,128)} %shard_map.107.sum_ref, bf16[4,2048,256]{2,1,0:T(8,128)(2,1)} %get-tuple-element.25.table0_ref, bf16[4,2048,256]{2,1,0:T(8,128)(2,1)} %get-tuple-element.26.table1_ref, ...), custom_call_target="tpu_custom_call" | custom-call | flops 2147483648 | bytes 8388608 | tf_op jit(solution)/shard_map/pallas_call | solution.py:37
  (19 shorter events, 0.0 us)
Async XLA Ops:
  2.9 2.7 %collective-permute-start = (bf16[33,16,128]{2,1,0:T(8,128)(2,1)}, bf16[33,16,128]{2,1,0:T(8,128)(2,1)S(1)}, u32[]{:S(2)}, u32[]{:S(2)}) collective-permute-start(bf16[33,16,128]{2,1,0:T(8,128)(2,1)} %get-tuple-element.17), channel_id=1, source_target_pairs={{0,1},{1,0},{2,3},{3,2},{4,5},{5,4},{6,7},{7,6},{8,9},{9,8},{10,11... | collective-permute-start | bytes 405512 | tf_op jit(solution)/shard_map/ppermute | solution.py:425
  7.2 11.0 %copy-start = (bf16[2,33,16,128]{3,2,1,0:T(8,128)(2,1)S(1)}, bf16[2,33,16,128]{3,2,1,0:T(8,128)(2,1)}, u32[]{:S(2)}) copy-start(bf16[2,33,16,128]{3,2,1,0:T(8,128)(2,1)} %pad_maximum_fusion.after_ref.refs_0_) | copy-start | bytes 811012
  17.8 30.4 %collective-permute-start.8 = (bf16[4,128,1024]{2,1,0:T(8,128)(2,1)}, bf16[4,128,1024]{2,1,0:T(8,128)(2,1)S(1)}, u32[]{:S(2)}, u32[]{:S(2)}) collective-permute-start(bf16[4,128,1024]{2,1,0:T(8,128)(2,1)} %get-tuple-element.20), channel_id=1, source_target_pairs={{0,1},{1,0},{2,3},{3,2},{4,5},{5,4},{6,7},{7,6},{8,9},{9,8},{10,11... | collective-permute-start | bytes 3145736 | tf_op jit(solution)/shard_map/ppermute | solution.py:475
  18.2 9.5 %collective-permute-start.4 = (bf16[2,33,16,128]{3,2,1,0:T(8,128)(2,1)S(1)}, bf16[2,33,16,128]{3,2,1,0:T(8,128)(2,1)S(1)}, u32[]{:S(2)}, u32[]{:S(2)}) collective-permute-start(bf16[2,33,16,128]{3,2,1,0:T(8,128)(2,1)S(1)} %copy-done), channel_id=1, source_target_pairs={{0,8},{8,0},{1,9},{9,1},{2,10},{10,2},{3,11},{11,3},{4,12},{12,4},... | collective-permute-start | bytes 811016 | tf_op jit(solution)/shard_map/ppermute | solution.py:426
  21.3 10.2 %collective-permute-start.3 = (bf16[2,33,16,128]{3,2,1,0:T(8,128)(2,1)S(1)}, bf16[2,33,16,128]{3,2,1,0:T(8,128)(2,1)S(1)}, u32[]{:S(2)}, u32[]{:S(2)}) collective-permute-start(bf16[2,33,16,128]{3,2,1,0:T(8,128)(2,1)S(1)} %copy-done), channel_id=1, source_target_pairs={{6,0},{0,2},{2,4},{4,6},{7,1},{1,3},{3,5},{5,7},{14,8},{8,10},{10,... | collective-permute-start | bytes 811016 | tf_op jit(solution)/shard_map/ppermute | solution.py:411
  22.9 15.3 %collective-permute-start.2 = (bf16[2,33,16,128]{3,2,1,0:T(8,128)(2,1)S(1)}, bf16[2,33,16,128]{3,2,1,0:T(8,128)(2,1)S(1)}, u32[]{:S(2)}, u32[]{:S(2)}) collective-permute-start(bf16[2,33,16,128]{3,2,1,0:T(8,128)(2,1)S(1)} %copy-done), channel_id=1, source_target_pairs={{4,0},{6,2},{0,4},{2,6},{5,1},{7,3},{1,5},{3,7},{12,8},{14,10},{8,... | collective-permute-start | bytes 811016 | tf_op jit(solution)/shard_map/ppermute | solution.py:411
  26.2 21.9 %collective-permute-start.1 = (bf16[2,33,16,128]{3,2,1,0:T(8,128)(2,1)S(1)}, bf16[2,33,16,128]{3,2,1,0:T(8,128)(2,1)S(1)}, u32[]{:S(2)}, u32[]{:S(2)}) collective-permute-start(bf16[2,33,16,128]{3,2,1,0:T(8,128)(2,1)S(1)} %copy-done), channel_id=1, source_target_pairs={{2,0},{4,2},{6,4},{0,6},{3,1},{5,3},{7,5},{1,7},{10,8},{12,10},{14... | collective-permute-start | bytes 811016 | tf_op jit(solution)/shard_map/ppermute | solution.py:411
  27.7 13.3 %copy-start.2 = (bf16[2,33,16,128]{3,2,1,0:T(8,128)(2,1)}, bf16[2,33,16,128]{3,2,1,0:T(8,128)(2,1)S(1)}, u32[]{:S(2)}) copy-start(bf16[2,33,16,128]{3,2,1,0:T(8,128)(2,1)S(1)} %collective-permute-done.4.after0_ref.refs_4_) | copy-start | bytes 811012
  27.7 20.4 %collective-permute-start.7 = (bf16[2,33,16,128]{3,2,1,0:T(8,128)(2,1)S(1)}, bf16[2,33,16,128]{3,2,1,0:T(8,128)(2,1)S(1)}, u32[]{:S(2)}, u32[]{:S(2)}) collective-permute-start(bf16[2,33,16,128]{3,2,1,0:T(8,128)(2,1)S(1)} %collective-permute-done.4.after0_ref.refs_4_), channel_id=1, source_target_pairs={{6,0},{0,2},{2,4},{4,6},{7,1},{1,3},{3,5},{5,7},{14,8},{8,10},{10,... | collective-permute-start | bytes 811016 | tf_op jit(solution)/shard_map/ppermute | solution.py:411
  31.5 16.6 %copy-start.3 = (bf16[2,33,16,128]{3,2,1,0:T(8,128)(2,1)}, bf16[2,33,16,128]{3,2,1,0:T(8,128)(2,1)S(1)}, u32[]{:S(2)}) copy-start(bf16[2,33,16,128]{3,2,1,0:T(8,128)(2,1)S(1)} %collective-permute-done.3.refs_3_) | copy-start | bytes 811012
  31.5 16.7 %collective-permute-start.5 = (bf16[2,33,16,128]{3,2,1,0:T(8,128)(2,1)S(1)}, bf16[2,33,16,128]{3,2,1,0:T(8,128)(2,1)S(1)}, u32[]{:S(2)}, u32[]{:S(2)}) collective-permute-start(bf16[2,33,16,128]{3,2,1,0:T(8,128)(2,1)S(1)} %collective-permute-done.4.after0_ref.refs_4_), channel_id=1, source_target_pairs={{2,0},{4,2},{6,4},{0,6},{3,1},{5,3},{7,5},{1,7},{10,8},{12,10},{14... | collective-permute-start | bytes 811016 | tf_op jit(solution)/shard_map/ppermute | solution.py:411
  38.2 2.8 %copy-start.4 = (bf16[2,33,16,128]{3,2,1,0:T(8,128)(2,1)}, bf16[2,33,16,128]{3,2,1,0:T(8,128)(2,1)S(1)}, u32[]{:S(2)}) copy-start(bf16[2,33,16,128]{3,2,1,0:T(8,128)(2,1)S(1)} %collective-permute-done.2.after1_ref.refs_2_) | copy-start | bytes 811012
  38.2 10.0 %collective-permute-start.6 = (bf16[2,33,16,128]{3,2,1,0:T(8,128)(2,1)S(1)}, bf16[2,33,16,128]{3,2,1,0:T(8,128)(2,1)S(1)}, u32[]{:S(2)}, u32[]{:S(2)}) collective-permute-start(bf16[2,33,16,128]{3,2,1,0:T(8,128)(2,1)S(1)} %collective-permute-done.2.after1_ref.refs_2_), channel_id=1, source_target_pairs={{0,8},{8,0},{1,9},{9,1},{2,10},{10,2},{3,11},{11,3},{4,12},{12,4},... | collective-permute-start | bytes 811016 | tf_op jit(solution)/shard_map/ppermute | solution.py:430
  48.1 14.8 %copy-start.12 = (s32[256]{0:T(256)S(1)}, s32[256]{0:T(256)}, u32[]{:S(2)}) copy-start(s32[256]{0:T(256)} %param.15) | copy-start | bytes 3076
  48.1 0.7 copy-start.5
  48.1 0.8 copy-start.6
  48.2 0.9 copy-start.7
  48.2 1.0 copy-start.8
  48.2 1.2 %copy-start.10 = (bf16[4,128,1024]{2,1,0:T(8,128)(2,1)}, bf16[4,128,1024]{2,1,0:T(8,128)(2,1)S(1)}, u32[]{:S(2)}) copy-start(bf16[4,128,1024]{2,1,0:T(8,128)(2,1)S(1)} %collective-permute-done.8.refs_9_) | copy-start | bytes 3145732
  55.2 18.4 %all-to-all-start = ((bf16[64,32,128]{2,1,0:T(8,128)(2,1)}), bf16[64,32,128]{2,1,0:T(8,128)(2,1)S(1)}, u32[]{:S(2)}, u32[]{:S(2)}) async-start(bf16[64,32,128]{2,1,0:T(8,128)(2,1)} %bitcast.17), calls=%async_computation | async-start | bytes 1048576 | tf_op jit(solution)/shard_map/all_to_all | solution.py:505
  63.7 3.6 %collective-permute-start.9 = (f32[2,16,128]{2,1,0:T(8,128)S(1)}, f32[2,16,128]{2,1,0:T(8,128)S(1)}, u32[]{:S(2)}, u32[]{:S(2)}) collective-permute-start(f32[2,16,128]{2,1,0:T(8,128)S(1)} %pad_maximum_fusion.2), channel_id=1, source_target_pairs={{0,1},{1,0},{2,3},{3,2},{4,5},{5,4},{6,7},{7,6},{8,9},{9,8},{10,11... | collective-permute-start | bytes 49160 | tf_op jit(solution)/shard_map/ppermute | solution.py:443
  67.3 6.2 %copy-start.11 = (f32[2,16,128]{2,1,0:T(8,128)}, f32[2,16,128]{2,1,0:T(8,128)S(1)}, u32[]{:S(2)}) copy-start(f32[2,16,128]{2,1,0:T(8,128)S(1)} %collective-permute-done.9.lent_ref) | copy-start | bytes 49156
  73.5 0.8 copy-start.1
  97.5 14.6 %collective-permute-start.10 = (bf16[4,128,1024]{2,1,0:T(8,128)(2,1)}, bf16[4,128,1024]{2,1,0:T(8,128)(2,1)S(1)}, u32[]{:S(2)}, u32[]{:S(2)}) collective-permute-start(bf16[4,128,1024]{2,1,0:T(8,128)(2,1)} %get-tuple-element.23), channel_id=1, source_target_pairs={{0,1},{1,0},{2,3},{3,2},{4,5},{5,4},{6,7},{7,6},{8,9},{9,8},{10,11... | collective-permute-start | bytes 3145736 | tf_op jit(solution)/shard_map/ppermute | solution.py:519
  112.1 1.0 copy-start.9

commit v2 on v1

--- a/solution.py
+++ b/solution.py
@@ -18,7 +18,7 @@
 HBM = pl.BlockSpec(memory_space=pltpu.HBM)
 
 
-def run(kernel, out_shape, in_specs, flops, scratch=(), out_specs=None, mib=60):
+def run(kernel, out_shape, in_specs, flops, scratch=(), out_specs=None, mib=24):
     outs = out_shape if isinstance(out_shape, list) else [out_shape]
     if out_specs is None:
         out_specs = [VMEM] * len(outs)
@@ -303,27 +303,19 @@
 def streamed(tables, rows, block_ref, sems):
     steps = tables[0].shape[0]
 
-    def fetch(i, n, slot):
-        return pltpu.make_async_copy(tables[i].at[n, rows, :], block_ref.at[slot], sems.at[slot])
-
-    def at(i, n):
-        slot = lax.rem(n, 2)
-
-        @pl.when(n + 1 < steps)
-        def _():
-            fetch(i, n + 1, 1 - slot).start()
-
-        if i + 1 < len(tables):
-
-            @pl.when(n + 1 == steps)
-            def _():
-                fetch(i + 1, 0, 1 - slot).start()
-
-        fetch(i, n, slot).wait()
-        return block_ref[slot]
-
-    fetch(0, 0, 0).start()
-    return at
+    def fetch(i, n):
+        at = i * steps + n
+        return pltpu.make_async_copy(tables[i].at[n, rows, :], block_ref.at[at], sems.at[at])
+
+    for i in range(len(tables)):
+        for n in range(steps):
+            fetch(i, n).start()
+
+    def block(i, n):
+        fetch(i, n).wait()
+        return block_ref[i * steps + n]
+
+    return block
 
 
 def inverse_own(core_ref, own_ref, table0_ref, table1_ref, sum_ref, block_ref, sems):
@@ -471,6 +463,7 @@
         flops,
         [pltpu.VMEM(control.shape, F32)] + work + [pltpu.SemaphoreType.DMA((members,))],
         [VMEM, VMEM, HBM],
+        mib=48,
     )(core_index, control, row_b, loc_col, factors, lead, here)
     par = lax.ppermute(send, "core", swap)
     own, table1 = run(
@@ -480,6 +473,7 @@
         flops,
         work,
         [VMEM, HBM],
+        mib=48,
     )(core_index, scaled, factors, lead, facing, here2)
     table_rows = run(
         spread_rows, bf16(8, 4 * rows, 2 * TILE), [SMEM, VMEM, VMEM], 1 << 22
@@ -514,17 +508,18 @@
         [SMEM] + [VMEM] * 9 + [HBM],
         1 << 28,
         [pltpu.VMEM((per_core, 4 * rows, tiles), BF16), pltpu.SemaphoreType.DMA],
-        mib=58,
+        mib=24,
     )(place, *arrived, scores.reshape(per_core, 8, 2 * 16, TILE), turned)
     back_other = lax.ppermute(back_send, "core", swap)
-    stream = [pltpu.VMEM((2, half, WIDE), BF16), pltpu.SemaphoreType.DMA((2,))]
+    parts = width // WIDE
+    stream = [pltpu.VMEM((parts, half, WIDE), BF16), pltpu.SemaphoreType.DMA((parts,))]
     summed = run(
         inverse_own,
         f32(width // WIDE, members * depth, WIDE),
         [SMEM, VMEM, HBM, HBM],
         flops,
         stream,
-        mib=54,
+        mib=46,
     )(core_index, back_own, table0, table1)
     return run(
         inverse_par,
@@ -533,7 +528,7 @@
         flops,
         [pltpu.VMEM((2, members, levels, rows, WIDE), F32), pltpu.SemaphoreType.DMA((2,))] + stream,
         [HBM],
-        mib=54,
+        mib=46,
     )(core_index, back_other, summed, table0, table1, row_b, loc_col)
 
 

time: 125 us -> 104 us (0.83)
  Pallas kernels: 54.9 us -> 31.5 us
  local copies, waits for them, and re-layouts: 5.21 us -> 11.5 us
  other arithmetic: 2.99 us -> 0.21 us
    pallas_call x9, Pallas kernels: 54.9 us -> 31.5 us  [launch(): results = call(*args)]
    unnamed x26 -> x28, local copies, waits for them, and re-layouts: 3.04 us -> 9.94 us
    another operation x1, other arithmetic: 1.64 us -> 0.03 us  [shards(): here = jnp.stack([own_tiles, lax.ppermute(send_tiles, 'core', swap)])]
  transfers between devices with their start and end apart: 12 -> 12, of which waited for: 6 -> 7; matrix products, arithmetic and copies ran while one was open for 2% -> 1% of each run, Pallas kernels for 15% -> 10%
where the time goes in v2:
time: 104 us
  Pallas kernels  31.5 us (30%)
  starting transfers between devices  28.4 us (27%)
  waiting for transfers between devices  16.9 us (16%)
  blocking collectives  15.1 us (15%)
  local copies, waits for them, and re-layouts  11.5 us (11%)
    pallas_call x9, Pallas kernels, launch(): results = call(*args)  31.5 us
    all_to_all x1, blocking collectives, shards(): lax.all_to_all(scores, SAME_CORE, split_axis=0, concat_axis=0, tiled=True)  15.1 us
    unnamed x28, local copies, waits for them, and re-layouts  9.94 us
    ppermute x5, starting transfers between devices, from_next(): return lax.ppermute(array, 'along', [((i + step) % 4, i) for i in range(4)])  8.49 us
    ppermute x5, waiting for transfers between devices, from_next(): return lax.ppermute(array, 'along', [((i + step) % 4, i) for i in range(4)])  7.63 us
    all_to_all x1, starting transfers between devices, shards(): lax.all_to_all(partial.reshape(peers, 2 * 16, TILE), SAME_CORE, split_axi...  7.3 us
    all_to_all x1, waiting for transfers between devices, shards(): lax.all_to_all(partial.reshape(peers, 2 * 16, TILE), SAME_CORE, split_axi...  6.24 us
    ppermute x1, starting transfers between devices, shards(): back_other = lax.ppermute(back_send, 'core', swap)  4.97 us
  transfers between devices with their start and end apart: 12, of which 7 were waited for; matrix products, arithmetic and copies ran while one was open for 1% of the time, Pallas kernels for 10%

profile of v2, /device:TPU:1, one launch (start us, length us, event | category | flops | bytes accessed | tf_op | source)
XLA Modules:
  0.0 103.8 jit_solution(1481803393981640426)
XLA Ops:
  0.0 1.6 %copy-done = bf16[4,2,64,2048]{3,2,1,0:T(8,128)(2,1)S(1)} copy-done((bf16[4,2,64,2048]{3,2,1,0:T(8,128)(2,1)S(1)}, bf16[4,2,64,2048]{3,2,1,0:T(8,128)(2,1)}, u32[]{:S(2)}) %copy-start) | copy-done | bytes 2097176
  1.6 0.7 copy-done.8
  2.3 1.0 shard_map.100
  3.2 1.5 %collective-permute-start = (bf16[33,16,128]{2,1,0:T(8,128)(2,1)S(1)}, bf16[33,16,128]{2,1,0:T(8,128)(2,1)S(1)}, u32[]{:S(2)}, u32[]{:S(2)}) collective-permute-start(bf16[33,16,128]{2,1,0:T(8,128)(2,1)S(1)} %get-tuple-element.17), channel_id=1, source_target_pairs={{0,1},{1,0},{2,3},{3,2},{4,5},{5,4},{6,7},{7,6},{8,9},{9,8},{10,11... | collective-permute-start | bytes 405512 | tf_op jit(solution)/shard_map/ppermute | solution.py:417
  4.7 1.0 collective-permute-done
  5.7 0.8 broadcast_in_dim.2.row_ref
  6.5 0.0 copy-start.3
  6.5 0.9 copy-done.3
  7.5 0.7 copy-done.6
  8.2 0.9 copy-done.9
  9.1 7.6 %shard_map.101 = (bf16[4,128,1024]{2,1,0:T(8,128)(2,1)}, bf16[512,2048]{1,0:T(8,128)(2,1)S(1)}, bf16[4,2048,256]{2,1,0:T(8,128)(2,1)}) custom-call(s32[1]{0:T(128)} %bitcast.core_ref, f32[4,2,64,2048]{3,2,1,0:T(8,128)} %control_ref.1, f32[2,64,128]{2,1,0:T(8,128)S(1)} %broadcast_in_dim.2.row_ref, f32[2,2048]{1,0:T(2,128)S(1)} %copy-done.6, ...), custom_call_target="tpu_custom_call" | custom-call | flops 2147483648 | bytes 14680064 | tf_op jit(solution)/shard_map/pallas_call | solution.py:37
  16.8 0.0 copy-start.11
  16.8 1.3 %copy-done.11 = bf16[512,2048]{1,0:T(8,128)(2,1)} copy-done((bf16[512,2048]{1,0:T(8,128)(2,1)}, bf16[512,2048]{1,0:T(8,128)(2,1)S(1)}, u32[]{:S(2)}) %copy-start.11) | copy-done | bytes 2097176
  18.1 0.4 collective-permute-start.8
  18.4 3.0 %collective-permute-start.4 = (bf16[2,33,16,128]{3,2,1,0:T(8,128)(2,1)S(1)}, bf16[2,33,16,128]{3,2,1,0:T(8,128)(2,1)S(1)}, u32[]{:S(2)}, u32[]{:S(2)}) collective-permute-start(bf16[2,33,16,128]{3,2,1,0:T(8,128)(2,1)S(1)} %pad_maximum_fusion.after_ref.refs_0_), channel_id=1, source_target_pairs={{0,8},{8,0},{1,9},{9,1},{2,10},{10,2},{3,11},{11,3},{4,12},{12,4},... | collective-permute-start | bytes 811016 | tf_op jit(solution)/shard_map/ppermute | solution.py:418
  21.5 1.6 %collective-permute-start.3 = (bf16[2,33,16,128]{3,2,1,0:T(8,128)(2,1)S(1)}, bf16[2,33,16,128]{3,2,1,0:T(8,128)(2,1)S(1)}, u32[]{:S(2)}, u32[]{:S(2)}) collective-permute-start(bf16[2,33,16,128]{3,2,1,0:T(8,128)(2,1)S(1)} %pad_maximum_fusion.after_ref.refs_0_), channel_id=1, source_target_pairs={{6,0},{0,2},{2,4},{4,6},{7,1},{1,3},{3,5},{5,7},{14,8},{8,10},{10,... | collective-permute-start | bytes 811016 | tf_op jit(solution)/shard_map/ppermute | solution.py:403
  23.1 3.3 %collective-permute-start.2 = (bf16[2,33,16,128]{3,2,1,0:T(8,128)(2,1)S(1)}, bf16[2,33,16,128]{3,2,1,0:T(8,128)(2,1)S(1)}, u32[]{:S(2)}, u32[]{:S(2)}) collective-permute-start(bf16[2,33,16,128]{3,2,1,0:T(8,128)(2,1)S(1)} %pad_maximum_fusion.after_ref.refs_0_), channel_id=1, source_target_pairs={{4,0},{6,2},{0,4},{2,6},{5,1},{7,3},{1,5},{3,7},{12,8},{14,10},{8,... | collective-permute-start | bytes 811016 | tf_op jit(solution)/shard_map/ppermute | solution.py:403
  26.4 0.7 collective-permute-start.1
  27.1 0.8 collective-permute-done.4.after0_ref.refs_4_
  27.9 1.6 %collective-permute-start.7 = (bf16[2,33,16,128]{3,2,1,0:T(8,128)(2,1)S(1)}, bf16[2,33,16,128]{3,2,1,0:T(8,128)(2,1)S(1)}, u32[]{:S(2)}, u32[]{:S(2)}) collective-permute-start(bf16[2,33,16,128]{3,2,1,0:T(8,128)(2,1)S(1)} %collective-permute-done.4.after0_ref.refs_4_), channel_id=1, source_target_pairs={{6,0},{0,2},{2,4},{4,6},{7,1},{1,3},{3,5},{5,7},{14,8},{8,10},{10,... | collective-permute-start | bytes 811016 | tf_op jit(solution)/shard_map/ppermute | solution.py:403
  29.6 2.1 %collective-permute-done.3.refs_3_ = bf16[2,33,16,128]{3,2,1,0:T(8,128)(2,1)S(1)} collective-permute-done((bf16[2,33,16,128]{3,2,1,0:T(8,128)(2,1)S(1)}, bf16[2,33,16,128]{3,2,1,0:T(8,128)(2,1)S(1)}, u32[]{:S(2)}, u32[]{:S(2)}) %collective-permute-start.3) | collective-permute-done | bytes 270368 | tf_op jit(solution)/shard_map/ppermute | solution.py:403
  31.7 1.2 %collective-permute-start.5 = (bf16[2,33,16,128]{3,2,1,0:T(8,128)(2,1)S(1)}, bf16[2,33,16,128]{3,2,1,0:T(8,128)(2,1)S(1)}, u32[]{:S(2)}, u32[]{:S(2)}) collective-permute-start(bf16[2,33,16,128]{3,2,1,0:T(8,128)(2,1)S(1)} %collective-permute-done.4.after0_ref.refs_4_), channel_id=1, source_target_pairs={{2,0},{4,2},{6,4},{0,6},{3,1},{5,3},{7,5},{1,7},{10,8},{12,10},{14... | collective-permute-start | bytes 811016 | tf_op jit(solution)/shard_map/ppermute | solution.py:403
  32.8 5.6 %collective-permute-done.2.after1_ref.refs_2_ = bf16[2,33,16,128]{3,2,1,0:T(8,128)(2,1)S(1)} collective-permute-done((bf16[2,33,16,128]{3,2,1,0:T(8,128)(2,1)S(1)}, bf16[2,33,16,128]{3,2,1,0:T(8,128)(2,1)S(1)}, u32[]{:S(2)}, u32[]{:S(2)}) %collective-permute-start.2) | collective-permute-done | bytes 270368 | tf_op jit(solution)/shard_map/ppermute | solution.py:403
  38.4 0.1 collective-permute-start.6
  38.4 0.1 pad_add_fusion.place_ref
  38.5 0.7 shard_map.103.refs_10_
  39.2 0.0 copy-start.12
  39.3 1.6 %copy-done.12 = bf16[512,2048]{1,0:T(8,128)(2,1)S(1)} copy-done((bf16[512,2048]{1,0:T(8,128)(2,1)S(1)}, bf16[512,2048]{1,0:T(8,128)(2,1)}, u32[]{:S(2)}) %copy-start.12) | copy-done | bytes 2097176
  40.8 4.5 %shard_map.102 = (bf16[4,128,1024]{2,1,0:T(8,128)(2,1)S(1)}, bf16[4,2048,256]{2,1,0:T(8,128)(2,1)}) custom-call(s32[1]{0:T(128)} %bitcast.core_ref, bf16[512,2048]{1,0:T(8,128)(2,1)S(1)} %copy-done.12, f32[192,128]{1,0:T(8,128)S(1)} %copy-done.10, f32[2,16,16,128]{3,2,1,0:T(8,128)S(1)} %copy-done.4, ...), custom_call_target="tpu_custom_call" | custom-call | flops 2147483648 | bytes 10485760 | tf_op jit(solution)/shard_map/pallas_call | solution.py:37
  45.3 0.0 copy-start.13
  45.4 0.0 collective-permute-done.1.refs_1_
  45.4 0.4 collective-permute-done.6.refs_6_
  45.8 4.0 %shard_map.104 = (bf16[8,8,32,128]{3,2,1,0:T(8,128)(2,1)}, bf16[8,256,256]{2,1,0:T(8,128)(2,1)S(1)}) custom-call(s32[3]{0:T(128)S(1)} %pad_add_fusion.place_ref, bf16[2,33,16,128]{3,2,1,0:T(8,128)(2,1)S(1)} %pad_maximum_fusion.after_ref.refs_0_, bf16[2,33,16,128]{3,2,1,0:T(8,128)(2,1)S(1)} %collective-permute-done.1.refs_1_, ...), custom_call_target="tpu_custom_call" | custom-call | flops 1073741824 | bytes 3145728 | tf_op jit(solution)/shard_map/pallas_call | solution.py:37
  49.7 0.0 copy-start.1
  49.8 1.0 copy-done.1
  50.7 7.3 %all-to-all-start = ((bf16[64,32,128]{2,1,0:T(8,128)(2,1)}), bf16[64,32,128]{2,1,0:T(8,128)(2,1)S(1)}, u32[]{:S(2)}, u32[]{:S(2)}) async-start(bf16[64,32,128]{2,1,0:T(8,128)(2,1)} %bitcast.6), calls=%async_computation | async-start | bytes 1048576 | tf_op jit(solution)/shard_map/all_to_all | solution.py:499
  58.0 0.1 fusion
  58.1 0.7 dynamic-slice_bitcast_fusion
  58.9 2.7 %collective-permute-start.9 = (f32[2,16,128]{2,1,0:T(8,128)S(1)}, f32[2,16,128]{2,1,0:T(8,128)S(1)}, u32[]{:S(2)}, u32[]{:S(2)}) collective-permute-start(f32[2,16,128]{2,1,0:T(8,128)S(1)} %pad_maximum_fusion.2), channel_id=1, source_target_pairs={{0,1},{1,0},{2,3},{3,2},{4,5},{5,4},{6,7},{7,6},{8,9},{9,8},{10,11... | collective-permute-start | bytes 49160 | tf_op jit(solution)/shard_map/ppermute | solution.py:435
  61.6 0.8 collective-permute-done.9.lent_ref
  62.5 6.2 %all-to-all-done.cells_ref = bf16[64,32,128]{2,1,0:T(8,128)(2,1)S(1)} async-done(((bf16[64,32,128]{2,1,0:T(8,128)(2,1)}), bf16[64,32,128]{2,1,0:T(8,128)(2,1)S(1)}, u32[]{:S(2)}, u32[]{:S(2)}) %all-to-all-start) | async-done | bytes 524320 | tf_op jit(solution)/shard_map/all_to_all | solution.py:499
  68.7 0.1 shard_map.105
  68.8 15.1 %all_to_all.10 = bf16[64,32,128]{2,1,0:T(8,128)(2,1)S(1)} all-to-all(bf16[64,32,128]{2,1,0:T(8,128)(2,1)S(1)} %shard_map.105), channel_id=1, replica_groups=mesh['member'=8,'across'=2,'along'=4,'core'=2] {'member','across','along'}, dimensions={0} | all-to-all | bytes 1048576 | tf_op jit(solution)/shard_map/all_to_all | solution.py:503
  84.0 1.2 %copy-done.2 = bf16[8,256,256]{2,1,0:T(8,128)(2,1)S(1)} copy-done((bf16[8,256,256]{2,1,0:T(8,128)(2,1)S(1)}, bf16[8,256,256]{2,1,0:T(8,128)(2,1)}, u32[]{:S(2)}) %copy-start.2) | copy-done | bytes 1048600
  85.2 1.6 %shard_map.106 = (bf16[4,128,1024]{2,1,0:T(8,128)(2,1)S(1)}, bf16[4,128,1024]{2,1,0:T(8,128)(2,1)S(1)}) custom-call(s32[3]{0:T(128)S(1)} %pad_add_fusion.place_ref, bf16[2,33,16,128]{3,2,1,0:T(8,128)(2,1)S(1)} %pad_maximum_fusion.after_ref.refs_0_, bf16[2,33,16,128]{3,2,1,0:T(8,128)(2,1)S(1)} %collective-permute-done.1.refs_1_, ...), custom_call_target="tpu_custom_call" | custom-call | flops 268435456 | bytes 4194304 | tf_op jit(solution)/shard_map/pallas_call | solution.py:37
  86.8 5.0 %collective-permute-start.10 = (bf16[4,128,1024]{2,1,0:T(8,128)(2,1)S(1)}, bf16[4,128,1024]{2,1,0:T(8,128)(2,1)S(1)}, u32[]{:S(2)}, u32[]{:S(2)}) collective-permute-start(bf16[4,128,1024]{2,1,0:T(8,128)(2,1)S(1)} %get-tuple-element.23), channel_id=1, source_target_pairs={{0,1},{1,0},{2,3},{3,2},{4,5},{5,4},{6,7},{7,6},{8,9},{9,8},{10,11... | collective-permute-start | bytes 3145736 | tf_op jit(solution)/shard_map/ppermute | solution.py:513
  91.7 5.1 %shard_map.107.sum_ref = f32[8,512,256]{2,1,0:T(8,128)S(1)} custom-call(s32[1]{0:T(128)} %bitcast.core_ref, bf16[4,128,1024]{2,1,0:T(8,128)(2,1)S(1)} %get-tuple-element.24.own_ref, bf16[4,2048,256]{2,1,0:T(8,128)(2,1)} %get-tuple-element.25.table0_ref, bf16[4,2048,256]{2,1,0:T(8,128)(2,1)} %get-tuple-element.26.table1_ref), custom_call_target="tpu_custom_call" | custom-call | flops 2147483648 | bytes 8388608 | tf_op jit(solution)/shard_map/pallas_call | solution.py:37
  96.8 7.0 %shard_map.108 = f32[4,2,64,2048]{3,2,1,0:T(8,128)} custom-call(s32[1]{0:T(128)} %bitcast.core_ref, bf16[4,128,1024]{2,1,0:T(8,128)(2,1)S(1)} %collective-permute-done.10.par_ref, f32[8,512,256]{2,1,0:T(8,128)S(1)} %shard_map.107.sum_ref, bf16[4,2048,256]{2,1,0:T(8,128)(2,1)} %get-tuple-element.25.table0_ref, ...), custom_call_target="tpu_custom_call" | custom-call | flops 2147483648 | bytes 8388608 | tf_op jit(solution)/shard_map/pallas_call | solution.py:37
  (21 shorter events, 0.1 us)
Async XLA Ops:
  0.0 1.6 %copy-start = (bf16[4,2,64,2048]{3,2,1,0:T(8,128)(2,1)S(1)}, bf16[4,2,64,2048]{3,2,1,0:T(8,128)(2,1)}, u32[]{:S(2)}) copy-start(bf16[4,2,64,2048]{3,2,1,0:T(8,128)(2,1)} %pert_ref.1) | copy-start | bytes 6291460
  1.6 0.7 copy-start.8
  3.2 2.5 %collective-permute-start = (bf16[33,16,128]{2,1,0:T(8,128)(2,1)S(1)}, bf16[33,16,128]{2,1,0:T(8,128)(2,1)S(1)}, u32[]{:S(2)}, u32[]{:S(2)}) collective-permute-start(bf16[33,16,128]{2,1,0:T(8,128)(2,1)S(1)} %get-tuple-element.17), channel_id=1, source_target_pairs={{0,1},{1,0},{2,3},{3,2},{4,5},{5,4},{6,7},{7,6},{8,9},{9,8},{10,11... | collective-permute-start | bytes 405512 | tf_op jit(solution)/shard_map/ppermute | solution.py:417
  5.7 32.8 %copy-start.4 = (f32[2,16,16,128]{3,2,1,0:T(8,128)S(1)}, f32[2,16,16,128]{3,2,1,0:T(8,128)}, u32[]{:S(2)}) copy-start(f32[2,16,16,128]{3,2,1,0:T(8,128)} %constant.32.clone.lead_ref) | copy-start | bytes 786436
  5.7 32.8 %copy-start.5 = (f32[160,128]{1,0:T(8,128)S(1)}, f32[160,128]{1,0:T(8,128)}, u32[]{:S(2)}) copy-start(f32[160,128]{1,0:T(8,128)} %constant.34.clone.factor_ref) | copy-start | bytes 245764
  6.5 1.0 copy-start.3
  7.5 0.7 copy-start.6
  8.2 0.9 copy-start.9
  9.1 30.1 %copy-start.10 = (f32[192,128]{1,0:T(8,128)S(1)}, f32[192,128]{1,0:T(8,128)}, u32[]{:S(2)}) copy-start(f32[192,128]{1,0:T(8,128)} %constant.33.clone.factor_ref) | copy-start | bytes 294916
  16.8 1.3 %copy-start.11 = (bf16[512,2048]{1,0:T(8,128)(2,1)}, bf16[512,2048]{1,0:T(8,128)(2,1)S(1)}, u32[]{:S(2)}) copy-start(bf16[512,2048]{1,0:T(8,128)(2,1)S(1)} %get-tuple-element.18.scaled_ref) | copy-start | bytes 6291460
  18.1 27.7 %collective-permute-start.8 = (bf16[4,128,1024]{2,1,0:T(8,128)(2,1)}, bf16[4,128,1024]{2,1,0:T(8,128)(2,1)}, u32[]{:S(2)}, u32[]{:S(2)}) collective-permute-start(bf16[4,128,1024]{2,1,0:T(8,128)(2,1)} %get-tuple-element.20), channel_id=1, source_target_pairs={{0,1},{1,0},{2,3},{3,2},{4,5},{5,4},{6,7},{7,6},{8,9},{9,8},{10,11... | collective-permute-start | bytes 3145736 | tf_op jit(solution)/shard_map/ppermute | solution.py:468
  18.4 9.5 %collective-permute-start.4 = (bf16[2,33,16,128]{3,2,1,0:T(8,128)(2,1)S(1)}, bf16[2,33,16,128]{3,2,1,0:T(8,128)(2,1)S(1)}, u32[]{:S(2)}, u32[]{:S(2)}) collective-permute-start(bf16[2,33,16,128]{3,2,1,0:T(8,128)(2,1)S(1)} %pad_maximum_fusion.after_ref.refs_0_), channel_id=1, source_target_pairs={{0,8},{8,0},{1,9},{9,1},{2,10},{10,2},{3,11},{11,3},{4,12},{12,4},... | collective-permute-start | bytes 811016 | tf_op jit(solution)/shard_map/ppermute | solution.py:418
  21.5 10.2 %collective-permute-start.3 = (bf16[2,33,16,128]{3,2,1,0:T(8,128)(2,1)S(1)}, bf16[2,33,16,128]{3,2,1,0:T(8,128)(2,1)S(1)}, u32[]{:S(2)}, u32[]{:S(2)}) collective-permute-start(bf16[2,33,16,128]{3,2,1,0:T(8,128)(2,1)S(1)} %pad_maximum_fusion.after_ref.refs_0_), channel_id=1, source_target_pairs={{6,0},{0,2},{2,4},{4,6},{7,1},{1,3},{3,5},{5,7},{14,8},{8,10},{10,... | collective-permute-start | bytes 811016 | tf_op jit(solution)/shard_map/ppermute | solution.py:403
  23.1 15.3 %collective-permute-start.2 = (bf16[2,33,16,128]{3,2,1,0:T(8,128)(2,1)S(1)}, bf16[2,33,16,128]{3,2,1,0:T(8,128)(2,1)S(1)}, u32[]{:S(2)}, u32[]{:S(2)}) collective-permute-start(bf16[2,33,16,128]{3,2,1,0:T(8,128)(2,1)S(1)} %pad_maximum_fusion.after_ref.refs_0_), channel_id=1, source_target_pairs={{4,0},{6,2},{0,4},{2,6},{5,1},{7,3},{1,5},{3,7},{12,8},{14,10},{8,... | collective-permute-start | bytes 811016 | tf_op jit(solution)/shard_map/ppermute | solution.py:403
  26.4 19.0 %collective-permute-start.1 = (bf16[2,33,16,128]{3,2,1,0:T(8,128)(2,1)S(1)}, bf16[2,33,16,128]{3,2,1,0:T(8,128)(2,1)S(1)}, u32[]{:S(2)}, u32[]{:S(2)}) collective-permute-start(bf16[2,33,16,128]{3,2,1,0:T(8,128)(2,1)S(1)} %pad_maximum_fusion.after_ref.refs_0_), channel_id=1, source_target_pairs={{2,0},{4,2},{6,4},{0,6},{3,1},{5,3},{7,5},{1,7},{10,8},{12,10},{14... | collective-permute-start | bytes 811016 | tf_op jit(solution)/shard_map/ppermute | solution.py:403
  27.9 17.4 %collective-permute-start.7 = (bf16[2,33,16,128]{3,2,1,0:T(8,128)(2,1)S(1)}, bf16[2,33,16,128]{3,2,1,0:T(8,128)(2,1)S(1)}, u32[]{:S(2)}, u32[]{:S(2)}) collective-permute-start(bf16[2,33,16,128]{3,2,1,0:T(8,128)(2,1)S(1)} %collective-permute-done.4.after0_ref.refs_4_), channel_id=1, source_target_pairs={{6,0},{0,2},{2,4},{4,6},{7,1},{1,3},{3,5},{5,7},{14,8},{8,10},{10,... | collective-permute-start | bytes 811016 | tf_op jit(solution)/shard_map/ppermute | solution.py:403
  31.7 13.7 %collective-permute-start.5 = (bf16[2,33,16,128]{3,2,1,0:T(8,128)(2,1)S(1)}, bf16[2,33,16,128]{3,2,1,0:T(8,128)(2,1)S(1)}, u32[]{:S(2)}, u32[]{:S(2)}) collective-permute-start(bf16[2,33,16,128]{3,2,1,0:T(8,128)(2,1)S(1)} %collective-permute-done.4.after0_ref.refs_4_), channel_id=1, source_target_pairs={{2,0},{4,2},{6,4},{0,6},{3,1},{5,3},{7,5},{1,7},{10,8},{12,10},{14... | collective-permute-start | bytes 811016 | tf_op jit(solution)/shard_map/ppermute | solution.py:403
  38.4 7.4 %collective-permute-start.6 = (bf16[2,33,16,128]{3,2,1,0:T(8,128)(2,1)S(1)}, bf16[2,33,16,128]{3,2,1,0:T(8,128)(2,1)S(1)}, u32[]{:S(2)}, u32[]{:S(2)}) collective-permute-start(bf16[2,33,16,128]{3,2,1,0:T(8,128)(2,1)S(1)} %collective-permute-done.2.after1_ref.refs_2_), channel_id=1, source_target_pairs={{0,8},{8,0},{1,9},{9,1},{2,10},{10,2},{3,11},{11,3},{4,12},{12,4},... | collective-permute-start | bytes 811016 | tf_op jit(solution)/shard_map/ppermute | solution.py:422
  39.2 1.6 %copy-start.12 = (bf16[512,2048]{1,0:T(8,128)(2,1)S(1)}, bf16[512,2048]{1,0:T(8,128)(2,1)}, u32[]{:S(2)}) copy-start(bf16[512,2048]{1,0:T(8,128)(2,1)} %copy-done.11) | copy-start | bytes 6291460
  45.3 12.7 %copy-start.13 = (s32[256]{0:T(256)S(1)}, s32[256]{0:T(256)}, u32[]{:S(2)}) copy-start(s32[256]{0:T(256)} %param.15) | copy-start | bytes 3076
  49.7 1.0 copy-start.1
  50.7 18.0 %all-to-all-start = ((bf16[64,32,128]{2,1,0:T(8,128)(2,1)}), bf16[64,32,128]{2,1,0:T(8,128)(2,1)S(1)}, u32[]{:S(2)}, u32[]{:S(2)}) async-start(bf16[64,32,128]{2,1,0:T(8,128)(2,1)} %bitcast.6), calls=%async_computation | async-start | bytes 1048576 | tf_op jit(solution)/shard_map/all_to_all | solution.py:499
  58.9 3.6 %collective-permute-start.9 = (f32[2,16,128]{2,1,0:T(8,128)S(1)}, f32[2,16,128]{2,1,0:T(8,128)S(1)}, u32[]{:S(2)}, u32[]{:S(2)}) collective-permute-start(f32[2,16,128]{2,1,0:T(8,128)S(1)} %pad_maximum_fusion.2), channel_id=1, source_target_pairs={{0,1},{1,0},{2,3},{3,2},{4,5},{5,4},{6,7},{7,6},{8,9},{9,8},{10,11... | collective-permute-start | bytes 49160 | tf_op jit(solution)/shard_map/ppermute | solution.py:435
  84.0 1.2 %copy-start.2 = (bf16[8,256,256]{2,1,0:T(8,128)(2,1)S(1)}, bf16[8,256,256]{2,1,0:T(8,128)(2,1)}, u32[]{:S(2)}) copy-start(bf16[8,256,256]{2,1,0:T(8,128)(2,1)} %copy-done.1) | copy-start | bytes 3145732
  86.8 10.1 %collective-permute-start.10 = (bf16[4,128,1024]{2,1,0:T(8,128)(2,1)S(1)}, bf16[4,128,1024]{2,1,0:T(8,128)(2,1)S(1)}, u32[]{:S(2)}, u32[]{:S(2)}) collective-permute-start(bf16[4,128,1024]{2,1,0:T(8,128)(2,1)S(1)} %get-tuple-element.23), channel_id=1, source_target_pairs={{0,1},{1,0},{2,3},{3,2},{4,5},{5,4},{6,7},{7,6},{8,9},{9,8},{10,11... | collective-permute-start | bytes 3145736 | tf_op jit(solution)/shard_map/ppermute | solution.py:513
  91.7 5.1 %copy-start.7 = (f32[2,2048]{1,0:T(2,128)S(1)}, f32[2,2048]{1,0:T(2,128)}, u32[]{:S(2)}) copy-start(f32[2,2048]{1,0:T(2,128)} %col_ref.3) | copy-start | bytes 49156

commit v3 on v2

--- a/solution.py
+++ b/solution.py
@@ -18,7 +18,7 @@
 HBM = pl.BlockSpec(memory_space=pltpu.HBM)
 
 
-def run(kernel, out_shape, in_specs, flops, scratch=(), out_specs=None, mib=24):
+def run(kernel, out_shape, in_specs, flops, scratch=(), out_specs=None, mib=46):
     outs = out_shape if isinstance(out_shape, list) else [out_shape]
     if out_specs is None:
         out_specs = [VMEM] * len(outs)
@@ -101,17 +101,14 @@
     members, depth, _ = target.shape
     half = width // WIDE // 2
 
-    def copy(nb, slot):
-        return pltpu.make_async_copy(block_ref.at[slot], table_ref.at[nb], sems.at[slot])
-
-    def step(n, carry):
+    def copy(n):
+        return pltpu.make_async_copy(block_ref.at[n % 2], table_ref.at[n], sems.at[n % 2])
+
+    for n in range(half):
         nb = which * half + n
-        slot = lax.rem(n, 2)
-
-        @pl.when(n >= 2)
-        def _():
-            copy(n - 2, slot).wait()
-
+        slot = n % 2
+        if n >= 2:
+            copy(n - 2).wait()
         for q in range(WIDE // TILE):
             c = lead_ref[0, nb * (WIDE // TILE) + q]
             s = lead_ref[1, nb * (WIDE // TILE) + q]
@@ -120,15 +117,12 @@
             block_ref[slot, :, q * TILE : (q + 1) * TILE] = (
                 c * plus[...] + s * minus[...]
             ).astype(BF16)
-        copy(n, slot).start()
+        copy(n).start()
         product = jnp.dot(scaled[...], block_ref[slot], preferred_element_type=F32)
-        to = pl.ds(pl.multiple_of(n * WIDE, WIDE), WIDE)
+        to = slice(n * WIDE, (n + 1) * WIDE)
         target[:, :, to] = product.astype(BF16).reshape(members, depth, WIDE)
-        return carry
-
-    lax.fori_loop(0, half, step, 0)
-    for slot in range(2):
-        copy(slot, slot).wait()
+    for n in range(half - 2, half):
+        copy(n).wait()
 
 
 def forward_send(
@@ -260,7 +254,7 @@
             for l in range(2):
                 at = (2 * l + q) * rows
                 turned_ref[k, (2 * q + l) * rows : (2 * q + l + 1) * rows, :] = turned[at : at + rows]
-    stores.append(pltpu.make_async_copy(turned_ref, turned_hbm, writes.at[8]))
+    stores.append(pltpu.make_async_copy(turned_ref, turned_hbm.at[:8], writes.at[8]))
     stores[-1].start()
     for store in stores:
         store.wait()
@@ -281,7 +275,7 @@
 def back(place_ref, *refs):
     blocks, (score_ref, turned_hbm, own_ref, par_ref, turned, sem) = refs[:8], refs[8:]
     members, depth, _ = own_ref.shape
-    load = pltpu.make_async_copy(turned_hbm, turned, sem)
+    load = pltpu.make_async_copy(turned_hbm.at[:8], turned, sem)
     load.start()
     for k in range(8):
         weight = jnp.concatenate(
@@ -303,39 +297,31 @@
 def streamed(tables, rows, block_ref, sems):
     steps = tables[0].shape[0]
 
-    def fetch(i, n):
-        at = i * steps + n
-        return pltpu.make_async_copy(tables[i].at[n, rows, :], block_ref.at[at], sems.at[at])
-
-    for i in range(len(tables)):
-        for n in range(steps):
-            fetch(i, n).start()
-
-    def block(i, n):
-        fetch(i, n).wait()
-        return block_ref[i * steps + n]
-
+    def fetch(at):
+        return pltpu.make_async_copy(
+            tables[at // steps].at[at % steps, rows, :], block_ref.at[at], sems.at[at]
+        )
+
+    def block(at):
+        if at + 3 < len(tables) * steps:
+            fetch(at + 3).start()
+        fetch(at).wait()
+        return block_ref[at]
+
+    for at in range(3):
+        fetch(at).start()
     return block
 
 
 def inverse_own(core_ref, own_ref, table0_ref, table1_ref, sum_ref, block_ref, sems):
     members, depth, width = own_ref.shape
-    near = pl.ds(pl.multiple_of(core_ref[0] * width, width), width)
-    half = table0_ref.shape[0]
     core = core_ref[0]
+    near = pl.ds(pl.multiple_of(core * width, width), width)
     block = streamed((table0_ref, table1_ref), near, block_ref, sems)
-    for i in range(2):
-        which = (1 - core) if i == 0 else core
-
-        def step(n, carry, i=i, which=which):
-            sum_ref[which * half + n] = jnp.dot(
-                own_ref[...].reshape(members * depth, width),
-                block(i, n),
-                preferred_element_type=F32,
-            )
-            return carry
-
-        lax.fori_loop(0, half, step, 0)
+    for n in range(sum_ref.shape[0]):
+        sum_ref[n] = jnp.dot(
+            own_ref[...].reshape(members * depth, width), block(n), preferred_element_type=F32
+        )
 
 
 def inverse_par(
@@ -345,42 +331,34 @@
     members, depth, width = par_ref.shape
     levels, rows, _ = row_ref.shape
     core = core_ref[0]
-    half = table0_ref.shape[0]
+    steps = sum_ref.shape[0]
+    half = steps // 2
     far = pl.ds(pl.multiple_of((1 - core) * width, width), width)
-
-    def copy(nb, slot):
+    block = streamed((table0_ref, table1_ref), far, block_ref, reads)
+
+    def copy(n):
+        nb = ((1 - core) if n < half else core) * half + n % half
         cols = pl.ds(pl.multiple_of(nb * WIDE, WIDE), WIDE)
-        return pltpu.make_async_copy(piece.at[slot], out_ref.at[:, :, :, cols], sems.at[slot])
-
-    block = streamed((table0_ref, table1_ref), far, block_ref, reads)
-    for i in range(2):
-        which = (1 - core) if i == 0 else core
-
-        def step(n, carry, i=i, which=which):
-            slot = lax.rem(n, 2)
-            nb = which * half + n
-            cols = pl.ds(pl.multiple_of(nb * WIDE, WIDE), WIDE)
-            product = sum_ref[nb] + jnp.dot(
-                par_ref[...].reshape(members * depth, width),
-                block(i, n),
-                preferred_element_type=F32,
-            )
-            product = product.reshape(members, levels, rows, WIDE)
-
-            @pl.when(n >= (2 if i == 0 else 0))
-            def _():
-                copy(nb, slot).wait()
-
-            for l in range(levels):
-                amplitude = row_ref[l][:, :1] * col_ref[l : l + 1, cols]
-                for m in range(members):
-                    piece[slot, m, l] = product[m, l] * amplitude
-            copy(nb, slot).start()
-            return carry
-
-        lax.fori_loop(0, half, step, 0)
-    for slot in range(2):
-        copy(slot, slot).wait()
+        slot = n % piece.shape[0]
+        return cols, slot, pltpu.make_async_copy(
+            piece.at[slot], out_ref.at[:, :, :, cols], sems.at[slot]
+        )
+
+    for n in range(steps):
+        cols, slot, store = copy(n)
+        product = sum_ref[n] + jnp.dot(
+            par_ref[...].reshape(members * depth, width), block(n), preferred_element_type=F32
+        )
+        product = product.reshape(members, levels, rows, WIDE)
+        if n >= piece.shape[0]:
+            copy(n - piece.shape[0])[2].wait()
+        for l in range(levels):
+            amplitude = row_ref[l][:, :1] * col_ref[l : l + 1, cols]
+            for m in range(members):
+                piece[slot, m, l] = product[m, l] * amplitude
+        store.start()
+    for n in range(steps - piece.shape[0], steps):
+        copy(n)[2].wait()
 
 
 def shards(control, perturbation, loc_row, loc_col, obs_tile, obs_count, obs_value):
@@ -482,7 +460,7 @@
     tiles = slabs * 16
     partial, turned = run(
         cells,
-        [bf16(per_core, 8, 2 * 16, TILE), bf16(per_core, 4 * rows, tiles)],
+        [bf16(per_core, 8, 2 * 16, TILE), bf16(12 * per_core, 4 * rows, tiles)],
         [SMEM] + [VMEM] * 8 + [HBM, HBM, VMEM],
         1 << 30,
         [
@@ -508,7 +486,7 @@
         [SMEM] + [VMEM] * 9 + [HBM],
         1 << 28,
         [pltpu.VMEM((per_core, 4 * rows, tiles), BF16), pltpu.SemaphoreType.DMA],
-        mib=24,
+        mib=46,
     )(place, *arrived, scores.reshape(per_core, 8, 2 * 16, TILE), turned)
     back_other = lax.ppermute(back_send, "core", swap)
     parts = width // WIDE

time: 104 us -> 113 us (1.087)
  Pallas kernels: 31.5 us -> 39.4 us
  local copies, waits for them, and re-layouts: 11.5 us -> 9.27 us
  blocking collectives: 15.1 us -> 16.4 us
    pallas_call x9, Pallas kernels: 31.5 us -> 39.4 us  [launch(): results = call(*args)]
    all_to_all x1, starting transfers between devices: 7.3 us -> 10.5 us  [shards(): lax.all_to_all(partial.reshape(peers, 2 * 16, TILE), SAME_CORE, split_axi...]
    all_to_all x1, waiting for transfers between devices: 6.24 us -> 8.65 us  [shards(): lax.all_to_all(partial.reshape(peers, 2 * 16, TILE), SAME_CORE, split_axi...]
    unnamed x28 -> x24, local copies, waits for them, and re-layouts: 9.94 us -> 7.75 us
    ppermute x5, waiting for transfers between devices: 7.63 us -> 5.54 us  [from_next(): return lax.ppermute(array, 'along', [((i + step) % 4, i) for i in range(4)])]
    ppermute x1, starting transfers between devices: 4.97 us -> 3.37 us  [shards(): back_other = lax.ppermute(back_send, 'core', swap)]
    ppermute x1, starting transfers between devices: 2.74 us -> 1.19 us  [shards(): lent = lax.ppermute(lent, 'core', swap)]
    all_to_all x1, blocking collectives: 15.1 us -> 16.4 us  [shards(): lax.all_to_all(scores, SAME_CORE, split_axis=0, concat_axis=0, tiled=True)]
  transfers between devices with their start and end apart: 12 -> 12, of which waited for: 7 -> 5; matrix products, arithmetic and copies ran while one was open for 1% -> 1% of each run, Pallas kernels for 10% -> 12%
where the time goes in v3:
time: 113 us; the launch traced here: 112 us
  Pallas kernels  39.4 us (35%)
  starting transfers between devices  29.3 us (26%)
  waiting for transfers between devices  17.4 us (15%)
  blocking collectives  16.4 us (15%)
  local copies, waits for them, and re-layouts  9.27 us (8%)
    pallas_call x9, Pallas kernels, launch(): results = call(*args)  39.4 us
    all_to_all x1, blocking collectives, shards(): lax.all_to_all(scores, SAME_CORE, split_axis=0, concat_axis=0, tiled=True)  16.4 us
    all_to_all x1, starting transfers between devices, shards(): lax.all_to_all(partial.reshape(peers, 2 * 16, TILE), SAME_CORE, split_axi...  10.5 us
    ppermute x5, starting transfers between devices, from_next(): return lax.ppermute(array, 'along', [((i + step) % 4, i) for i in range(4)])  9.37 us
    all_to_all x1, waiting for transfers between devices, shards(): lax.all_to_all(partial.reshape(peers, 2 * 16, TILE), SAME_CORE, split_axi...  8.65 us
    unnamed x24, local copies, waits for them, and re-layouts  7.75 us
    ppermute x5, waiting for transfers between devices, from_next(): return lax.ppermute(array, 'along', [((i + step) % 4, i) for i in range(4)])  5.54 us
    ppermute x1, starting transfers between devices, shards(): back_other = lax.ppermute(back_send, 'core', swap)  3.37 us
  transfers between devices with their start and end apart: 12, of which 5 were waited for; matrix products, arithmetic and copies ran while one was open for 1% of the time, Pallas kernels for 12%

profile of v3, /device:TPU:1, one launch (start us, length us, event | category | flops | bytes accessed | tf_op | source)
XLA Modules:
  0.0 112.4 jit_solution(14691666570678191203)
XLA Ops:
  0.0 1.6 %copy-done = bf16[4,2,64,2048]{3,2,1,0:T(8,128)(2,1)S(1)} copy-done((bf16[4,2,64,2048]{3,2,1,0:T(8,128)(2,1)S(1)}, bf16[4,2,64,2048]{3,2,1,0:T(8,128)(2,1)}, u32[]{:S(2)}) %copy-start) | copy-done | bytes 2097176
  1.6 0.7 copy-done.6
  2.3 1.0 shard_map.100
  3.2 1.5 %collective-permute-start = (bf16[33,16,128]{2,1,0:T(8,128)(2,1)S(1)}, bf16[33,16,128]{2,1,0:T(8,128)(2,1)S(1)}, u32[]{:S(2)}, u32[]{:S(2)}) collective-permute-start(bf16[33,16,128]{2,1,0:T(8,128)(2,1)S(1)} %get-tuple-element.17), channel_id=1, source_target_pairs={{0,1},{1,0},{2,3},{3,2},{4,5},{5,4},{6,7},{7,6},{8,9},{9,8},{10,11... | collective-permute-start | bytes 405512 | tf_op jit(solution)/shard_map/ppermute | solution.py:395
  4.7 1.0 collective-permute-done
  5.7 0.8 broadcast_in_dim.2.row_ref
  6.5 0.0 copy-start.1
  6.5 0.9 copy-done.1
  7.5 0.7 copy-done.4
  8.2 0.9 copy-done.7
  9.1 8.7 %shard_map.101 = (bf16[4,128,1024]{2,1,0:T(8,128)(2,1)}, bf16[512,2048]{1,0:T(8,128)(2,1)S(1)}, bf16[4,2048,256]{2,1,0:T(8,128)(2,1)}) custom-call(s32[1]{0:T(128)} %bitcast.core_ref, f32[4,2,64,2048]{3,2,1,0:T(8,128)} %control_ref.1, f32[2,64,128]{2,1,0:T(8,128)S(1)} %broadcast_in_dim.2.row_ref, f32[2,2048]{1,0:T(2,128)S(1)} %copy-done.4, ...), custom_call_target="tpu_custom_call" | custom-call | flops 2147483648 | bytes 14680064 | tf_op jit(solution)/shard_map/pallas_call | solution.py:37
  17.8 0.0 copy-start.9
  17.8 1.3 %copy-done.9 = bf16[512,2048]{1,0:T(8,128)(2,1)} copy-done((bf16[512,2048]{1,0:T(8,128)(2,1)}, bf16[512,2048]{1,0:T(8,128)(2,1)S(1)}, u32[]{:S(2)}) %copy-start.9) | copy-done | bytes 2097176
  19.1 0.4 collective-permute-start.8
  19.5 3.0 %collective-permute-start.4 = (bf16[2,33,16,128]{3,2,1,0:T(8,128)(2,1)S(1)}, bf16[2,33,16,128]{3,2,1,0:T(8,128)(2,1)S(1)}, u32[]{:S(2)}, u32[]{:S(2)}) collective-permute-start(bf16[2,33,16,128]{3,2,1,0:T(8,128)(2,1)S(1)} %pad_maximum_fusion.after_ref.refs_0_), channel_id=1, source_target_pairs={{0,8},{8,0},{1,9},{9,1},{2,10},{10,2},{3,11},{11,3},{4,12},{12,4},... | collective-permute-start | bytes 811016 | tf_op jit(solution)/shard_map/ppermute | solution.py:396
  22.5 3.6 %collective-permute-start.2 = (bf16[2,33,16,128]{3,2,1,0:T(8,128)(2,1)S(1)}, bf16[2,33,16,128]{3,2,1,0:T(8,128)(2,1)S(1)}, u32[]{:S(2)}, u32[]{:S(2)}) collective-permute-start(bf16[2,33,16,128]{3,2,1,0:T(8,128)(2,1)S(1)} %pad_maximum_fusion.after_ref.refs_0_), channel_id=1, source_target_pairs={{4,0},{6,2},{0,4},{2,6},{5,1},{7,3},{1,5},{3,7},{12,8},{14,10},{8,... | collective-permute-start | bytes 811016 | tf_op jit(solution)/shard_map/ppermute | solution.py:381
  26.1 0.4 collective-permute-start.1
  26.5 1.0 collective-permute-start.3
  27.6 1.4 %collective-permute-done.4.after0_ref.refs_4_ = bf16[2,33,16,128]{3,2,1,0:T(8,128)(2,1)S(1)} collective-permute-done((bf16[2,33,16,128]{3,2,1,0:T(8,128)(2,1)S(1)}, bf16[2,33,16,128]{3,2,1,0:T(8,128)(2,1)S(1)}, u32[]{:S(2)}, u32[]{:S(2)}) %collective-permute-start.4) | collective-permute-done | bytes 270368 | tf_op jit(solution)/shard_map/ppermute | solution.py:396
  29.0 3.8 %collective-permute-start.5 = (bf16[2,33,16,128]{3,2,1,0:T(8,128)(2,1)S(1)}, bf16[2,33,16,128]{3,2,1,0:T(8,128)(2,1)S(1)}, u32[]{:S(2)}, u32[]{:S(2)}) collective-permute-start(bf16[2,33,16,128]{3,2,1,0:T(8,128)(2,1)S(1)} %collective-permute-done.4.after0_ref.refs_4_), channel_id=1, source_target_pairs={{2,0},{4,2},{6,4},{0,6},{3,1},{5,3},{7,5},{1,7},{10,8},{12,10},{14... | collective-permute-start | bytes 811016 | tf_op jit(solution)/shard_map/ppermute | solution.py:381
  32.8 0.0 collective-permute-done.2.after1_ref.refs_2_
  32.8 0.6 collective-permute-start.7
  33.3 5.5 %collective-permute-done.1.refs_1_ = bf16[2,33,16,128]{3,2,1,0:T(8,128)(2,1)S(1)} collective-permute-done((bf16[2,33,16,128]{3,2,1,0:T(8,128)(2,1)S(1)}, bf16[2,33,16,128]{3,2,1,0:T(8,128)(2,1)S(1)}, u32[]{:S(2)}, u32[]{:S(2)}) %collective-permute-start.1) | collective-permute-done | bytes 270368 | tf_op jit(solution)/shard_map/ppermute | solution.py:381
  38.8 0.1 collective-permute-start.6
  38.9 0.1 pad_add_fusion.place_ref
  39.0 0.7 shard_map.103.refs_10_
  39.7 0.0 copy-start.10
  39.7 1.6 %copy-done.10 = bf16[512,2048]{1,0:T(8,128)(2,1)S(1)} copy-done((bf16[512,2048]{1,0:T(8,128)(2,1)S(1)}, bf16[512,2048]{1,0:T(8,128)(2,1)}, u32[]{:S(2)}) %copy-start.10) | copy-done | bytes 2097176
  41.3 5.6 %shard_map.102 = (bf16[4,128,1024]{2,1,0:T(8,128)(2,1)S(1)}, bf16[4,2048,256]{2,1,0:T(8,128)(2,1)}) custom-call(s32[1]{0:T(128)} %bitcast.core_ref, bf16[512,2048]{1,0:T(8,128)(2,1)S(1)} %copy-done.10, f32[192,128]{1,0:T(8,128)S(1)} %copy-done.8, f32[2,16,16,128]{3,2,1,0:T(8,128)S(1)} %copy-done.2, ...), custom_call_target="tpu_custom_call" | custom-call | flops 2147483648 | bytes 10485760 | tf_op jit(solution)/shard_map/pallas_call | solution.py:37
  46.9 0.0 copy-start.11
  46.9 0.0 collective-permute-done.3.refs_3_
  46.9 0.0 collective-permute-done.5.refs_5_
  47.0 0.0 collective-permute-done.7.refs_7_
  47.0 0.0 collective-permute-done.6.refs_6_
  47.0 4.4 %shard_map.104 = (bf16[8,8,32,128]{3,2,1,0:T(8,128)(2,1)}, bf16[96,256,256]{2,1,0:T(8,128)(2,1)}) custom-call(s32[3]{0:T(128)S(1)} %pad_add_fusion.place_ref, bf16[2,33,16,128]{3,2,1,0:T(8,128)(2,1)S(1)} %pad_maximum_fusion.after_ref.refs_0_, bf16[2,33,16,128]{3,2,1,0:T(8,128)(2,1)S(1)} %collective-permute-done.1.refs_1_, ...), custom_call_target="tpu_custom_call" | custom-call | flops 1073741824 | bytes 26214400 | tf_op jit(solution)/shard_map/pallas_call | solution.py:37
  51.3 10.5 %all-to-all-start = ((bf16[64,32,128]{2,1,0:T(8,128)(2,1)}), bf16[64,32,128]{2,1,0:T(8,128)(2,1)S(1)}, u32[]{:S(2)}, u32[]{:S(2)}) async-start(bf16[64,32,128]{2,1,0:T(8,128)(2,1)} %bitcast.6), calls=%async_computation | async-start | bytes 1048576 | tf_op jit(solution)/shard_map/all_to_all | solution.py:477
  61.9 0.1 fusion
  62.0 0.7 dynamic-slice_bitcast_fusion
  62.7 1.2 %collective-permute-start.9 = (f32[2,16,128]{2,1,0:T(8,128)S(1)}, f32[2,16,128]{2,1,0:T(8,128)S(1)}, u32[]{:S(2)}, u32[]{:S(2)}) collective-permute-start(f32[2,16,128]{2,1,0:T(8,128)S(1)} %pad_maximum_fusion.2), channel_id=1, source_target_pairs={{0,1},{1,0},{2,3},{3,2},{4,5},{5,4},{6,7},{7,6},{8,9},{9,8},{10,11... | collective-permute-start | bytes 49160 | tf_op jit(solution)/shard_map/ppermute | solution.py:413
  63.9 0.8 collective-permute-done.9.lent_ref
  64.7 8.6 %all-to-all-done.cells_ref = bf16[64,32,128]{2,1,0:T(8,128)(2,1)S(1)} async-done(((bf16[64,32,128]{2,1,0:T(8,128)(2,1)}), bf16[64,32,128]{2,1,0:T(8,128)(2,1)S(1)}, u32[]{:S(2)}, u32[]{:S(2)}) %all-to-all-start) | async-done | bytes 524320 | tf_op jit(solution)/shard_map/all_to_all | solution.py:477
  73.4 0.1 shard_map.105
  73.5 16.4 %all_to_all.10 = bf16[64,32,128]{2,1,0:T(8,128)(2,1)S(1)} all-to-all(bf16[64,32,128]{2,1,0:T(8,128)(2,1)S(1)} %shard_map.105), channel_id=1, replica_groups=mesh['member'=8,'across'=2,'along'=4,'core'=2] {'member','across','along'}, dimensions={0} | all-to-all | bytes 1048576 | tf_op jit(solution)/shard_map/all_to_all | solution.py:481
  89.9 2.7 %shard_map.106 = (bf16[4,128,1024]{2,1,0:T(8,128)(2,1)S(1)}, bf16[4,128,1024]{2,1,0:T(8,128)(2,1)S(1)}) custom-call(s32[3]{0:T(128)S(1)} %pad_add_fusion.place_ref, bf16[2,33,16,128]{3,2,1,0:T(8,128)(2,1)S(1)} %pad_maximum_fusion.after_ref.refs_0_, bf16[2,33,16,128]{3,2,1,0:T(8,128)(2,1)S(1)} %collective-permute-done.1.refs_1_, ...), custom_call_target="tpu_custom_call" | custom-call | flops 268435456 | bytes 4194304 | tf_op jit(solution)/shard_map/pallas_call | solution.py:37
  92.6 3.4 %collective-permute-start.10 = (bf16[4,128,1024]{2,1,0:T(8,128)(2,1)S(1)}, bf16[4,128,1024]{2,1,0:T(8,128)(2,1)S(1)}, u32[]{:S(2)}, u32[]{:S(2)}) collective-permute-start(bf16[4,128,1024]{2,1,0:T(8,128)(2,1)S(1)} %get-tuple-element.23), channel_id=1, source_target_pairs={{0,1},{1,0},{2,3},{3,2},{4,5},{5,4},{6,7},{7,6},{8,9},{9,8},{10,11... | collective-permute-start | bytes 3145736 | tf_op jit(solution)/shard_map/ppermute | solution.py:491
  96.0 7.2 %shard_map.107.sum_ref = f32[8,512,256]{2,1,0:T(8,128)S(1)} custom-call(s32[1]{0:T(128)} %bitcast.core_ref, bf16[4,128,1024]{2,1,0:T(8,128)(2,1)S(1)} %get-tuple-element.24.own_ref, bf16[4,2048,256]{2,1,0:T(8,128)(2,1)} %get-tuple-element.25.table0_ref, bf16[4,2048,256]{2,1,0:T(8,128)(2,1)} %get-tuple-element.26.table1_ref), custom_call_target="tpu_custom_call" | custom-call | flops 2147483648 | bytes 8388608 | tf_op jit(solution)/shard_map/pallas_call | solution.py:37
  103.2 0.0 collective-permute-done.10.par_ref
  103.2 9.0 %shard_map.108 = f32[4,2,64,2048]{3,2,1,0:T(8,128)} custom-call(s32[1]{0:T(128)} %bitcast.core_ref, bf16[4,128,1024]{2,1,0:T(8,128)(2,1)S(1)} %collective-permute-done.10.par_ref, f32[8,512,256]{2,1,0:T(8,128)S(1)} %shard_map.107.sum_ref, bf16[4,2048,256]{2,1,0:T(8,128)(2,1)} %get-tuple-element.25.table0_ref, ...), custom_call_target="tpu_custom_call" | custom-call | flops 2147483648 | bytes 8388608 | tf_op jit(solution)/shard_map/pallas_call | solution.py:37
  (17 shorter events, 0.1 us)
Async XLA Ops:
  0.0 1.6 %copy-start = (bf16[4,2,64,2048]{3,2,1,0:T(8,128)(2,1)S(1)}, bf16[4,2,64,2048]{3,2,1,0:T(8,128)(2,1)}, u32[]{:S(2)}) copy-start(bf16[4,2,64,2048]{3,2,1,0:T(8,128)(2,1)} %pert_ref.1) | copy-start | bytes 6291460
  1.6 0.7 copy-start.6
  3.2 2.5 %collective-permute-start = (bf16[33,16,128]{2,1,0:T(8,128)(2,1)S(1)}, bf16[33,16,128]{2,1,0:T(8,128)(2,1)S(1)}, u32[]{:S(2)}, u32[]{:S(2)}) collective-permute-start(bf16[33,16,128]{2,1,0:T(8,128)(2,1)S(1)} %get-tuple-element.17), channel_id=1, source_target_pairs={{0,1},{1,0},{2,3},{3,2},{4,5},{5,4},{6,7},{7,6},{8,9},{9,8},{10,11... | collective-permute-start | bytes 405512 | tf_op jit(solution)/shard_map/ppermute | solution.py:395
  5.7 33.3 %copy-start.2 = (f32[2,16,16,128]{3,2,1,0:T(8,128)S(1)}, f32[2,16,16,128]{3,2,1,0:T(8,128)}, u32[]{:S(2)}) copy-start(f32[2,16,16,128]{3,2,1,0:T(8,128)} %constant.32.clone.lead_ref) | copy-start | bytes 786436
  5.7 33.3 %copy-start.3 = (f32[160,128]{1,0:T(8,128)S(1)}, f32[160,128]{1,0:T(8,128)}, u32[]{:S(2)}) copy-start(f32[160,128]{1,0:T(8,128)} %constant.34.clone.factor_ref) | copy-start | bytes 245764
  6.5 1.0 copy-start.1
  7.5 0.7 copy-start.4
  8.2 0.9 copy-start.7
  9.1 30.6 %copy-start.8 = (f32[192,128]{1,0:T(8,128)S(1)}, f32[192,128]{1,0:T(8,128)}, u32[]{:S(2)}) copy-start(f32[192,128]{1,0:T(8,128)} %constant.33.clone.factor_ref) | copy-start | bytes 294916
  17.8 1.3 %copy-start.9 = (bf16[512,2048]{1,0:T(8,128)(2,1)}, bf16[512,2048]{1,0:T(8,128)(2,1)S(1)}, u32[]{:S(2)}) copy-start(bf16[512,2048]{1,0:T(8,128)(2,1)S(1)} %get-tuple-element.18.scaled_ref) | copy-start | bytes 6291460
  19.1 27.9 %collective-permute-start.8 = (bf16[4,128,1024]{2,1,0:T(8,128)(2,1)}, bf16[4,128,1024]{2,1,0:T(8,128)(2,1)}, u32[]{:S(2)}, u32[]{:S(2)}) collective-permute-start(bf16[4,128,1024]{2,1,0:T(8,128)(2,1)} %get-tuple-element.20), channel_id=1, source_target_pairs={{0,1},{1,0},{2,3},{3,2},{4,5},{5,4},{6,7},{7,6},{8,9},{9,8},{10,11... | collective-permute-start | bytes 3145736 | tf_op jit(solution)/shard_map/ppermute | solution.py:446
  19.5 9.5 %collective-permute-start.4 = (bf16[2,33,16,128]{3,2,1,0:T(8,128)(2,1)S(1)}, bf16[2,33,16,128]{3,2,1,0:T(8,128)(2,1)S(1)}, u32[]{:S(2)}, u32[]{:S(2)}) collective-permute-start(bf16[2,33,16,128]{3,2,1,0:T(8,128)(2,1)S(1)} %pad_maximum_fusion.after_ref.refs_0_), channel_id=1, source_target_pairs={{0,8},{8,0},{1,9},{9,1},{2,10},{10,2},{3,11},{11,3},{4,12},{12,4},... | collective-permute-start | bytes 811016 | tf_op jit(solution)/shard_map/ppermute | solution.py:396
  22.5 10.2 %collective-permute-start.2 = (bf16[2,33,16,128]{3,2,1,0:T(8,128)(2,1)S(1)}, bf16[2,33,16,128]{3,2,1,0:T(8,128)(2,1)S(1)}, u32[]{:S(2)}, u32[]{:S(2)}) collective-permute-start(bf16[2,33,16,128]{3,2,1,0:T(8,128)(2,1)S(1)} %pad_maximum_fusion.after_ref.refs_0_), channel_id=1, source_target_pairs={{4,0},{6,2},{0,4},{2,6},{5,1},{7,3},{1,5},{3,7},{12,8},{14,10},{8,... | collective-permute-start | bytes 811016 | tf_op jit(solution)/shard_map/ppermute | solution.py:381
  26.1 12.7 %collective-permute-start.1 = (bf16[2,33,16,128]{3,2,1,0:T(8,128)(2,1)S(1)}, bf16[2,33,16,128]{3,2,1,0:T(8,128)(2,1)S(1)}, u32[]{:S(2)}, u32[]{:S(2)}) collective-permute-start(bf16[2,33,16,128]{3,2,1,0:T(8,128)(2,1)S(1)} %pad_maximum_fusion.after_ref.refs_0_), channel_id=1, source_target_pairs={{2,0},{4,2},{6,4},{0,6},{3,1},{5,3},{7,5},{1,7},{10,8},{12,10},{14... | collective-permute-start | bytes 811016 | tf_op jit(solution)/shard_map/ppermute | solution.py:381
  26.5 20.4 %collective-permute-start.3 = (bf16[2,33,16,128]{3,2,1,0:T(8,128)(2,1)S(1)}, bf16[2,33,16,128]{3,2,1,0:T(8,128)(2,1)S(1)}, u32[]{:S(2)}, u32[]{:S(2)}) collective-permute-start(bf16[2,33,16,128]{3,2,1,0:T(8,128)(2,1)S(1)} %pad_maximum_fusion.after_ref.refs_0_), channel_id=1, source_target_pairs={{6,0},{0,2},{2,4},{4,6},{7,1},{1,3},{3,5},{5,7},{14,8},{8,10},{10,... | collective-permute-start | bytes 811016 | tf_op jit(solution)/shard_map/ppermute | solution.py:381
  29.0 18.0 %collective-permute-start.5 = (bf16[2,33,16,128]{3,2,1,0:T(8,128)(2,1)S(1)}, bf16[2,33,16,128]{3,2,1,0:T(8,128)(2,1)S(1)}, u32[]{:S(2)}, u32[]{:S(2)}) collective-permute-start(bf16[2,33,16,128]{3,2,1,0:T(8,128)(2,1)S(1)} %collective-permute-done.4.after0_ref.refs_4_), channel_id=1, source_target_pairs={{2,0},{4,2},{6,4},{0,6},{3,1},{5,3},{7,5},{1,7},{10,8},{12,10},{14... | collective-permute-start | bytes 811016 | tf_op jit(solution)/shard_map/ppermute | solution.py:381
  32.8 14.2 %collective-permute-start.7 = (bf16[2,33,16,128]{3,2,1,0:T(8,128)(2,1)S(1)}, bf16[2,33,16,128]{3,2,1,0:T(8,128)(2,1)S(1)}, u32[]{:S(2)}, u32[]{:S(2)}) collective-permute-start(bf16[2,33,16,128]{3,2,1,0:T(8,128)(2,1)S(1)} %collective-permute-done.4.after0_ref.refs_4_), channel_id=1, source_target_pairs={{6,0},{0,2},{2,4},{4,6},{7,1},{1,3},{3,5},{5,7},{14,8},{8,10},{10,... | collective-permute-start | bytes 811016 | tf_op jit(solution)/shard_map/ppermute | solution.py:381
  38.8 8.1 %collective-permute-start.6 = (bf16[2,33,16,128]{3,2,1,0:T(8,128)(2,1)S(1)}, bf16[2,33,16,128]{3,2,1,0:T(8,128)(2,1)S(1)}, u32[]{:S(2)}, u32[]{:S(2)}) collective-permute-start(bf16[2,33,16,128]{3,2,1,0:T(8,128)(2,1)S(1)} %collective-permute-done.2.after1_ref.refs_2_), channel_id=1, source_target_pairs={{0,8},{8,0},{1,9},{9,1},{2,10},{10,2},{3,11},{11,3},{4,12},{12,4},... | collective-permute-start | bytes 811016 | tf_op jit(solution)/shard_map/ppermute | solution.py:400
  39.7 1.6 %copy-start.10 = (bf16[512,2048]{1,0:T(8,128)(2,1)S(1)}, bf16[512,2048]{1,0:T(8,128)(2,1)}, u32[]{:S(2)}) copy-start(bf16[512,2048]{1,0:T(8,128)(2,1)} %copy-done.9) | copy-start | bytes 6291460
  46.9 14.9 %copy-start.11 = (s32[256]{0:T(256)S(1)}, s32[256]{0:T(256)}, u32[]{:S(2)}) copy-start(s32[256]{0:T(256)} %param.15) | copy-start | bytes 3076
  51.3 22.0 %all-to-all-start = ((bf16[64,32,128]{2,1,0:T(8,128)(2,1)}), bf16[64,32,128]{2,1,0:T(8,128)(2,1)S(1)}, u32[]{:S(2)}, u32[]{:S(2)}) async-start(bf16[64,32,128]{2,1,0:T(8,128)(2,1)} %bitcast.6), calls=%async_computation | async-start | bytes 1048576 | tf_op jit(solution)/shard_map/all_to_all | solution.py:477
  62.7 2.0 %collective-permute-start.9 = (f32[2,16,128]{2,1,0:T(8,128)S(1)}, f32[2,16,128]{2,1,0:T(8,128)S(1)}, u32[]{:S(2)}, u32[]{:S(2)}) collective-permute-start(f32[2,16,128]{2,1,0:T(8,128)S(1)} %pad_maximum_fusion.2), channel_id=1, source_target_pairs={{0,1},{1,0},{2,3},{3,2},{4,5},{5,4},{6,7},{7,6},{8,9},{9,8},{10,11... | collective-permute-start | bytes 49160 | tf_op jit(solution)/shard_map/ppermute | solution.py:413
  92.6 10.6 %collective-permute-start.10 = (bf16[4,128,1024]{2,1,0:T(8,128)(2,1)S(1)}, bf16[4,128,1024]{2,1,0:T(8,128)(2,1)S(1)}, u32[]{:S(2)}, u32[]{:S(2)}) collective-permute-start(bf16[4,128,1024]{2,1,0:T(8,128)(2,1)S(1)} %get-tuple-element.23), channel_id=1, source_target_pairs={{0,1},{1,0},{2,3},{3,2},{4,5},{5,4},{6,7},{7,6},{8,9},{9,8},{10,11... | collective-permute-start | bytes 3145736 | tf_op jit(solution)/shard_map/ppermute | solution.py:491
  96.0 7.3 %copy-start.5 = (f32[2,2048]{1,0:T(2,128)S(1)}, f32[2,2048]{1,0:T(2,128)}, u32[]{:S(2)}) copy-start(f32[2,2048]{1,0:T(2,128)} %col_ref.3) | copy-start | bytes 49156

commit v4 on v2

--- a/solution.py
+++ b/solution.py
@@ -9,6 +9,7 @@
 
 TILE = 128
 WIDE = 256
+LEAD = 192
 BF16 = jnp.bfloat16
 F32 = jnp.float32
 SLAB = ("across", "along", "core")
@@ -18,7 +19,7 @@
 HBM = pl.BlockSpec(memory_space=pltpu.HBM)
 
 
-def run(kernel, out_shape, in_specs, flops, scratch=(), out_specs=None, mib=24):
+def run(kernel, out_shape, in_specs, flops, scratch=(), out_specs=None, mib=46):
     outs = out_shape if isinstance(out_shape, list) else [out_shape]
     if out_specs is None:
         out_specs = [VMEM] * len(outs)
@@ -84,6 +85,11 @@
         ref[8 * members] = jnp.broadcast_to(mine.astype(F32), (16, TILE)).astype(BF16)
 
 
+def lead_of(factor_ref, part, index):
+    at = pl.multiple_of(LEAD + part * 256 + index * 16, 16)
+    return factor_ref[pl.ds(at, 16), :]
+
+
 def table_factors(factor_ref, width, plus, minus):
     inner = 64
     outer = width // inner
@@ -96,7 +102,7 @@
         minus[at, :] = c * near_m - s * near_p
 
 
-def transform(which, scaled, lead_ref, plus, minus, block_ref, table_ref, sems, target):
+def transform(which, scaled, factor_ref, plus, minus, block_ref, table_ref, sems, target):
     width = plus.shape[0]
     members, depth, _ = target.shape
     half = width // WIDE // 2
@@ -113,8 +119,8 @@
             copy(n - 2, slot).wait()
 
         for q in range(WIDE // TILE):
-            c = lead_ref[0, nb * (WIDE // TILE) + q]
-            s = lead_ref[1, nb * (WIDE // TILE) + q]
+            c = lead_of(factor_ref, 0, nb * (WIDE // TILE) + q)
+            s = lead_of(factor_ref, 1, nb * (WIDE // TILE) + q)
             c = jnp.broadcast_to(c[None], (width // 16, 16, TILE)).reshape(width, TILE)
             s = jnp.broadcast_to(s[None], (width // 16, 16, TILE)).reshape(width, TILE)
             block_ref[slot, :, q * TILE : (q + 1) * TILE] = (
@@ -132,9 +138,9 @@
 
 
 def forward_send(
-    core_ref, control_ref, row_ref, col_ref, factor_ref, lead_ref, after_ref,
-    send_ref, scaled_ref, table_ref,
-    control, plus, minus, block_ref, sems, reads,
+    core_ref, control_ref, row_ref, col_ref, factor_ref, after_ref,
+    send_ref, scaled_hbm, table_ref,
+    control, scaled_ref, plus, minus, block_ref, sems, reads, kept,
 ):
     members, levels, rows, width = control.shape
     copies = [
@@ -149,33 +155,41 @@
             amplitude = row_ref[l][:, :1] * col_ref[l : l + 1, :]
             at = (m * levels + l) * rows
             scaled_ref[at : at + rows, :] = (control[m, l] * amplitude).astype(BF16)
+    keep = pltpu.make_async_copy(scaled_ref, scaled_hbm.at[: scaled_ref.shape[0]], kept)
+    keep.start()
     transform(
-        1 - core_ref[0], scaled_ref, lead_ref, plus, minus, block_ref, table_ref, sems, send_ref
+        1 - core_ref[0], scaled_ref, factor_ref, plus, minus, block_ref, table_ref, sems, send_ref
     )
+    keep.wait()
 
 
 def forward_own(
-    core_ref, scaled_ref, factor_ref, lead_ref, after0_ref, after1_ref,
-    own_ref, table_ref, plus, minus, block_ref, sems,
+    core_ref, scaled_hbm, factor_ref, after0_ref, after1_ref,
+    own_ref, table_ref, scaled_ref, plus, minus, block_ref, sems, kept,
 ):
+    load = pltpu.make_async_copy(scaled_hbm.at[: scaled_ref.shape[0]], scaled_ref, kept)
+    load.start()
     table_factors(factor_ref, plus.shape[0], plus, minus)
-    transform(core_ref[0], scaled_ref, lead_ref, plus, minus, block_ref, table_ref, sems, own_ref)
+    load.wait()
+    transform(core_ref[0], scaled_ref, factor_ref, plus, minus, block_ref, table_ref, sems, own_ref)
 
 
 def chip_of(place_ref, h):
-    across, along = place_ref[0], place_ref[1]
+    across, along = place_ref[0] // 8, place_ref[0] // 2 % 4
     return ((across + h // 4) % 2) * 4 + (along + h % 4) % 4
 
 
-def spread_rows(place_ref, factor_ref, lead_ref, out_ref):
-    core = place_ref[2]
+def spread_rows(place_ref, factor_ref, out_ref):
+    core = place_ref[0] % 2
     rows = out_ref.shape[1] // 4
-    inner_p, inner_m = factor_ref[:rows, :], factor_ref[rows : 2 * rows, :]
+    first = factor_ref.shape[0] - 2 * rows - 32
+    inner_p = factor_ref[first : first + rows, :]
+    inner_m = factor_ref[first + rows : first + 2 * rows, :]
     plus, minus = [], []
     for q in range(2):
         slab = chip_of(place_ref, 0) * 2 + (core + q) % 2
-        c = jnp.broadcast_to(lead_ref[0, slab][None], (rows // 16, 16, TILE)).reshape(rows, TILE)
-        s = jnp.broadcast_to(lead_ref[1, slab][None], (rows // 16, 16, TILE)).reshape(rows, TILE)
+        c = jnp.broadcast_to(lead_of(factor_ref, 0, slab)[None], (rows // 16, 16, TILE)).reshape(rows, TILE)
+        s = jnp.broadcast_to(lead_of(factor_ref, 1, slab)[None], (rows // 16, 16, TILE)).reshape(rows, TILE)
         plus.append(c * inner_p + s * inner_m)
         minus.append(c * inner_m - s * inner_p)
     left = lax.broadcasted_iota(jnp.int32, (rows, TILE), 1) < rows
@@ -185,8 +199,8 @@
     for h in range(out_ref.shape[0]):
         for r in range(2):
             slab = chip_of(place_ref, h) * 2 + (core + r) % 2
-            c = factor_ref[pl.ds(2 * rows + slab, 1), :]
-            s = factor_ref[pl.ds(2 * rows + 16 + slab, 1), :]
+            c = factor_ref[pl.ds(first + 2 * rows + slab, 1), :]
+            s = factor_ref[pl.ds(first + 2 * rows + 16 + slab, 1), :]
             entry = (c * plus + s * minus).astype(BF16)
             for l in range(2):
                 at = slice((2 * l + r) * rows, (2 * l + r + 1) * rows)
@@ -260,7 +274,7 @@
             for l in range(2):
                 at = (2 * l + q) * rows
                 turned_ref[k, (2 * q + l) * rows : (2 * q + l + 1) * rows, :] = turned[at : at + rows]
-    stores.append(pltpu.make_async_copy(turned_ref, turned_hbm, writes.at[8]))
+    stores.append(pltpu.make_async_copy(turned_ref, turned_hbm.at[:8], writes.at[8]))
     stores[-1].start()
     for store in stores:
         store.wait()
@@ -281,7 +295,7 @@
 def back(place_ref, *refs):
     blocks, (score_ref, turned_hbm, own_ref, par_ref, turned, sem) = refs[:8], refs[8:]
     members, depth, _ = own_ref.shape
-    load = pltpu.make_async_copy(turned_hbm, turned, sem)
+    load = pltpu.make_async_copy(turned_hbm.at[:8], turned, sem)
     load.start()
     for k in range(8):
         weight = jnp.concatenate(
@@ -307,11 +321,20 @@
         at = i * steps + n
         return pltpu.make_async_copy(tables[i].at[n, rows, :], block_ref.at[at], sems.at[at])
 
-    for i in range(len(tables)):
-        for n in range(steps):
-            fetch(i, n).start()
+    for n in range(3):
+        fetch(0, n).start()
 
     def block(i, n):
+        @pl.when(n + 3 < steps)
+        def _():
+            fetch(i, n + 3).start()
+
+        if i + 1 < len(tables):
+
+            @pl.when(n + 3 >= steps)
+            def _():
+                fetch(i + 1, n + 3 - steps).start()
+
         fetch(i, n).wait()
         return block_ref[i * steps + n]
 
@@ -396,7 +419,7 @@
     core = lax.axis_index("core").astype(jnp.int32)
     group = lax.axis_index("member").astype(jnp.int32)
     core_index = core.reshape(1)
-    place = jnp.stack([across, along, core])
+    place = (across * 8 + along * 2 + core).reshape(1)
     swap = [(0, 1), (1, 0)]
 
     def from_next(array, step):
@@ -435,21 +458,23 @@
     lent = lax.ppermute(lent, "core", swap)
 
     lead = cas(np.arange(16), np.arange(16), 16)
-    lead = jnp.asarray(np.repeat(np.stack(lead[2:])[:, :, :, None], TILE, axis=3))
+    lead = np.repeat(np.stack(lead[2:]).reshape(-1, 1), TILE, axis=1)
     inner = 64
     outer = cas(np.arange(width // inner), np.arange(TILE), width // inner)
     near = cas(np.arange(inner), np.arange(TILE), width)
     root = np.float32(np.sqrt(width))
-    factors = jnp.asarray(np.concatenate([outer[2], outer[3], near[0] / root, near[1] / root]))
+    factors = [outer[2], outer[3], near[0] / root, near[1] / root, lead]
     wave = np.arange(TILE) % rows
     base = cas(np.arange(rows), wave, height)
     turn = cas(np.arange(16), wave, 16)
     root = np.float32(np.sqrt(height))
-    row_factors = jnp.asarray(np.concatenate([base[0] / root, base[1] / root, turn[2], turn[3]]))
+    factors += [base[0] / root, base[1] / root, turn[2], turn[3]]
+    factors = jnp.asarray(np.concatenate(factors))
 
     row_b = jnp.broadcast_to(loc_row[:, :, None], (levels, rows, TILE))
     table_half = bf16(width // WIDE // 2, width, WIDE)
     work = [
+        pltpu.VMEM((members * depth, width), BF16),
         pltpu.VMEM((width, TILE), F32),
         pltpu.VMEM((width, TILE), F32),
         pltpu.VMEM((2, width, WIDE), BF16),
@@ -458,31 +483,33 @@
     flops = members * depth * width * width
     send, scaled, table0 = run(
         forward_send,
-        [bf16(members, depth, half), bf16(members * depth, width), table_half],
-        [SMEM, HBM, VMEM, VMEM, VMEM, VMEM, HBM],
+        [bf16(members, depth, half), bf16(6 * members * depth, width), table_half],
+        [SMEM, HBM, VMEM, VMEM, VMEM, HBM],
         flops,
-        [pltpu.VMEM(control.shape, F32)] + work + [pltpu.SemaphoreType.DMA((members,))],
-        [VMEM, VMEM, HBM],
-        mib=48,
-    )(core_index, control, row_b, loc_col, factors, lead, here)
+        [pltpu.VMEM(control.shape, F32)]
+        + work
+        + [pltpu.SemaphoreType.DMA((members,)), pltpu.SemaphoreType.DMA],
+        [VMEM, HBM, HBM],
+        mib=50,
+    )(core_index, control, row_b, loc_col, factors, here)
     par = lax.ppermute(send, "core", swap)
     own, table1 = run(
         forward_own,
         [bf16(members, depth, half), table_half],
-        [SMEM, VMEM, VMEM, VMEM, HBM, HBM],
+        [SMEM, HBM, VMEM, HBM, HBM],
         flops,
-        work,
+        work + [pltpu.SemaphoreType.DMA],
         [VMEM, HBM],
-        mib=48,
-    )(core_index, scaled, factors, lead, facing, here2)
+        mib=50,
+    )(core_index, scaled, factors, facing, here2)
     table_rows = run(
-        spread_rows, bf16(8, 4 * rows, 2 * TILE), [SMEM, VMEM, VMEM], 1 << 22
-    )(place, row_factors, lead)
+        spread_rows, bf16(8, 4 * rows, 2 * TILE), [SMEM, VMEM], 1 << 22
+    )(place, factors)
 
     tiles = slabs * 16
     partial, turned = run(
         cells,
-        [bf16(per_core, 8, 2 * 16, TILE), bf16(per_core, 4 * rows, tiles)],
+        [bf16(per_core, 8, 2 * 16, TILE), bf16(12 * per_core, 4 * rows, tiles)],
         [SMEM] + [VMEM] * 8 + [HBM, HBM, VMEM],
         1 << 30,
         [
@@ -508,7 +535,7 @@
         [SMEM] + [VMEM] * 9 + [HBM],
         1 << 28,
         [pltpu.VMEM((per_core, 4 * rows, tiles), BF16), pltpu.SemaphoreType.DMA],
-        mib=24,
+        mib=46,
     )(place, *arrived, scores.reshape(per_core, 8, 2 * 16, TILE), turned)
     back_other = lax.ppermute(back_send, "core", swap)
     parts = width // WIDE

time: 104 us -> 103 us (level)
  local copies, waits for them, and re-layouts: 11.5 us -> 5.54 us
  blocking collectives: 15.1 us -> 17 us
    unnamed x28 -> x14, local copies, waits for them, and re-layouts: 9.94 us -> 4.02 us
    all_to_all x1, starting transfers between devices: 7.3 us -> 9.88 us  [shards(): lax.all_to_all(partial.reshape(peers, 2 * 16, TILE), SAME_CORE, split_axi...]
    ppermute x5, waiting for transfers between devices: 7.63 us -> 5.53 us  [from_next(): return lax.ppermute(array, 'along', [((i + step) % 4, i) for i in range(4)])]
    all_to_all x1, blocking collectives: 15.1 us -> 17 us  [shards(): lax.all_to_all(scores, SAME_CORE, split_axis=0, concat_axis=0, tiled=True)]
    ppermute x1, starting transfers between devices: 4.97 us -> 3.15 us  [shards(): back_other = lax.ppermute(back_send, 'core', swap)]
    all_to_all x1, waiting for transfers between devices: 6.24 us -> 7.51 us  [shards(): lax.all_to_all(partial.reshape(peers, 2 * 16, TILE), SAME_CORE, split_axi...]
  transfers between devices with their start and end apart: 12 -> 12, of which waited for: 7 -> 6; matrix products, arithmetic and copies ran while one was open for 1% -> 1% of each run, Pallas kernels for 10% -> 11%
where the time goes in v4:
time: 103 us; the launch traced here: 102 us
  Pallas kernels  32.5 us (32%)
  starting transfers between devices  29.2 us (28%)
  waiting for transfers between devices  17.7 us (17%)
  blocking collectives  17 us (17%)
  local copies, waits for them, and re-layouts  5.54 us (5%)
    pallas_call x9, Pallas kernels, launch(): results = call(*args)  32.5 us
    all_to_all x1, blocking collectives, shards(): lax.all_to_all(scores, SAME_CORE, split_axis=0, concat_axis=0, tiled=True)  17 us
    all_to_all x1, starting transfers between devices, shards(): lax.all_to_all(partial.reshape(peers, 2 * 16, TILE), SAME_CORE, split_axi...  9.88 us
    ppermute x5, starting transfers between devices, from_next(): return lax.ppermute(array, 'along', [((i + step) % 4, i) for i in range(4)])  9.38 us
    all_to_all x1, waiting for transfers between devices, shards(): lax.all_to_all(partial.reshape(peers, 2 * 16, TILE), SAME_CORE, split_axi...  7.51 us
    ppermute x5, waiting for transfers between devices, from_next(): return lax.ppermute(array, 'along', [((i + step) % 4, i) for i in range(4)])  5.53 us
    unnamed x14, local copies, waits for them, and re-layouts  4.02 us
    ppermute x1, starting transfers between devices, shards(): back_other = lax.ppermute(back_send, 'core', swap)  3.15 us
  transfers between devices with their start and end apart: 12, of which 6 were waited for; matrix products, arithmetic and copies ran while one was open for 1% of the time, Pallas kernels for 11%

profile of v4, /device:TPU:1, one launch (start us, length us, event | category | flops | bytes accessed | tf_op | source)
XLA Modules:
  0.0 102.1 jit_solution(519784044184238167)
XLA Ops:
  0.0 0.0 copy-start
  0.0 1.6 %copy-done = bf16[4,2,64,2048]{3,2,1,0:T(8,128)(2,1)S(1)} copy-done((bf16[4,2,64,2048]{3,2,1,0:T(8,128)(2,1)S(1)}, bf16[4,2,64,2048]{3,2,1,0:T(8,128)(2,1)}, u32[]{:S(2)}) %copy-start) | copy-done | bytes 2097176
  1.6 0.0 copy-start.5
  1.6 0.7 copy-done.5
  2.3 1.0 shard_map.82
  3.2 1.5 %collective-permute-start = (bf16[33,16,128]{2,1,0:T(8,128)(2,1)S(1)}, bf16[33,16,128]{2,1,0:T(8,128)(2,1)S(1)}, u32[]{:S(2)}, u32[]{:S(2)}) collective-permute-start(bf16[33,16,128]{2,1,0:T(8,128)(2,1)S(1)} %get-tuple-element.17), channel_id=1, source_target_pairs={{0,1},{1,0},{2,3},{3,2},{4,5},{5,4},{6,7},{7,6},{8,9},{9,8},{10,11... | collective-permute-start | bytes 405512 | tf_op jit(solution)/shard_map/ppermute | solution.py:440
  4.7 1.0 collective-permute-done
  5.7 0.8 broadcast_in_dim.2.row_ref
  6.5 0.0 copy-start.1
  6.5 1.0 copy-done.1
  7.6 0.7 copy-done.3
  8.3 7.5 %shard_map.83 = (bf16[4,128,1024]{2,1,0:T(8,128)(2,1)}, bf16[3072,2048]{1,0:T(8,128)(2,1)}, bf16[4,2048,256]{2,1,0:T(8,128)(2,1)}) custom-call(s32[1]{0:T(128)} %bitcast.core_ref, f32[4,2,64,2048]{3,2,1,0:T(8,128)} %control_ref.1, f32[2,64,128]{2,1,0:T(8,128)S(1)} %broadcast_in_dim.2.row_ref, f32[2,2048]{1,0:T(2,128)S(1)} %copy-done.3, ...), custom_call_target="tpu_custom_call" | custom-call | flops 2147483648 | bytes 35651584 | tf_op jit(solution)/shard_map/pallas_call | solution.py:38
  15.8 0.4 collective-permute-start.8
  16.2 3.0 %collective-permute-start.4 = (bf16[2,33,16,128]{3,2,1,0:T(8,128)(2,1)S(1)}, bf16[2,33,16,128]{3,2,1,0:T(8,128)(2,1)S(1)}, u32[]{:S(2)}, u32[]{:S(2)}) collective-permute-start(bf16[2,33,16,128]{3,2,1,0:T(8,128)(2,1)S(1)} %pad_maximum_fusion.after_ref.refs_0_), channel_id=1, source_target_pairs={{0,8},{8,0},{1,9},{9,1},{2,10},{10,2},{3,11},{11,3},{4,12},{12,4},... | collective-permute-start | bytes 811016 | tf_op jit(solution)/shard_map/ppermute | solution.py:441
  19.2 3.6 %collective-permute-start.2 = (bf16[2,33,16,128]{3,2,1,0:T(8,128)(2,1)S(1)}, bf16[2,33,16,128]{3,2,1,0:T(8,128)(2,1)S(1)}, u32[]{:S(2)}, u32[]{:S(2)}) collective-permute-start(bf16[2,33,16,128]{3,2,1,0:T(8,128)(2,1)S(1)} %pad_maximum_fusion.after_ref.refs_0_), channel_id=1, source_target_pairs={{4,0},{6,2},{0,4},{2,6},{5,1},{7,3},{1,5},{3,7},{12,8},{14,10},{8,... | collective-permute-start | bytes 811016 | tf_op jit(solution)/shard_map/ppermute | solution.py:426
  22.8 0.4 collective-permute-start.1
  23.3 1.0 %collective-permute-start.3 = (bf16[2,33,16,128]{3,2,1,0:T(8,128)(2,1)S(1)}, bf16[2,33,16,128]{3,2,1,0:T(8,128)(2,1)S(1)}, u32[]{:S(2)}, u32[]{:S(2)}) collective-permute-start(bf16[2,33,16,128]{3,2,1,0:T(8,128)(2,1)S(1)} %pad_maximum_fusion.after_ref.refs_0_), channel_id=1, source_target_pairs={{6,0},{0,2},{2,4},{4,6},{7,1},{1,3},{3,5},{5,7},{14,8},{8,10},{10,... | collective-permute-start | bytes 811016 | tf_op jit(solution)/shard_map/ppermute | solution.py:426
  24.3 1.4 %collective-permute-done.4.after0_ref.refs_4_ = bf16[2,33,16,128]{3,2,1,0:T(8,128)(2,1)S(1)} collective-permute-done((bf16[2,33,16,128]{3,2,1,0:T(8,128)(2,1)S(1)}, bf16[2,33,16,128]{3,2,1,0:T(8,128)(2,1)S(1)}, u32[]{:S(2)}, u32[]{:S(2)}) %collective-permute-start.4) | collective-permute-done | bytes 270368 | tf_op jit(solution)/shard_map/ppermute | solution.py:441
  25.7 3.8 %collective-permute-start.5 = (bf16[2,33,16,128]{3,2,1,0:T(8,128)(2,1)S(1)}, bf16[2,33,16,128]{3,2,1,0:T(8,128)(2,1)S(1)}, u32[]{:S(2)}, u32[]{:S(2)}) collective-permute-start(bf16[2,33,16,128]{3,2,1,0:T(8,128)(2,1)S(1)} %collective-permute-done.4.after0_ref.refs_4_), channel_id=1, source_target_pairs={{2,0},{4,2},{6,4},{0,6},{3,1},{5,3},{7,5},{1,7},{10,8},{12,10},{14... | collective-permute-start | bytes 811016 | tf_op jit(solution)/shard_map/ppermute | solution.py:426
  29.5 0.0 collective-permute-done.2.after1_ref.refs_2_
  29.5 0.6 collective-permute-start.7
  30.0 5.5 %collective-permute-done.1.refs_1_ = bf16[2,33,16,128]{3,2,1,0:T(8,128)(2,1)S(1)} collective-permute-done((bf16[2,33,16,128]{3,2,1,0:T(8,128)(2,1)S(1)}, bf16[2,33,16,128]{3,2,1,0:T(8,128)(2,1)S(1)}, u32[]{:S(2)}, u32[]{:S(2)}) %collective-permute-start.1) | collective-permute-done | bytes 270368 | tf_op jit(solution)/shard_map/ppermute | solution.py:426
  35.5 0.1 collective-permute-start.6
  35.6 0.0 copy-done.2
  35.6 0.2 shard_map.85.refs_10_
  35.8 5.7 %shard_map.84 = (bf16[4,128,1024]{2,1,0:T(8,128)(2,1)S(1)}, bf16[4,2048,256]{2,1,0:T(8,128)(2,1)}) custom-call(s32[1]{0:T(128)} %bitcast.core_ref, bf16[3072,2048]{1,0:T(8,128)(2,1)} %get-tuple-element.18.scaled_hbm, f32[864,128]{1,0:T(8,128)S(1)} %copy-done.2, bf16[2,33,16,128]{3,2,1,0:T(8,128)(2,1)S(1)} %collective-permute-done.4.after0_ref.refs_4_, ...), custom_call_target="tpu_custom_call" | custom-call | flops 2147483648 | bytes 10485760 | tf_op jit(solution)/shard_map/pallas_call | solution.py:38
  41.5 0.0 copy-start.6
  41.5 0.0 collective-permute-done.3.refs_3_
  41.5 0.0 collective-permute-done.5.refs_5_
  41.5 0.0 collective-permute-done.7.refs_7_
  41.5 1.4 %collective-permute-done.6.refs_6_ = bf16[2,33,16,128]{3,2,1,0:T(8,128)(2,1)S(1)} collective-permute-done((bf16[2,33,16,128]{3,2,1,0:T(8,128)(2,1)S(1)}, bf16[2,33,16,128]{3,2,1,0:T(8,128)(2,1)S(1)}, u32[]{:S(2)}, u32[]{:S(2)}) %collective-permute-start.6) | collective-permute-done | bytes 270368 | tf_op jit(solution)/shard_map/ppermute | solution.py:445
  42.9 0.0 collective-permute-done.8.refs_9_
  42.9 3.8 %shard_map.86 = (bf16[8,8,32,128]{3,2,1,0:T(8,128)(2,1)}, bf16[96,256,256]{2,1,0:T(8,128)(2,1)}) custom-call(s32[1]{0:T(128)} %bitcast.1.place_ref, bf16[2,33,16,128]{3,2,1,0:T(8,128)(2,1)S(1)} %pad_maximum_fusion.after_ref.refs_0_, bf16[2,33,16,128]{3,2,1,0:T(8,128)(2,1)S(1)} %collective-permute-done.1.refs_1_, ...), custom_call_target="tpu_custom_call" | custom-call | flops 1073741824 | bytes 26214400 | tf_op jit(solution)/shard_map/pallas_call | solution.py:38
  46.8 9.9 %all-to-all-start = ((bf16[64,32,128]{2,1,0:T(8,128)(2,1)}), bf16[64,32,128]{2,1,0:T(8,128)(2,1)S(1)}, u32[]{:S(2)}, u32[]{:S(2)}) async-start(bf16[64,32,128]{2,1,0:T(8,128)(2,1)} %bitcast.5), calls=%async_computation | async-start | bytes 1048576 | tf_op jit(solution)/shard_map/all_to_all | solution.py:526
  56.7 0.0 copy-done.6
  56.7 0.1 fusion
  56.8 0.7 dynamic-slice_bitcast_fusion
  57.5 1.8 %collective-permute-start.9 = (f32[2,16,128]{2,1,0:T(8,128)S(1)}, f32[2,16,128]{2,1,0:T(8,128)S(1)}, u32[]{:S(2)}, u32[]{:S(2)}) collective-permute-start(f32[2,16,128]{2,1,0:T(8,128)S(1)} %pad_maximum_fusion.2), channel_id=1, source_target_pairs={{0,1},{1,0},{2,3},{3,2},{4,5},{5,4},{6,7},{7,6},{8,9},{9,8},{10,11... | collective-permute-start | bytes 49160 | tf_op jit(solution)/shard_map/ppermute | solution.py:458
  59.3 0.8 collective-permute-done.9.lent_ref
  60.1 7.5 %all-to-all-done.cells_ref = bf16[64,32,128]{2,1,0:T(8,128)(2,1)S(1)} async-done(((bf16[64,32,128]{2,1,0:T(8,128)(2,1)}), bf16[64,32,128]{2,1,0:T(8,128)(2,1)S(1)}, u32[]{:S(2)}, u32[]{:S(2)}) %all-to-all-start) | async-done | bytes 524320 | tf_op jit(solution)/shard_map/all_to_all | solution.py:526
  67.6 0.1 shard_map.87
  67.8 17.0 %all_to_all.10 = bf16[64,32,128]{2,1,0:T(8,128)(2,1)S(1)} all-to-all(bf16[64,32,128]{2,1,0:T(8,128)(2,1)S(1)} %shard_map.87), channel_id=1, replica_groups=mesh['member'=8,'across'=2,'along'=4,'core'=2] {'member','across','along'}, dimensions={0} | all-to-all | bytes 1048576 | tf_op jit(solution)/shard_map/all_to_all | solution.py:530
  84.7 2.1 %shard_map.88 = (bf16[4,128,1024]{2,1,0:T(8,128)(2,1)S(1)}, bf16[4,128,1024]{2,1,0:T(8,128)(2,1)S(1)}) custom-call(s32[1]{0:T(128)} %bitcast.1.place_ref, bf16[2,33,16,128]{3,2,1,0:T(8,128)(2,1)S(1)} %pad_maximum_fusion.after_ref.refs_0_, bf16[2,33,16,128]{3,2,1,0:T(8,128)(2,1)S(1)} %collective-permute-done.1.refs_1_, ...), custom_call_target="tpu_custom_call" | custom-call | flops 268435456 | bytes 4194304 | tf_op jit(solution)/shard_map/pallas_call | solution.py:38
  86.9 3.2 %collective-permute-start.10 = (bf16[4,128,1024]{2,1,0:T(8,128)(2,1)S(1)}, bf16[4,128,1024]{2,1,0:T(8,128)(2,1)S(1)}, u32[]{:S(2)}, u32[]{:S(2)}) collective-permute-start(bf16[4,128,1024]{2,1,0:T(8,128)(2,1)S(1)} %get-tuple-element.23), channel_id=1, source_target_pairs={{0,1},{1,0},{2,3},{3,2},{4,5},{5,4},{6,7},{7,6},{8,9},{9,8},{10,11... | collective-permute-start | bytes 3145736 | tf_op jit(solution)/shard_map/ppermute | solution.py:540
  90.0 5.1 %shard_map.89.sum_ref = f32[8,512,256]{2,1,0:T(8,128)S(1)} custom-call(s32[1]{0:T(128)} %bitcast.core_ref, bf16[4,128,1024]{2,1,0:T(8,128)(2,1)S(1)} %get-tuple-element.24.own_ref, bf16[4,2048,256]{2,1,0:T(8,128)(2,1)} %get-tuple-element.25.table0_ref, bf16[4,2048,256]{2,1,0:T(8,128)(2,1)} %get-tuple-element.26.table1_ref), custom_call_target="tpu_custom_call" | custom-call | flops 2147483648 | bytes 8388608 | tf_op jit(solution)/shard_map/pallas_call | solution.py:38
  95.1 0.0 collective-permute-done.10.par_ref
  95.1 0.0 copy-done.4
  95.1 7.0 %shard_map.90 = f32[4,2,64,2048]{3,2,1,0:T(8,128)} custom-call(s32[1]{0:T(128)} %bitcast.core_ref, bf16[4,128,1024]{2,1,0:T(8,128)(2,1)S(1)} %collective-permute-done.10.par_ref, f32[8,512,256]{2,1,0:T(8,128)S(1)} %shard_map.89.sum_ref, bf16[4,2048,256]{2,1,0:T(8,128)(2,1)} %get-tuple-element.25.table0_ref, ...), custom_call_target="tpu_custom_call" | custom-call | flops 2147483648 | bytes 8388608 | tf_op jit(solution)/shard_map/pallas_call | solution.py:38
  (6 shorter events, 0.0 us)
Async XLA Ops:
  0.0 1.6 %copy-start = (bf16[4,2,64,2048]{3,2,1,0:T(8,128)(2,1)S(1)}, bf16[4,2,64,2048]{3,2,1,0:T(8,128)(2,1)}, u32[]{:S(2)}) copy-start(bf16[4,2,64,2048]{3,2,1,0:T(8,128)(2,1)} %pert_ref.1) | copy-start | bytes 6291460
  1.6 0.7 copy-start.5
  3.2 2.5 %collective-permute-start = (bf16[33,16,128]{2,1,0:T(8,128)(2,1)S(1)}, bf16[33,16,128]{2,1,0:T(8,128)(2,1)S(1)}, u32[]{:S(2)}, u32[]{:S(2)}) collective-permute-start(bf16[33,16,128]{2,1,0:T(8,128)(2,1)S(1)} %get-tuple-element.17), channel_id=1, source_target_pairs={{0,1},{1,0},{2,3},{3,2},{4,5},{5,4},{6,7},{7,6},{8,9},{9,8},{10,11... | collective-permute-start | bytes 405512 | tf_op jit(solution)/shard_map/ppermute | solution.py:440
  5.7 29.9 %copy-start.2 = (f32[864,128]{1,0:T(8,128)S(1)}, f32[864,128]{1,0:T(8,128)}, u32[]{:S(2)}) copy-start(f32[864,128]{1,0:T(8,128)} %constant.30.clone.factor_ref) | copy-start | bytes 1327108
  6.5 1.0 %copy-start.1 = (f32[864,128]{1,0:T(8,128)S(1)}, f32[864,128]{1,0:T(8,128)}, u32[]{:S(2)}) copy-start(f32[864,128]{1,0:T(8,128)} %constant.30.clone.factor_ref) | copy-start | bytes 1327108
  7.6 0.7 copy-start.3
  15.8 27.2 %collective-permute-start.8 = (bf16[4,128,1024]{2,1,0:T(8,128)(2,1)}, bf16[4,128,1024]{2,1,0:T(8,128)(2,1)}, u32[]{:S(2)}, u32[]{:S(2)}) collective-permute-start(bf16[4,128,1024]{2,1,0:T(8,128)(2,1)} %get-tuple-element.20), channel_id=1, source_target_pairs={{0,1},{1,0},{2,3},{3,2},{4,5},{5,4},{6,7},{7,6},{8,9},{9,8},{10,11... | collective-permute-start | bytes 3145736 | tf_op jit(solution)/shard_map/ppermute | solution.py:495
  16.2 9.5 %collective-permute-start.4 = (bf16[2,33,16,128]{3,2,1,0:T(8,128)(2,1)S(1)}, bf16[2,33,16,128]{3,2,1,0:T(8,128)(2,1)S(1)}, u32[]{:S(2)}, u32[]{:S(2)}) collective-permute-start(bf16[2,33,16,128]{3,2,1,0:T(8,128)(2,1)S(1)} %pad_maximum_fusion.after_ref.refs_0_), channel_id=1, source_target_pairs={{0,8},{8,0},{1,9},{9,1},{2,10},{10,2},{3,11},{11,3},{4,12},{12,4},... | collective-permute-start | bytes 811016 | tf_op jit(solution)/shard_map/ppermute | solution.py:441
  19.2 10.2 %collective-permute-start.2 = (bf16[2,33,16,128]{3,2,1,0:T(8,128)(2,1)S(1)}, bf16[2,33,16,128]{3,2,1,0:T(8,128)(2,1)S(1)}, u32[]{:S(2)}, u32[]{:S(2)}) collective-permute-start(bf16[2,33,16,128]{3,2,1,0:T(8,128)(2,1)S(1)} %pad_maximum_fusion.after_ref.refs_0_), channel_id=1, source_target_pairs={{4,0},{6,2},{0,4},{2,6},{5,1},{7,3},{1,5},{3,7},{12,8},{14,10},{8,... | collective-permute-start | bytes 811016 | tf_op jit(solution)/shard_map/ppermute | solution.py:426
  22.8 12.7 %collective-permute-start.1 = (bf16[2,33,16,128]{3,2,1,0:T(8,128)(2,1)S(1)}, bf16[2,33,16,128]{3,2,1,0:T(8,128)(2,1)S(1)}, u32[]{:S(2)}, u32[]{:S(2)}) collective-permute-start(bf16[2,33,16,128]{3,2,1,0:T(8,128)(2,1)S(1)} %pad_maximum_fusion.after_ref.refs_0_), channel_id=1, source_target_pairs={{2,0},{4,2},{6,4},{0,6},{3,1},{5,3},{7,5},{1,7},{10,8},{12,10},{14... | collective-permute-start | bytes 811016 | tf_op jit(solution)/shard_map/ppermute | solution.py:426
  23.3 18.2 %collective-permute-start.3 = (bf16[2,33,16,128]{3,2,1,0:T(8,128)(2,1)S(1)}, bf16[2,33,16,128]{3,2,1,0:T(8,128)(2,1)S(1)}, u32[]{:S(2)}, u32[]{:S(2)}) collective-permute-start(bf16[2,33,16,128]{3,2,1,0:T(8,128)(2,1)S(1)} %pad_maximum_fusion.after_ref.refs_0_), channel_id=1, source_target_pairs={{6,0},{0,2},{2,4},{4,6},{7,1},{1,3},{3,5},{5,7},{14,8},{8,10},{10,... | collective-permute-start | bytes 811016 | tf_op jit(solution)/shard_map/ppermute | solution.py:426
  25.7 15.8 %collective-permute-start.5 = (bf16[2,33,16,128]{3,2,1,0:T(8,128)(2,1)S(1)}, bf16[2,33,16,128]{3,2,1,0:T(8,128)(2,1)S(1)}, u32[]{:S(2)}, u32[]{:S(2)}) collective-permute-start(bf16[2,33,16,128]{3,2,1,0:T(8,128)(2,1)S(1)} %collective-permute-done.4.after0_ref.refs_4_), channel_id=1, source_target_pairs={{2,0},{4,2},{6,4},{0,6},{3,1},{5,3},{7,5},{1,7},{10,8},{12,10},{14... | collective-permute-start | bytes 811016 | tf_op jit(solution)/shard_map/ppermute | solution.py:426
  29.5 12.1 %collective-permute-start.7 = (bf16[2,33,16,128]{3,2,1,0:T(8,128)(2,1)S(1)}, bf16[2,33,16,128]{3,2,1,0:T(8,128)(2,1)S(1)}, u32[]{:S(2)}, u32[]{:S(2)}) collective-permute-start(bf16[2,33,16,128]{3,2,1,0:T(8,128)(2,1)S(1)} %collective-permute-done.4.after0_ref.refs_4_), channel_id=1, source_target_pairs={{6,0},{0,2},{2,4},{4,6},{7,1},{1,3},{3,5},{5,7},{14,8},{8,10},{10,... | collective-permute-start | bytes 811016 | tf_op jit(solution)/shard_map/ppermute | solution.py:426
  35.5 7.4 %collective-permute-start.6 = (bf16[2,33,16,128]{3,2,1,0:T(8,128)(2,1)S(1)}, bf16[2,33,16,128]{3,2,1,0:T(8,128)(2,1)S(1)}, u32[]{:S(2)}, u32[]{:S(2)}) collective-permute-start(bf16[2,33,16,128]{3,2,1,0:T(8,128)(2,1)S(1)} %collective-permute-done.2.after1_ref.refs_2_), channel_id=1, source_target_pairs={{0,8},{8,0},{1,9},{9,1},{2,10},{10,2},{3,11},{11,3},{4,12},{12,4},... | collective-permute-start | bytes 811016 | tf_op jit(solution)/shard_map/ppermute | solution.py:445
  41.5 15.2 %copy-start.6 = (s32[256]{0:T(256)S(1)}, s32[256]{0:T(256)}, u32[]{:S(2)}) copy-start(s32[256]{0:T(256)} %param.13) | copy-start | bytes 3076
  46.8 20.9 %all-to-all-start = ((bf16[64,32,128]{2,1,0:T(8,128)(2,1)}), bf16[64,32,128]{2,1,0:T(8,128)(2,1)S(1)}, u32[]{:S(2)}, u32[]{:S(2)}) async-start(bf16[64,32,128]{2,1,0:T(8,128)(2,1)} %bitcast.5), calls=%async_computation | async-start | bytes 1048576 | tf_op jit(solution)/shard_map/all_to_all | solution.py:526
  57.5 2.6 %collective-permute-start.9 = (f32[2,16,128]{2,1,0:T(8,128)S(1)}, f32[2,16,128]{2,1,0:T(8,128)S(1)}, u32[]{:S(2)}, u32[]{:S(2)}) collective-permute-start(f32[2,16,128]{2,1,0:T(8,128)S(1)} %pad_maximum_fusion.2), channel_id=1, source_target_pairs={{0,1},{1,0},{2,3},{3,2},{4,5},{5,4},{6,7},{7,6},{8,9},{9,8},{10,11... | collective-permute-start | bytes 49160 | tf_op jit(solution)/shard_map/ppermute | solution.py:458
  86.9 8.3 %collective-permute-start.10 = (bf16[4,128,1024]{2,1,0:T(8,128)(2,1)S(1)}, bf16[4,128,1024]{2,1,0:T(8,128)(2,1)S(1)}, u32[]{:S(2)}, u32[]{:S(2)}) collective-permute-start(bf16[4,128,1024]{2,1,0:T(8,128)(2,1)S(1)} %get-tuple-element.23), channel_id=1, source_target_pairs={{0,1},{1,0},{2,3},{3,2},{4,5},{5,4},{6,7},{7,6},{8,9},{9,8},{10,11... | collective-permute-start | bytes 3145736 | tf_op jit(solution)/shard_map/ppermute | solution.py:540
  90.0 5.1 %copy-start.4 = (f32[2,2048]{1,0:T(2,128)S(1)}, f32[2,2048]{1,0:T(2,128)}, u32[]{:S(2)}) copy-start(f32[2,2048]{1,0:T(2,128)} %col_ref.3) | copy-start | bytes 49156

commit v5 on v4

--- a/solution.py
+++ b/solution.py
@@ -317,26 +317,23 @@
 def streamed(tables, rows, block_ref, sems):
     steps = tables[0].shape[0]
 
-    def fetch(i, n):
-        at = i * steps + n
-        return pltpu.make_async_copy(tables[i].at[n, rows, :], block_ref.at[at], sems.at[at])
+    def fetch(table, n, at):
+        return pltpu.make_async_copy(table.at[n, rows, :], block_ref.at[at], sems.at[at])
 
     for n in range(3):
-        fetch(0, n).start()
-
-    def block(i, n):
+        fetch(tables[0], n, n).start()
+
+    def block(n):
         @pl.when(n + 3 < steps)
         def _():
-            fetch(i, n + 3).start()
-
-        if i + 1 < len(tables):
-
-            @pl.when(n + 3 >= steps)
-            def _():
-                fetch(i + 1, n + 3 - steps).start()
-
-        fetch(i, n).wait()
-        return block_ref[i * steps + n]
+            fetch(tables[0], n + 3, n + 3).start()
+
+        @pl.when((n + 3 >= steps) & (n + 3 < 2 * steps))
+        def _():
+            fetch(tables[1], n + 3 - steps, n + 3).start()
+
+        fetch(tables[0], 0, n).wait()
+        return block_ref[n]
 
     return block
 
@@ -344,21 +341,15 @@
 def inverse_own(core_ref, own_ref, table0_ref, table1_ref, sum_ref, block_ref, sems):
     members, depth, width = own_ref.shape
     near = pl.ds(pl.multiple_of(core_ref[0] * width, width), width)
-    half = table0_ref.shape[0]
-    core = core_ref[0]
     block = streamed((table0_ref, table1_ref), near, block_ref, sems)
-    for i in range(2):
-        which = (1 - core) if i == 0 else core
-
-        def step(n, carry, i=i, which=which):
-            sum_ref[which * half + n] = jnp.dot(
-                own_ref[...].reshape(members * depth, width),
-                block(i, n),
-                preferred_element_type=F32,
-            )
-            return carry
-
-        lax.fori_loop(0, half, step, 0)
+
+    def step(n, carry):
+        sum_ref[n] = jnp.dot(
+            own_ref[...].reshape(members * depth, width), block(n), preferred_element_type=F32
+        )
+        return carry
+
+    lax.fori_loop(0, sum_ref.shape[0], step, 0)
 
 
 def inverse_par(
@@ -368,40 +359,36 @@
     members, depth, width = par_ref.shape
     levels, rows, _ = row_ref.shape
     core = core_ref[0]
-    half = table0_ref.shape[0]
+    steps = sum_ref.shape[0]
+    half = steps // 2
     far = pl.ds(pl.multiple_of((1 - core) * width, width), width)
+    block = streamed((table0_ref, table1_ref), far, block_ref, reads)
 
     def copy(nb, slot):
         cols = pl.ds(pl.multiple_of(nb * WIDE, WIDE), WIDE)
         return pltpu.make_async_copy(piece.at[slot], out_ref.at[:, :, :, cols], sems.at[slot])
 
-    block = streamed((table0_ref, table1_ref), far, block_ref, reads)
-    for i in range(2):
-        which = (1 - core) if i == 0 else core
-
-        def step(n, carry, i=i, which=which):
-            slot = lax.rem(n, 2)
-            nb = which * half + n
-            cols = pl.ds(pl.multiple_of(nb * WIDE, WIDE), WIDE)
-            product = sum_ref[nb] + jnp.dot(
-                par_ref[...].reshape(members * depth, width),
-                block(i, n),
-                preferred_element_type=F32,
-            )
-            product = product.reshape(members, levels, rows, WIDE)
-
-            @pl.when(n >= (2 if i == 0 else 0))
-            def _():
-                copy(nb, slot).wait()
-
-            for l in range(levels):
-                amplitude = row_ref[l][:, :1] * col_ref[l : l + 1, cols]
-                for m in range(members):
-                    piece[slot, m, l] = product[m, l] * amplitude
-            copy(nb, slot).start()
-            return carry
-
-        lax.fori_loop(0, half, step, 0)
+    def step(n, carry):
+        slot = lax.rem(n, 2)
+        nb = lax.rem(n + (1 - core) * half, steps)
+        cols = pl.ds(pl.multiple_of(nb * WIDE, WIDE), WIDE)
+        product = sum_ref[n] + jnp.dot(
+            par_ref[...].reshape(members * depth, width), block(n), preferred_element_type=F32
+        )
+        product = product.reshape(members, levels, rows, WIDE)
+
+        @pl.when(n >= 2)
+        def _():
+            copy(nb, slot).wait()
+
+        for l in range(levels):
+            amplitude = row_ref[l][:, :1] * col_ref[l : l + 1, cols]
+            for m in range(members):
+                piece[slot, m, l] = product[m, l] * amplitude
+        copy(nb, slot).start()
+        return carry
+
+    lax.fori_loop(0, steps, step, 0)
     for slot in range(2):
         copy(slot, slot).wait()
 

time: 103 us -> 103 us (level)
  no operation moved by 1% of the time
where the time goes in v5:
time: 103 us; the launch traced here: 102 us
  Pallas kernels  32.5 us (32%)
  starting transfers between devices  29.2 us (28%)
  waiting for transfers between devices  17.7 us (17%)
  blocking collectives  17 us (17%)
  local copies, waits for them, and re-layouts  5.54 us (5%)
    pallas_call x9, Pallas kernels, launch(): results = call(*args)  32.5 us
    all_to_all x1, blocking collectives, shards(): lax.all_to_all(scores, SAME_CORE, split_axis=0, concat_axis=0, tiled=True)  17 us
    all_to_all x1, starting transfers between devices, shards(): lax.all_to_all(partial.reshape(peers, 2 * 16, TILE), SAME_CORE, split_axi...  9.88 us
    ppermute x5, starting transfers between devices, from_next(): return lax.ppermute(array, 'along', [((i + step) % 4, i) for i in range(4)])  9.38 us
    all_to_all x1, waiting for transfers between devices, shards(): lax.all_to_all(partial.reshape(peers, 2 * 16, TILE), SAME_CORE, split_axi...  7.51 us
    ppermute x5, waiting for transfers between devices, from_next(): return lax.ppermute(array, 'along', [((i + step) % 4, i) for i in range(4)])  5.53 us
    unnamed x14, local copies, waits for them, and re-layouts  4.02 us
    ppermute x1, starting transfers between devices, shards(): back_other = lax.ppermute(back_send, 'core', swap)  3.15 us
  transfers between devices with their start and end apart: 12, of which 6 were waited for; matrix products, arithmetic and copies ran while one was open for 1% of the time, Pallas kernels for 11%

profile of v5, /device:TPU:1, one launch (start us, length us, event | category | flops | bytes accessed | tf_op | source)
XLA Modules:
  0.0 102.1 jit_solution(6662287972934242984)
XLA Ops:
  0.0 0.0 copy-start
  0.0 1.6 %copy-done = bf16[4,2,64,2048]{3,2,1,0:T(8,128)(2,1)S(1)} copy-done((bf16[4,2,64,2048]{3,2,1,0:T(8,128)(2,1)S(1)}, bf16[4,2,64,2048]{3,2,1,0:T(8,128)(2,1)}, u32[]{:S(2)}) %copy-start) | copy-done | bytes 2097176
  1.6 0.0 copy-start.5
  1.6 0.7 copy-done.5
  2.3 1.0 shard_map.82
  3.2 1.5 %collective-permute-start = (bf16[33,16,128]{2,1,0:T(8,128)(2,1)S(1)}, bf16[33,16,128]{2,1,0:T(8,128)(2,1)S(1)}, u32[]{:S(2)}, u32[]{:S(2)}) collective-permute-start(bf16[33,16,128]{2,1,0:T(8,128)(2,1)S(1)} %get-tuple-element.17), channel_id=1, source_target_pairs={{0,1},{1,0},{2,3},{3,2},{4,5},{5,4},{6,7},{7,6},{8,9},{9,8},{10,11... | collective-permute-start | bytes 405512 | tf_op jit(solution)/shard_map/ppermute | solution.py:427
  4.7 1.0 collective-permute-done
  5.7 0.8 broadcast_in_dim.2.row_ref
  6.5 0.0 copy-start.1
  6.5 1.0 copy-done.1
  7.6 0.7 copy-done.3
  8.3 7.5 %shard_map.83 = (bf16[4,128,1024]{2,1,0:T(8,128)(2,1)}, bf16[3072,2048]{1,0:T(8,128)(2,1)}, bf16[4,2048,256]{2,1,0:T(8,128)(2,1)}) custom-call(s32[1]{0:T(128)} %bitcast.core_ref, f32[4,2,64,2048]{3,2,1,0:T(8,128)} %control_ref.1, f32[2,64,128]{2,1,0:T(8,128)S(1)} %broadcast_in_dim.2.row_ref, f32[2,2048]{1,0:T(2,128)S(1)} %copy-done.3, ...), custom_call_target="tpu_custom_call" | custom-call | flops 2147483648 | bytes 35651584 | tf_op jit(solution)/shard_map/pallas_call | solution.py:38
  15.8 0.4 collective-permute-start.8
  16.2 3.0 %collective-permute-start.4 = (bf16[2,33,16,128]{3,2,1,0:T(8,128)(2,1)S(1)}, bf16[2,33,16,128]{3,2,1,0:T(8,128)(2,1)S(1)}, u32[]{:S(2)}, u32[]{:S(2)}) collective-permute-start(bf16[2,33,16,128]{3,2,1,0:T(8,128)(2,1)S(1)} %pad_maximum_fusion.after_ref.refs_0_), channel_id=1, source_target_pairs={{0,8},{8,0},{1,9},{9,1},{2,10},{10,2},{3,11},{11,3},{4,12},{12,4},... | collective-permute-start | bytes 811016 | tf_op jit(solution)/shard_map/ppermute | solution.py:428
  19.2 3.6 %collective-permute-start.2 = (bf16[2,33,16,128]{3,2,1,0:T(8,128)(2,1)S(1)}, bf16[2,33,16,128]{3,2,1,0:T(8,128)(2,1)S(1)}, u32[]{:S(2)}, u32[]{:S(2)}) collective-permute-start(bf16[2,33,16,128]{3,2,1,0:T(8,128)(2,1)S(1)} %pad_maximum_fusion.after_ref.refs_0_), channel_id=1, source_target_pairs={{4,0},{6,2},{0,4},{2,6},{5,1},{7,3},{1,5},{3,7},{12,8},{14,10},{8,... | collective-permute-start | bytes 811016 | tf_op jit(solution)/shard_map/ppermute | solution.py:413
  22.8 0.4 collective-permute-start.1
  23.3 1.0 %collective-permute-start.3 = (bf16[2,33,16,128]{3,2,1,0:T(8,128)(2,1)S(1)}, bf16[2,33,16,128]{3,2,1,0:T(8,128)(2,1)S(1)}, u32[]{:S(2)}, u32[]{:S(2)}) collective-permute-start(bf16[2,33,16,128]{3,2,1,0:T(8,128)(2,1)S(1)} %pad_maximum_fusion.after_ref.refs_0_), channel_id=1, source_target_pairs={{6,0},{0,2},{2,4},{4,6},{7,1},{1,3},{3,5},{5,7},{14,8},{8,10},{10,... | collective-permute-start | bytes 811016 | tf_op jit(solution)/shard_map/ppermute | solution.py:413
  24.3 1.4 %collective-permute-done.4.after0_ref.refs_4_ = bf16[2,33,16,128]{3,2,1,0:T(8,128)(2,1)S(1)} collective-permute-done((bf16[2,33,16,128]{3,2,1,0:T(8,128)(2,1)S(1)}, bf16[2,33,16,128]{3,2,1,0:T(8,128)(2,1)S(1)}, u32[]{:S(2)}, u32[]{:S(2)}) %collective-permute-start.4) | collective-permute-done | bytes 270368 | tf_op jit(solution)/shard_map/ppermute | solution.py:428
  25.7 3.8 %collective-permute-start.5 = (bf16[2,33,16,128]{3,2,1,0:T(8,128)(2,1)S(1)}, bf16[2,33,16,128]{3,2,1,0:T(8,128)(2,1)S(1)}, u32[]{:S(2)}, u32[]{:S(2)}) collective-permute-start(bf16[2,33,16,128]{3,2,1,0:T(8,128)(2,1)S(1)} %collective-permute-done.4.after0_ref.refs_4_), channel_id=1, source_target_pairs={{2,0},{4,2},{6,4},{0,6},{3,1},{5,3},{7,5},{1,7},{10,8},{12,10},{14... | collective-permute-start | bytes 811016 | tf_op jit(solution)/shard_map/ppermute | solution.py:413
  29.5 0.0 collective-permute-done.2.after1_ref.refs_2_
  29.5 0.6 collective-permute-start.7
  30.0 5.5 %collective-permute-done.1.refs_1_ = bf16[2,33,16,128]{3,2,1,0:T(8,128)(2,1)S(1)} collective-permute-done((bf16[2,33,16,128]{3,2,1,0:T(8,128)(2,1)S(1)}, bf16[2,33,16,128]{3,2,1,0:T(8,128)(2,1)S(1)}, u32[]{:S(2)}, u32[]{:S(2)}) %collective-permute-start.1) | collective-permute-done | bytes 270368 | tf_op jit(solution)/shard_map/ppermute | solution.py:413
  35.5 0.1 collective-permute-start.6
  35.6 0.0 copy-done.2
  35.6 0.2 shard_map.85.refs_10_
  35.8 5.7 %shard_map.84 = (bf16[4,128,1024]{2,1,0:T(8,128)(2,1)S(1)}, bf16[4,2048,256]{2,1,0:T(8,128)(2,1)}) custom-call(s32[1]{0:T(128)} %bitcast.core_ref, bf16[3072,2048]{1,0:T(8,128)(2,1)} %get-tuple-element.18.scaled_hbm, f32[864,128]{1,0:T(8,128)S(1)} %copy-done.2, bf16[2,33,16,128]{3,2,1,0:T(8,128)(2,1)S(1)} %collective-permute-done.4.after0_ref.refs_4_, ...), custom_call_target="tpu_custom_call" | custom-call | flops 2147483648 | bytes 10485760 | tf_op jit(solution)/shard_map/pallas_call | solution.py:38
  41.5 0.0 copy-start.6
  41.5 0.0 collective-permute-done.3.refs_3_
  41.5 0.0 collective-permute-done.5.refs_5_
  41.5 0.0 collective-permute-done.7.refs_7_
  41.5 1.4 %collective-permute-done.6.refs_6_ = bf16[2,33,16,128]{3,2,1,0:T(8,128)(2,1)S(1)} collective-permute-done((bf16[2,33,16,128]{3,2,1,0:T(8,128)(2,1)S(1)}, bf16[2,33,16,128]{3,2,1,0:T(8,128)(2,1)S(1)}, u32[]{:S(2)}, u32[]{:S(2)}) %collective-permute-start.6) | collective-permute-done | bytes 270368 | tf_op jit(solution)/shard_map/ppermute | solution.py:432
  42.9 0.0 collective-permute-done.8.refs_9_
  42.9 3.8 %shard_map.86 = (bf16[8,8,32,128]{3,2,1,0:T(8,128)(2,1)}, bf16[96,256,256]{2,1,0:T(8,128)(2,1)}) custom-call(s32[1]{0:T(128)} %bitcast.1.place_ref, bf16[2,33,16,128]{3,2,1,0:T(8,128)(2,1)S(1)} %pad_maximum_fusion.after_ref.refs_0_, bf16[2,33,16,128]{3,2,1,0:T(8,128)(2,1)S(1)} %collective-permute-done.1.refs_1_, ...), custom_call_target="tpu_custom_call" | custom-call | flops 1073741824 | bytes 26214400 | tf_op jit(solution)/shard_map/pallas_call | solution.py:38
  46.8 9.9 %all-to-all-start = ((bf16[64,32,128]{2,1,0:T(8,128)(2,1)}), bf16[64,32,128]{2,1,0:T(8,128)(2,1)S(1)}, u32[]{:S(2)}, u32[]{:S(2)}) async-start(bf16[64,32,128]{2,1,0:T(8,128)(2,1)} %bitcast.5), calls=%async_computation | async-start | bytes 1048576 | tf_op jit(solution)/shard_map/all_to_all | solution.py:513
  56.7 0.0 copy-done.6
  56.7 0.1 fusion
  56.8 0.7 dynamic-slice_bitcast_fusion
  57.5 1.8 %collective-permute-start.9 = (f32[2,16,128]{2,1,0:T(8,128)S(1)}, f32[2,16,128]{2,1,0:T(8,128)S(1)}, u32[]{:S(2)}, u32[]{:S(2)}) collective-permute-start(f32[2,16,128]{2,1,0:T(8,128)S(1)} %pad_maximum_fusion.2), channel_id=1, source_target_pairs={{0,1},{1,0},{2,3},{3,2},{4,5},{5,4},{6,7},{7,6},{8,9},{9,8},{10,11... | collective-permute-start | bytes 49160 | tf_op jit(solution)/shard_map/ppermute | solution.py:445
  59.3 0.8 collective-permute-done.9.lent_ref
  60.1 7.5 %all-to-all-done.cells_ref = bf16[64,32,128]{2,1,0:T(8,128)(2,1)S(1)} async-done(((bf16[64,32,128]{2,1,0:T(8,128)(2,1)}), bf16[64,32,128]{2,1,0:T(8,128)(2,1)S(1)}, u32[]{:S(2)}, u32[]{:S(2)}) %all-to-all-start) | async-done | bytes 524320 | tf_op jit(solution)/shard_map/all_to_all | solution.py:513
  67.6 0.1 shard_map.87
  67.8 17.0 %all_to_all.10 = bf16[64,32,128]{2,1,0:T(8,128)(2,1)S(1)} all-to-all(bf16[64,32,128]{2,1,0:T(8,128)(2,1)S(1)} %shard_map.87), channel_id=1, replica_groups=mesh['member'=8,'across'=2,'along'=4,'core'=2] {'member','across','along'}, dimensions={0} | all-to-all | bytes 1048576 | tf_op jit(solution)/shard_map/all_to_all | solution.py:517
  84.7 2.1 %shard_map.88 = (bf16[4,128,1024]{2,1,0:T(8,128)(2,1)S(1)}, bf16[4,128,1024]{2,1,0:T(8,128)(2,1)S(1)}) custom-call(s32[1]{0:T(128)} %bitcast.1.place_ref, bf16[2,33,16,128]{3,2,1,0:T(8,128)(2,1)S(1)} %pad_maximum_fusion.after_ref.refs_0_, bf16[2,33,16,128]{3,2,1,0:T(8,128)(2,1)S(1)} %collective-permute-done.1.refs_1_, ...), custom_call_target="tpu_custom_call" | custom-call | flops 268435456 | bytes 4194304 | tf_op jit(solution)/shard_map/pallas_call | solution.py:38
  86.9 3.2 %collective-permute-start.10 = (bf16[4,128,1024]{2,1,0:T(8,128)(2,1)S(1)}, bf16[4,128,1024]{2,1,0:T(8,128)(2,1)S(1)}, u32[]{:S(2)}, u32[]{:S(2)}) collective-permute-start(bf16[4,128,1024]{2,1,0:T(8,128)(2,1)S(1)} %get-tuple-element.23), channel_id=1, source_target_pairs={{0,1},{1,0},{2,3},{3,2},{4,5},{5,4},{6,7},{7,6},{8,9},{9,8},{10,11... | collective-permute-start | bytes 3145736 | tf_op jit(solution)/shard_map/ppermute | solution.py:527
  90.0 5.1 %shard_map.89.sum_ref = f32[8,512,256]{2,1,0:T(8,128)S(1)} custom-call(s32[1]{0:T(128)} %bitcast.core_ref, bf16[4,128,1024]{2,1,0:T(8,128)(2,1)S(1)} %get-tuple-element.24.own_ref, bf16[4,2048,256]{2,1,0:T(8,128)(2,1)} %get-tuple-element.25.table0_ref, bf16[4,2048,256]{2,1,0:T(8,128)(2,1)} %get-tuple-element.26.table1_ref), custom_call_target="tpu_custom_call" | custom-call | flops 2147483648 | bytes 8388608 | tf_op jit(solution)/shard_map/pallas_call | solution.py:38
  95.1 0.0 collective-permute-done.10.par_ref
  95.1 0.0 copy-done.4
  95.1 7.0 %shard_map.90 = f32[4,2,64,2048]{3,2,1,0:T(8,128)} custom-call(s32[1]{0:T(128)} %bitcast.core_ref, bf16[4,128,1024]{2,1,0:T(8,128)(2,1)S(1)} %collective-permute-done.10.par_ref, f32[8,512,256]{2,1,0:T(8,128)S(1)} %shard_map.89.sum_ref, bf16[4,2048,256]{2,1,0:T(8,128)(2,1)} %get-tuple-element.25.table0_ref, ...), custom_call_target="tpu_custom_call" | custom-call | flops 2147483648 | bytes 8388608 | tf_op jit(solution)/shard_map/pallas_call | solution.py:38
  (6 shorter events, 0.0 us)
Async XLA Ops:
  0.0 1.6 %copy-start = (bf16[4,2,64,2048]{3,2,1,0:T(8,128)(2,1)S(1)}, bf16[4,2,64,2048]{3,2,1,0:T(8,128)(2,1)}, u32[]{:S(2)}) copy-start(bf16[4,2,64,2048]{3,2,1,0:T(8,128)(2,1)} %pert_ref.1) | copy-start | bytes 6291460
  1.6 0.7 copy-start.5
  3.2 2.5 %collective-permute-start = (bf16[33,16,128]{2,1,0:T(8,128)(2,1)S(1)}, bf16[33,16,128]{2,1,0:T(8,128)(2,1)S(1)}, u32[]{:S(2)}, u32[]{:S(2)}) collective-permute-start(bf16[33,16,128]{2,1,0:T(8,128)(2,1)S(1)} %get-tuple-element.17), channel_id=1, source_target_pairs={{0,1},{1,0},{2,3},{3,2},{4,5},{5,4},{6,7},{7,6},{8,9},{9,8},{10,11... | collective-permute-start | bytes 405512 | tf_op jit(solution)/shard_map/ppermute | solution.py:427
  5.7 29.9 %copy-start.2 = (f32[864,128]{1,0:T(8,128)S(1)}, f32[864,128]{1,0:T(8,128)}, u32[]{:S(2)}) copy-start(f32[864,128]{1,0:T(8,128)} %constant.30.clone.factor_ref) | copy-start | bytes 1327108
  6.5 1.0 %copy-start.1 = (f32[864,128]{1,0:T(8,128)S(1)}, f32[864,128]{1,0:T(8,128)}, u32[]{:S(2)}) copy-start(f32[864,128]{1,0:T(8,128)} %constant.30.clone.factor_ref) | copy-start | bytes 1327108
  7.6 0.7 copy-start.3
  15.8 27.2 %collective-permute-start.8 = (bf16[4,128,1024]{2,1,0:T(8,128)(2,1)}, bf16[4,128,1024]{2,1,0:T(8,128)(2,1)}, u32[]{:S(2)}, u32[]{:S(2)}) collective-permute-start(bf16[4,128,1024]{2,1,0:T(8,128)(2,1)} %get-tuple-element.20), channel_id=1, source_target_pairs={{0,1},{1,0},{2,3},{3,2},{4,5},{5,4},{6,7},{7,6},{8,9},{9,8},{10,11... | collective-permute-start | bytes 3145736 | tf_op jit(solution)/shard_map/ppermute | solution.py:482
  16.2 9.5 %collective-permute-start.4 = (bf16[2,33,16,128]{3,2,1,0:T(8,128)(2,1)S(1)}, bf16[2,33,16,128]{3,2,1,0:T(8,128)(2,1)S(1)}, u32[]{:S(2)}, u32[]{:S(2)}) collective-permute-start(bf16[2,33,16,128]{3,2,1,0:T(8,128)(2,1)S(1)} %pad_maximum_fusion.after_ref.refs_0_), channel_id=1, source_target_pairs={{0,8},{8,0},{1,9},{9,1},{2,10},{10,2},{3,11},{11,3},{4,12},{12,4},... | collective-permute-start | bytes 811016 | tf_op jit(solution)/shard_map/ppermute | solution.py:428
  19.2 10.2 %collective-permute-start.2 = (bf16[2,33,16,128]{3,2,1,0:T(8,128)(2,1)S(1)}, bf16[2,33,16,128]{3,2,1,0:T(8,128)(2,1)S(1)}, u32[]{:S(2)}, u32[]{:S(2)}) collective-permute-start(bf16[2,33,16,128]{3,2,1,0:T(8,128)(2,1)S(1)} %pad_maximum_fusion.after_ref.refs_0_), channel_id=1, source_target_pairs={{4,0},{6,2},{0,4},{2,6},{5,1},{7,3},{1,5},{3,7},{12,8},{14,10},{8,... | collective-permute-start | bytes 811016 | tf_op jit(solution)/shard_map/ppermute | solution.py:413
  22.8 12.7 %collective-permute-start.1 = (bf16[2,33,16,128]{3,2,1,0:T(8,128)(2,1)S(1)}, bf16[2,33,16,128]{3,2,1,0:T(8,128)(2,1)S(1)}, u32[]{:S(2)}, u32[]{:S(2)}) collective-permute-start(bf16[2,33,16,128]{3,2,1,0:T(8,128)(2,1)S(1)} %pad_maximum_fusion.after_ref.refs_0_), channel_id=1, source_target_pairs={{2,0},{4,2},{6,4},{0,6},{3,1},{5,3},{7,5},{1,7},{10,8},{12,10},{14... | collective-permute-start | bytes 811016 | tf_op jit(solution)/shard_map/ppermute | solution.py:413
  23.3 18.2 %collective-permute-start.3 = (bf16[2,33,16,128]{3,2,1,0:T(8,128)(2,1)S(1)}, bf16[2,33,16,128]{3,2,1,0:T(8,128)(2,1)S(1)}, u32[]{:S(2)}, u32[]{:S(2)}) collective-permute-start(bf16[2,33,16,128]{3,2,1,0:T(8,128)(2,1)S(1)} %pad_maximum_fusion.after_ref.refs_0_), channel_id=1, source_target_pairs={{6,0},{0,2},{2,4},{4,6},{7,1},{1,3},{3,5},{5,7},{14,8},{8,10},{10,... | collective-permute-start | bytes 811016 | tf_op jit(solution)/shard_map/ppermute | solution.py:413
  25.7 15.8 %collective-permute-start.5 = (bf16[2,33,16,128]{3,2,1,0:T(8,128)(2,1)S(1)}, bf16[2,33,16,128]{3,2,1,0:T(8,128)(2,1)S(1)}, u32[]{:S(2)}, u32[]{:S(2)}) collective-permute-start(bf16[2,33,16,128]{3,2,1,0:T(8,128)(2,1)S(1)} %collective-permute-done.4.after0_ref.refs_4_), channel_id=1, source_target_pairs={{2,0},{4,2},{6,4},{0,6},{3,1},{5,3},{7,5},{1,7},{10,8},{12,10},{14... | collective-permute-start | bytes 811016 | tf_op jit(solution)/shard_map/ppermute | solution.py:413
  29.5 12.1 %collective-permute-start.7 = (bf16[2,33,16,128]{3,2,1,0:T(8,128)(2,1)S(1)}, bf16[2,33,16,128]{3,2,1,0:T(8,128)(2,1)S(1)}, u32[]{:S(2)}, u32[]{:S(2)}) collective-permute-start(bf16[2,33,16,128]{3,2,1,0:T(8,128)(2,1)S(1)} %collective-permute-done.4.after0_ref.refs_4_), channel_id=1, source_target_pairs={{6,0},{0,2},{2,4},{4,6},{7,1},{1,3},{3,5},{5,7},{14,8},{8,10},{10,... | collective-permute-start | bytes 811016 | tf_op jit(solution)/shard_map/ppermute | solution.py:413
  35.5 7.4 %collective-permute-start.6 = (bf16[2,33,16,128]{3,2,1,0:T(8,128)(2,1)S(1)}, bf16[2,33,16,128]{3,2,1,0:T(8,128)(2,1)S(1)}, u32[]{:S(2)}, u32[]{:S(2)}) collective-permute-start(bf16[2,33,16,128]{3,2,1,0:T(8,128)(2,1)S(1)} %collective-permute-done.2.after1_ref.refs_2_), channel_id=1, source_target_pairs={{0,8},{8,0},{1,9},{9,1},{2,10},{10,2},{3,11},{11,3},{4,12},{12,4},... | collective-permute-start | bytes 811016 | tf_op jit(solution)/shard_map/ppermute | solution.py:432
  41.5 15.2 %copy-start.6 = (s32[256]{0:T(256)S(1)}, s32[256]{0:T(256)}, u32[]{:S(2)}) copy-start(s32[256]{0:T(256)} %param.13) | copy-start | bytes 3076
  46.8 20.9 %all-to-all-start = ((bf16[64,32,128]{2,1,0:T(8,128)(2,1)}), bf16[64,32,128]{2,1,0:T(8,128)(2,1)S(1)}, u32[]{:S(2)}, u32[]{:S(2)}) async-start(bf16[64,32,128]{2,1,0:T(8,128)(2,1)} %bitcast.5), calls=%async_computation | async-start | bytes 1048576 | tf_op jit(solution)/shard_map/all_to_all | solution.py:513
  57.5 2.6 %collective-permute-start.9 = (f32[2,16,128]{2,1,0:T(8,128)S(1)}, f32[2,16,128]{2,1,0:T(8,128)S(1)}, u32[]{:S(2)}, u32[]{:S(2)}) collective-permute-start(f32[2,16,128]{2,1,0:T(8,128)S(1)} %pad_maximum_fusion.2), channel_id=1, source_target_pairs={{0,1},{1,0},{2,3},{3,2},{4,5},{5,4},{6,7},{7,6},{8,9},{9,8},{10,11... | collective-permute-start | bytes 49160 | tf_op jit(solution)/shard_map/ppermute | solution.py:445
  86.9 8.3 %collective-permute-start.10 = (bf16[4,128,1024]{2,1,0:T(8,128)(2,1)S(1)}, bf16[4,128,1024]{2,1,0:T(8,128)(2,1)S(1)}, u32[]{:S(2)}, u32[]{:S(2)}) collective-permute-start(bf16[4,128,1024]{2,1,0:T(8,128)(2,1)S(1)} %get-tuple-element.23), channel_id=1, source_target_pairs={{0,1},{1,0},{2,3},{3,2},{4,5},{5,4},{6,7},{7,6},{8,9},{9,8},{10,11... | collective-permute-start | bytes 3145736 | tf_op jit(solution)/shard_map/ppermute | solution.py:527
  90.0 5.1 %copy-start.4 = (f32[2,2048]{1,0:T(2,128)S(1)}, f32[2,2048]{1,0:T(2,128)}, u32[]{:S(2)}) copy-start(f32[2,2048]{1,0:T(2,128)} %col_ref.3) | copy-start | bytes 49156
